TPU v7x, 128 devices: a whole 4x4x4 slice. The times are simulated.
128 devices in a mesh: scen: 8 (over x_hi, y), slab: 16 (over z, x_lo, core).
Axes of the slice: x: 4 (x_hi: 2, x_lo: 2; x = x_hi * 2 + x_lo), y: 4, z: 4, core: 2. Of those that a mesh axis runs over, the one named last changes fastest.
Arguments:
- start: float32 [8, 128, 256, 256], P('scen', 'slab'), may hold values from 0 to 2
- flow_east: float32 [8, 128, 256, 256], P('scen', 'slab'), may hold values from 0.3 to 1.2
- flow_north: float32 [8, 128, 256, 256], P('scen', 'slab'), may hold values from 0.3 to 1.2
- wells: int32 [128, 256, 256], P('slab'), may hold values 0 or 1
- monitors: int32 [128, 256, 256], P('slab'), may hold values 0 or 1
- control: float32 [8, 32, 4096], P('scen', 'slab'), may hold values from -3 to 3
- multiplier: float32 [8, 32, 4096], P('scen', 'slab'), may hold values from -3 to 3
- threshold: float32 [1], replicated, may hold values from 0.8 to 1.3
Outputs:
- final_fields: float32 [8, 128, 256, 256], P('scen', 'slab')
- consensus_next: float32 [32, 4096], P('slab')
- multiplier_next: float32 [8, 32, 4096], P('scen', 'slab')
- cvar: float32 [1], replicated
All inputs are finite; a program needn't handle non-finite values. No bound on the sum of `wells` or of `monitors` on one device may be relied on, other than what follows from the above.
Results may differ from a plain program's by a relative error of at most 0.00002.
Values sent between devices are 32-bit elements; how exact they have to be, the bound alone decides.
No kernel may reach another device: no remote copies, remote signals or barrier semaphores. Data moves between devices by JAX's collectives and lax.ppermute only.
A program may use at most 192 MiB of HBM per device.

v0:
```python
import jax
import jax.numpy as jnp
from jax import lax
from jax.sharding import PartitionSpec as P

STEPS = 4


EPS_LIMIT = 0.01
TIME_STEP = 0.25
DIFF_FLAT = 0.1
DIFF_VERTICAL = 0.25
BETA_LEVEL = 0.75
SOFT_WIDTH = 0.25


def with_halo(cells, sides, width):
    for axis, dim in sides:
        count = lax.axis_size(axis)
        ends = count - 1
        head = lax.slice_in_dim(cells, 0, width, axis=dim)
        tail = lax.slice_in_dim(cells, cells.shape[dim] - width, cells.shape[dim], axis=dim)
        cells = jnp.concatenate(
            [
                lax.ppermute(tail, axis, [(i, (i + 1) % count) for i in range(ends)]),
                cells,
                lax.ppermute(head, axis, [((i + 1) % count, i) for i in range(ends)]),
            ],
            axis=dim,
        )
    return cells


def pad_axis(field, which_axis, low_pad, high_pad):
    widths = [(0, 0)] * field.ndim
    widths[which_axis] = (low_pad, high_pad)
    return jnp.pad(field, widths)


def second_difference(padded, field, which_axis):
    length = field.shape[which_axis]
    upper_cells = lax.slice_in_dim(padded, 2, length + 2, axis=which_axis)
    lower_cells = lax.slice_in_dim(padded, 0, length, axis=which_axis)
    return upper_cells - 2.0 * field + lower_cells


def divergence(field, velocity, which_axis):
    length = field.shape[which_axis]
    padded = pad_axis(field, which_axis, 1, 1)
    lower_cells = lax.slice_in_dim(padded, 0, length, axis=which_axis)
    upper_cells = lax.slice_in_dim(padded, 2, length + 2, axis=which_axis)
    backward = field - lower_cells
    forward = upper_cells - field
    product = backward * forward
    weight = (product + jnp.sqrt(product * product + EPS_LIMIT * EPS_LIMIT)) / (
        backward * backward + forward * forward + EPS_LIMIT
    )
    face_value = field + 0.5 * weight * (backward / 3.0 + 2.0 * forward / 3.0)
    fluxes = velocity * face_value
    previous = lax.slice_in_dim(pad_axis(fluxes, which_axis, 1, 0), 0, length, axis=which_axis)
    return fluxes - previous


def horizontal(field, flow_east, flow_north, rate):
    advect = divergence(field, flow_east, 1) + divergence(field, flow_north, 2)
    spread = second_difference(pad_axis(field, 1, 1, 1), field, 1) + second_difference(
        pad_axis(field, 2, 1, 1), field, 2
    )
    return -advect + DIFF_FLAT * spread - rate * field


def prolong(coarse, row_count, column_count):
    plane_count = coarse.shape[0]
    cube = coarse.reshape(plane_count, 1, row_count // 4, 1, column_count // 4, 1)
    cube = jnp.broadcast_to(cube, (plane_count, 4, row_count // 4, 4, column_count // 4, 4))
    return cube.reshape(plane_count * 4, row_count, column_count)


def restrict(fine):
    plane_count, row_count, column_count = fine.shape
    blocks = fine.reshape(plane_count // 4, 4, row_count // 4, 4, column_count // 4, 4).sum(
        axis=(1, 3, 5)
    )
    return blocks.reshape(plane_count // 4, row_count // 4 * (column_count // 4))


def on_device(start, flow_east, flow_north, wells, monitors, control, multiplier, threshold):
    scen_count = lax.axis_size("scen")
    slab_count = lax.axis_size("slab")
    consensus = lax.psum(jnp.sum(control + multiplier, axis=0), "scen") / scen_count
    field = start[0]
    east = flow_east[0]
    north = flow_north[0]
    plane_count, row_count, column_count = field.shape
    wells_float = wells.astype(jnp.float32)
    monitor_float = monitors.astype(jnp.float32)
    rate = wells_float * prolong(consensus, row_count, column_count)
    states = []
    for step_index in range(STEPS):
        states.append(field)
        padded = with_halo(field, (("slab", 0),), 1)
        vertical = second_difference(padded, field, 0)
        field = field + TIME_STEP * (
            horizontal(field, east, north, rate) + DIFF_VERTICAL * vertical
        )
    mass, count = lax.psum((jnp.sum(monitor_float * field * field), jnp.sum(monitor_float)), "slab")
    count = jnp.maximum(count, 1.0)
    loss = mass / count
    scaled = (loss - threshold[0]) / SOFT_WIDTH
    weight = jax.nn.sigmoid(scaled) / ((1.0 - BETA_LEVEL) * scen_count)
    soft_term = SOFT_WIDTH * jax.nn.softplus(scaled) / ((1.0 - BETA_LEVEL) * scen_count)
    risk = lax.psum(soft_term, "scen")
    adjoint = weight * 2.0 * monitor_float * field / count
    rate_grad = jnp.zeros_like(field)
    for step_index in reversed(range(STEPS)):
        state = states[step_index]
        padded = with_halo(adjoint, (("slab", 0),), 1)
        unused, pullback = jax.vjp(lambda values: horizontal(values, east, north, rate), state)
        (pulled,) = pullback(adjoint)
        rate_grad = rate_grad - TIME_STEP * state * adjoint
        vertical = second_difference(padded, adjoint, 0)
        adjoint = adjoint + TIME_STEP * (pulled + DIFF_VERTICAL * vertical)
    coarse_cells = plane_count * slab_count * row_count * column_count / 64.0
    gradient = coarse_cells * restrict(wells_float * rate_grad)
    total = lax.psum(gradient, "scen")
    consensus_next = consensus - total
    multiplier_next = multiplier + control - consensus_next[None]
    cvar = threshold + risk
    return (field[None], consensus_next, multiplier_next, cvar)


def solution(mesh):
    placed = (
        P("scen", "slab", None, None),
        P("scen", "slab", None, None),
        P("scen", "slab", None, None),
        P("slab", None, None),
        P("slab", None, None),
        P("scen", "slab", None),
        P("scen", "slab", None),
        P(),
    )
    return jax.shard_map(
        on_device,
        mesh=mesh,
        in_specs=placed,
        out_specs=(P("scen", "slab", None, None), P("slab", None), P("scen", "slab", None), P()),
        check_vma=False,
    )
```

profile of v0, /device:TPU:2, one launch (start us, length us, event | category | flops | bytes accessed | tf_op | source)
XLA Modules:
  0.0 485.9 jit_solution(5351484315725654341)
XLA Ops:
  0.6 1.1 slice_bitcast_fusion.1
  1.7 1.9 collective-permute-start
  3.6 2.4 collective-permute-start.1
  6.0 0.8 add.433
  6.9 41.1 %psum.35 = f32[2,4096]{1,0:T(2,128)S(1)} all-reduce(f32[2,4096]{1,0:T(2,128)S(1)} %bitcast.40), channel_id=1, replica_groups=mesh['scen'=8,'slab'=16] {'scen'}, use_global_device_ids=true, to_apply=%region_0.0 | all-reduce | flops 8192 | bytes 65536 | tf_op jit(solution)/shard_map/psum | solution.py:90
  48.0 11.3 %bitcast_multiply_fusion.3 = (f32[8,256,256]{2,1,0:T(8,128)}, f32[8,256,256]{2,1,0:T(8,128)}) fusion(f32[1,8,256,256]{3,2,1,0:T(8,128)} %param.10, f32[8,256,256]{2,1,0:T(8,128)} %bitcast.37, f32[1,8,256,256]{3,2,1,0:T(8,128)} %param.9), kind=kLoop, calls=%fused_computation.197 | loop fusion | flops 18874368 | bytes 10485760 | tf_op jit(solution)/shard_map/mul | solution.py:59
  59.3 0.1 broadcast_in_dim.16
  59.4 21.5 %broadcast_in_dim.17 = f32[2,4,64,4,64,4]{5,4,3,2,1,0:T(8,128)} broadcast(f32[2,64,64]{2,1,0:T(8,128)S(1)} %broadcast_in_dim.16), dimensions={0,2,4} | broadcast | bytes 2129920 | tf_op jit(solution)/shard_map/broadcast_in_dim | solution.py:75
  80.9 56.1 %reshape.22 = f32[8,256,256]{2,1,0:T(8,128)} reshape(f32[2,4,64,4,64,4]{5,4,3,2,1,0:T(8,128)} %broadcast_in_dim.17) | data formatting | bytes 4194304 | tf_op jit(solution)/shard_map/reshape | solution.py:76
  137.6 0.0 copy-start
  137.7 12.0 %fusion.7 = (f32[8,256,256]{2,1,0:T(8,128)S(1)}, f32[8,256,256]{2,1,0:T(8,128)S(1)}) fusion(f32[8,256,256]{2,1,0:T(8,128)} %bitcast.38, f32[8,256,256]{2,1,0:T(8,128)} %get-tuple-element.78, f32[8,256,256]{2,1,0:T(8,128)} %get-tuple-element.77, f32[1,256,256]{2,1,0:T(8,128)S(1)} %collective-permute-done.1, f32[1,256,256]{2,1,0:T(8,128)S(1)} %collective-permute-done, ...), kind=kLoop, calls=%fused_computation.48 | loop fusion | flops 12582912 | bytes 15204352 | tf_op jit(solution)/shard_map/add | solution.py:103
  149.7 1.9 collective-permute-start.2
  151.7 2.4 collective-permute-start.3
  154.1 4.1 bitcast_multiply_fusion.2
  158.3 1.1 collective-permute-done.3
  159.4 3.2 fusion.15
  162.6 2.1 collective-permute-start.4
  164.7 3.6 collective-permute-start.5
  168.3 4.1 bitcast_multiply_fusion.1
  172.5 3.1 fusion.23
  175.6 2.5 collective-permute-start.6
  178.1 4.1 collective-permute-start.7
  182.2 4.1 bitcast_multiply_fusion.4
  186.4 5.0 %fusion.42 = (f32[]{:T(128)}, f32[]{:T(128)}, f32[8,256,256]{2,1,0:T(8,128)}) fusion(s32[8,256,256]{2,1,0:T(8,128)S(1)} %copy-done.21, f32[8,256,256]{2,1,0:T(8,128)S(1)} %fusion.23, f32[1,256,256]{2,1,0:T(8,128)S(1)} %collective-permute-done.7, f32[1,256,256]{2,1,0:T(8,128)S(1)} %collective-permute-done.6, f32[8,256,256]{2,1,0:T(8,128)S(1)} %get-tuple-element.44, ...), kind=kLoop, calls=%fused_computation.83 | loop fusion | flops 14155774 | bytes 13107208 | tf_op jit(solution)/shard_map/reduce_sum | solution.py:106
  191.4 27.4 %all-reduce.46 = (f32[]{:T(128)}, f32[]{:T(128)}) all-reduce(f32[]{:T(128)} %get-tuple-element.5, f32[]{:T(128)} %get-tuple-element.4), channel_id=1, replica_groups=mesh['scen'=8,'slab'=16] {'slab'}, use_global_device_ids=true, to_apply=%region_4.5 | all-reduce | flops 2 | bytes 16 | tf_op jit(solution)/shard_map/psum | solution.py:106
  220.2 0.0 copy-start.2
  220.2 4.4 broadcast_multiply_fusion.2
  224.6 8.3 %fusion.45 = (f32[8,256,256]{2,1,0:T(8,128)}, f32[8,256,256]{2,1,0:T(8,128)S(1)}, f32[8,256,256]{2,1,0:T(8,128)}, f32[8,256,256]{2,1,0:T(8,128)S(1)}) fusion(f32[8,256,256]{2,1,0:T(8,128)S(1)} %copy-done.10, f32[8,256,256]{2,1,0:T(8,128)S(1)} %get-tuple-element.33, f32[1,8,256,256]{3,2,1,0:T(8,128)S(1)} %copy-done, f32[1,8,256,256]{3,2,1,0:T(8,128)S(1)} %copy-done.2), kind=kLoop, calls=%fused_computation.86 | loop fusion | flops 39321600 | bytes 16777216 | tf_op jit(solution)/shard_map/transpose(jvp())/add_any | solution.py:54
  232.9 5.6 %collective-permute-start.8 = (f32[1,256,256]{2,1,0:T(8,128)S(1)}, f32[1,256,256]{2,1,0:T(8,128)S(1)}, u32[]{:S(2)}, u32[]{:S(2)}) collective-permute-start(f32[1,256,256]{2,1,0:T(8,128)S(1)} %get-tuple-element.61), channel_id=1, source_target_pairs={{1,0},{2,1},{3,2},{4,3},{5,4},{6,5},{7,6},{8,7},{9,8},{10,9},{11,1... | collective-permute-start | bytes 786440 | tf_op jit(solution)/shard_map/ppermute | solution.py:27
  238.5 2.1 collective-permute-start.9
  240.6 8.5 %fusion.190 = (f32[8,256,256]{2,1,0:T(8,128)}, f32[8,256,256]{2,1,0:T(8,128)}, f32[8,256,256]{2,1,0:T(8,128)}, f32[8,256,256]{2,1,0:T(8,128)}) fusion(f32[8,256,256]{2,1,0:T(8,128)S(1)} %get-tuple-element.35, f32[8,256,256]{2,1,0:T(8,128)S(1)} %copy-done.10, f32[8,256,256]{2,1,0:T(8,128)S(1)} %get-tuple-element.50), kind=kLoop, calls=%fused_computation.312 | loop fusion | flops 37748736 | bytes 14680064 | tf_op jit(solution)/shard_map/transpose(jvp())/neg | solution.py:52
  249.2 16.8 %broadcast_multiply_fusion.1 = (f32[8,256,256]{2,1,0:T(8,128)}, f32[8,256,256]{2,1,0:T(8,128)S(1)}) fusion(f32[8,256,256]{2,1,0:T(8,128)} %copy-done.13, f32[1,256,256]{2,1,0:T(8,128)S(1)} %collective-permute-done.9, f32[1,256,256]{2,1,0:T(8,128)S(1)} %collective-permute-done.8, f32[8,256,256]{2,1,0:T(8,128)} %get-tuple-element.59, ...), kind=kLoop, calls=%fused_computation.294 | loop fusion | flops 16777216 | bytes 27787264 | tf_op jit(solution)/shard_map/transpose(jvp())/mul | solution.py:69
  266.0 8.3 %fusion.51 = (f32[8,256,256]{2,1,0:T(8,128)}, f32[8,256,256]{2,1,0:T(8,128)S(1)}, f32[8,256,256]{2,1,0:T(8,128)}, f32[8,256,256]{2,1,0:T(8,128)S(1)}) fusion(f32[8,256,256]{2,1,0:T(8,128)S(1)} %copy-done.8, f32[8,256,256]{2,1,0:T(8,128)S(1)} %get-tuple-element.23, f32[1,8,256,256]{3,2,1,0:T(8,128)S(1)} %copy-done, f32[1,8,256,256]{3,2,1,0:T(8,128)S(1)} %copy-done.3), kind=kLoop, calls=%fused_computation.92 | loop fusion | flops 39321600 | bytes 16777216 | tf_op jit(solution)/shard_map/transpose(jvp())/add_any | solution.py:54
  274.4 3.6 collective-permute-start.10
  278.1 2.1 collective-permute-start.11
  280.2 8.4 %fusion.184 = (f32[8,256,256]{2,1,0:T(8,128)}, f32[8,256,256]{2,1,0:T(8,128)}, f32[8,256,256]{2,1,0:T(8,128)}, f32[8,256,256]{2,1,0:T(8,128)}) fusion(f32[8,256,256]{2,1,0:T(8,128)S(1)} %get-tuple-element.25, f32[8,256,256]{2,1,0:T(8,128)S(1)} %copy-done.8, f32[8,256,256]{2,1,0:T(8,128)S(1)} %get-tuple-element.48), kind=kLoop, calls=%fused_computation.310 | loop fusion | flops 37748736 | bytes 14680064 | tf_op jit(solution)/shard_map/transpose(jvp())/neg | solution.py:52
  288.7 16.4 %broadcast_multiply_fusion = (f32[8,256,256]{2,1,0:T(8,128)}, f32[8,256,256]{2,1,0:T(8,128)}) fusion(f32[8,256,256]{2,1,0:T(8,128)} %copy-done.14, f32[1,256,256]{2,1,0:T(8,128)S(1)} %collective-permute-done.11, f32[1,256,256]{2,1,0:T(8,128)S(1)} %collective-permute-done.10, f32[8,256,256]{2,1,0:T(8,128)} %get-tuple-element.55, ...), kind=kLoop, calls=%fused_computation.293 | loop fusion | flops 16777216 | bytes 27787264 | tf_op jit(solution)/shard_map/transpose(jvp())/mul | solution.py:69
  305.1 10.2 %fusion.57 = (f32[8,256,256]{2,1,0:T(8,128)}, f32[8,256,256]{2,1,0:T(8,128)S(1)}, f32[8,256,256]{2,1,0:T(8,128)}, f32[8,256,256]{2,1,0:T(8,128)S(1)}) fusion(f32[8,256,256]{2,1,0:T(8,128)S(1)} %copy-done.12, f32[8,256,256]{2,1,0:T(8,128)} %get-tuple-element.13, f32[1,8,256,256]{3,2,1,0:T(8,128)S(1)} %copy-done, f32[1,8,256,256]{3,2,1,0:T(8,128)S(1)} %copy-done.3), kind=kLoop, calls=%fused_computation.98 | loop fusion | flops 39321600 | bytes 16777216 | tf_op jit(solution)/shard_map/transpose(jvp())/add_any | solution.py:54
  315.3 1.4 fusion.196
  316.7 3.6 collective-permute-start.12
  320.4 2.2 collective-permute-start.13
  322.6 8.5 %fusion.177 = (f32[8,256,256]{2,1,0:T(8,128)}, f32[8,256,256]{2,1,0:T(8,128)}, f32[8,256,256]{2,1,0:T(8,128)}, f32[8,256,256]{2,1,0:T(8,128)}) fusion(f32[8,256,256]{2,1,0:T(8,128)S(1)} %get-tuple-element.15, f32[8,256,256]{2,1,0:T(8,128)S(1)} %copy-done.12, f32[8,256,256]{2,1,0:T(8,128)S(1)} %get-tuple-element.46), kind=kLoop, calls=%fused_computation.308 | loop fusion | flops 37748736 | bytes 14680064 | tf_op jit(solution)/shard_map/transpose(jvp())/neg | solution.py:52
  331.1 21.2 %fusion.68 = f32[8,256,256]{2,1,0:T(8,128)} fusion(f32[8,256,256]{2,1,0:T(8,128)} %get-tuple-element.13, f32[1,256,256]{2,1,0:T(8,128)S(1)} %collective-permute-done.13, f32[1,256,256]{2,1,0:T(8,128)S(1)} %collective-permute-done.12, f32[8,256,256]{2,1,0:T(8,128)} %get-tuple-element.51, f32[8,256,256]{2,1,0:T(8,128)} %get-tuple-element.45, ...), kind=kLoop, calls=%fused_computation.110 | loop fusion | flops 23592960 | bytes 40370176 | tf_op jit(solution)/shard_map/mul | solution.py:124
  352.3 71.4 %reshape.23 = f32[2,4,64,4,64,4]{5,4,3,2,1,0:T(8,128)} reshape(f32[8,256,256]{2,1,0:T(8,128)} %fusion.68) | data formatting | bytes 4194304 | tf_op jit(solution)/shard_map/reshape | solution.py:81
  423.8 20.8 %reduce_sum.36 = f32[2,64,64]{2,1,0:T(8,128)S(1)} reduce(f32[2,4,64,4,64,4]{5,4,3,2,1,0:T(8,128)} %reshape.23, f32[]{:T(128)} %constant.83.clone.1), dimensions={1,3,5}, to_apply=%region_5.6 | reduce | flops 516096 | bytes 2129924 | tf_op jit(solution)/shard_map/reduce_sum | solution.py:81
  444.6 0.1 mul.858
  444.7 38.5 %all-reduce.47 = (f32[2,4096]{1,0:T(2,128)S(1)}, f32[1]{0:T(128)}) all-reduce(f32[2,4096]{1,0:T(2,128)S(1)} %mul.858, f32[1]{0:T(128)} %bitcast.9), channel_id=1, replica_groups=mesh['scen'=8,'slab'=16] {'scen'}, use_global_device_ids=true, to_apply=%region_6.7 | all-reduce | flops 8193 | bytes 65544 | tf_op jit(solution)/shard_map/psum | solution.py:125
  483.2 0.7 bitcast_subtract_fusion
  (70 shorter events, 0.3 us)
Async XLA Ops:
  1.7 135.9 %collective-permute-start = (f32[1,256,256]{2,1,0:T(8,128)S(1)}, f32[1,256,256]{2,1,0:T(8,128)S(1)}, u32[]{:S(2)}, u32[]{:S(2)}) collective-permute-start(f32[1,256,256]{2,1,0:T(8,128)S(1)} %get-tuple-element.75), channel_id=1, source_target_pairs={{1,0},{2,1},{3,2},{4,3},{5,4},{6,5},{7,6},{8,7},{9,8},{10,9},{11,1... | collective-permute-start | bytes 786440 | tf_op jit(solution)/shard_map/ppermute | solution.py:27
  3.6 134.0 %collective-permute-start.1 = (f32[1,256,256]{2,1,0:T(8,128)S(1)}, f32[1,256,256]{2,1,0:T(8,128)S(1)}, u32[]{:S(2)}, u32[]{:S(2)}) collective-permute-start(f32[1,256,256]{2,1,0:T(8,128)S(1)} %get-tuple-element.76), channel_id=1, source_target_pairs={{0,1},{1,2},{2,3},{3,4},{4,5},{5,6},{6,7},{7,8},{8,9},{9,10},{10,1... | collective-permute-start | bytes 786440 | tf_op jit(solution)/shard_map/ppermute | solution.py:25
  6.8 52.4 %copy-start.22 = (f32[1,2,4096]{2,1,0:T(2,128)}, f32[1,2,4096]{2,1,0:T(2,128)S(1)}, u32[]{:S(2)}) copy-start(f32[1,2,4096]{2,1,0:T(2,128)S(1)} %add.433) | copy-start | bytes 98308
  47.9 11.3 %copy-start.24 = (f32[2,4096]{1,0:T(2,128)}, f32[2,4096]{1,0:T(2,128)S(1)}, u32[]{:S(2)}) copy-start(f32[2,4096]{1,0:T(2,128)S(1)} %psum.35) | copy-start | bytes 98308
  137.6 16.4 %copy-start = (f32[1,8,256,256]{3,2,1,0:T(8,128)S(1)}, f32[1,8,256,256]{3,2,1,0:T(8,128)}, u32[]{:S(2)}) copy-start(f32[1,8,256,256]{3,2,1,0:T(8,128)} %param.10) | copy-start | bytes 6291460
  137.7 16.4 %copy-start.1 = (f32[1,8,256,256]{3,2,1,0:T(8,128)S(1)}, f32[1,8,256,256]{3,2,1,0:T(8,128)}, u32[]{:S(2)}) copy-start(f32[1,8,256,256]{3,2,1,0:T(8,128)} %param.9) | copy-start | bytes 6291460
  149.7 9.7 %copy-start.11 = (f32[8,256,256]{2,1,0:T(8,128)}, f32[8,256,256]{2,1,0:T(8,128)S(1)}, u32[]{:S(2)}) copy-start(f32[8,256,256]{2,1,0:T(8,128)S(1)} %get-tuple-element.43) | copy-start | bytes 6291460
  149.7 36.7 %copy-start.4 = (f32[8,256,256]{2,1,0:T(8,128)}, f32[8,256,256]{2,1,0:T(8,128)S(1)}, u32[]{:S(2)}) copy-start(f32[8,256,256]{2,1,0:T(8,128)S(1)} %get-tuple-element.44) | copy-start | bytes 6291460
  149.7 8.5 %collective-permute-start.2 = (f32[1,256,256]{2,1,0:T(8,128)S(1)}, f32[1,256,256]{2,1,0:T(8,128)S(1)}, u32[]{:S(2)}, u32[]{:S(2)}) collective-permute-start(f32[1,256,256]{2,1,0:T(8,128)S(1)} %get-tuple-element.71), channel_id=1, source_target_pairs={{1,0},{2,1},{3,2},{4,3},{5,4},{6,5},{7,6},{8,7},{9,8},{10,9},{11,1... | collective-permute-start | bytes 786440 | tf_op jit(solution)/shard_map/ppermute | solution.py:27
  151.7 7.7 %collective-permute-start.3 = (f32[1,256,256]{2,1,0:T(8,128)S(1)}, f32[1,256,256]{2,1,0:T(8,128)S(1)}, u32[]{:S(2)}, u32[]{:S(2)}) collective-permute-start(f32[1,256,256]{2,1,0:T(8,128)S(1)} %get-tuple-element.72), channel_id=1, source_target_pairs={{0,1},{1,2},{2,3},{3,4},{4,5},{5,6},{6,7},{7,8},{8,9},{9,10},{10,1... | collective-permute-start | bytes 786440 | tf_op jit(solution)/shard_map/ppermute | solution.py:25
  162.5 9.9 %copy-start.7 = (f32[8,256,256]{2,1,0:T(8,128)}, f32[8,256,256]{2,1,0:T(8,128)S(1)}, u32[]{:S(2)}) copy-start(f32[8,256,256]{2,1,0:T(8,128)S(1)} %fusion.15) | copy-start | bytes 6291460
  162.6 9.8 %collective-permute-start.4 = (f32[1,256,256]{2,1,0:T(8,128)S(1)}, f32[1,256,256]{2,1,0:T(8,128)S(1)}, u32[]{:S(2)}, u32[]{:S(2)}) collective-permute-start(f32[1,256,256]{2,1,0:T(8,128)S(1)} %get-tuple-element.67), channel_id=1, source_target_pairs={{1,0},{2,1},{3,2},{4,3},{5,4},{6,5},{7,6},{8,7},{9,8},{10,9},{11,1... | collective-permute-start | bytes 786440 | tf_op jit(solution)/shard_map/ppermute | solution.py:27
  164.7 7.8 %collective-permute-start.5 = (f32[1,256,256]{2,1,0:T(8,128)S(1)}, f32[1,256,256]{2,1,0:T(8,128)S(1)}, u32[]{:S(2)}, u32[]{:S(2)}) collective-permute-start(f32[1,256,256]{2,1,0:T(8,128)S(1)} %get-tuple-element.68), channel_id=1, source_target_pairs={{0,1},{1,2},{2,3},{3,4},{4,5},{5,6},{6,7},{7,8},{8,9},{9,10},{10,1... | collective-permute-start | bytes 786440 | tf_op jit(solution)/shard_map/ppermute | solution.py:25
  175.5 10.8 %copy-start.9 = (f32[8,256,256]{2,1,0:T(8,128)}, f32[8,256,256]{2,1,0:T(8,128)S(1)}, u32[]{:S(2)}) copy-start(f32[8,256,256]{2,1,0:T(8,128)S(1)} %fusion.23) | copy-start | bytes 6291460
  175.6 10.8 %collective-permute-start.6 = (f32[1,256,256]{2,1,0:T(8,128)S(1)}, f32[1,256,256]{2,1,0:T(8,128)S(1)}, u32[]{:S(2)}, u32[]{:S(2)}) collective-permute-start(f32[1,256,256]{2,1,0:T(8,128)S(1)} %get-tuple-element.65), channel_id=1, source_target_pairs={{1,0},{2,1},{3,2},{4,3},{5,4},{6,5},{7,6},{8,7},{9,8},{10,9},{11,1... | collective-permute-start | bytes 786440 | tf_op jit(solution)/shard_map/ppermute | solution.py:27
  178.1 8.3 %copy-start.21 = (s32[8,256,256]{2,1,0:T(8,128)S(1)}, s32[8,256,256]{2,1,0:T(8,128)}, u32[]{:S(2)}) copy-start(s32[8,256,256]{2,1,0:T(8,128)} %param.12) | copy-start | bytes 6291460
  178.1 8.3 %collective-permute-start.7 = (f32[1,256,256]{2,1,0:T(8,128)S(1)}, f32[1,256,256]{2,1,0:T(8,128)S(1)}, u32[]{:S(2)}, u32[]{:S(2)}) collective-permute-start(f32[1,256,256]{2,1,0:T(8,128)S(1)} %get-tuple-element.66), channel_id=1, source_target_pairs={{0,1},{1,2},{2,3},{3,4},{4,5},{5,6},{6,7},{7,8},{8,9},{9,10},{10,1... | collective-permute-start | bytes 786440 | tf_op jit(solution)/shard_map/ppermute | solution.py:25
  220.2 4.4 copy-start.2
  220.2 4.4 copy-start.10
  224.6 8.3 %copy-start.13 = (f32[8,256,256]{2,1,0:T(8,128)}, f32[8,256,256]{2,1,0:T(8,128)S(1)}, u32[]{:S(2)}) copy-start(f32[8,256,256]{2,1,0:T(8,128)S(1)} %get-tuple-element.33) | copy-start | bytes 6291460
  232.8 7.7 %copy-start.17 = (f32[8,256,256]{2,1,0:T(8,128)}, f32[8,256,256]{2,1,0:T(8,128)S(1)}, u32[]{:S(2)}) copy-start(f32[8,256,256]{2,1,0:T(8,128)S(1)} %get-tuple-element.35) | copy-start | bytes 6291460
  232.8 7.7 %copy-start.18 = (f32[8,256,256]{2,1,0:T(8,128)}, f32[8,256,256]{2,1,0:T(8,128)S(1)}, u32[]{:S(2)}) copy-start(f32[8,256,256]{2,1,0:T(8,128)S(1)} %get-tuple-element.50) | copy-start | bytes 6291460
  232.9 16.3 %collective-permute-start.8 = (f32[1,256,256]{2,1,0:T(8,128)S(1)}, f32[1,256,256]{2,1,0:T(8,128)S(1)}, u32[]{:S(2)}, u32[]{:S(2)}) collective-permute-start(f32[1,256,256]{2,1,0:T(8,128)S(1)} %get-tuple-element.61), channel_id=1, source_target_pairs={{1,0},{2,1},{3,2},{4,3},{5,4},{6,5},{7,6},{8,7},{9,8},{10,9},{11,1... | collective-permute-start | bytes 786440 | tf_op jit(solution)/shard_map/ppermute | solution.py:27
  238.5 10.8 %collective-permute-start.9 = (f32[1,256,256]{2,1,0:T(8,128)S(1)}, f32[1,256,256]{2,1,0:T(8,128)S(1)}, u32[]{:S(2)}, u32[]{:S(2)}) collective-permute-start(f32[1,256,256]{2,1,0:T(8,128)S(1)} %get-tuple-element.62), channel_id=1, source_target_pairs={{0,1},{1,2},{2,3},{3,4},{4,5},{5,6},{6,7},{7,8},{8,9},{9,10},{10,1... | collective-permute-start | bytes 786440 | tf_op jit(solution)/shard_map/ppermute | solution.py:25
  249.2 16.8 %copy-start.3 = (f32[1,8,256,256]{3,2,1,0:T(8,128)S(1)}, f32[1,8,256,256]{3,2,1,0:T(8,128)}, u32[]{:S(2)}) copy-start(f32[1,8,256,256]{3,2,1,0:T(8,128)} %param.9) | copy-start | bytes 6291460
  249.2 16.8 %copy-start.8 = (f32[8,256,256]{2,1,0:T(8,128)S(1)}, f32[8,256,256]{2,1,0:T(8,128)}, u32[]{:S(2)}) copy-start(f32[8,256,256]{2,1,0:T(8,128)} %copy-done.7) | copy-start | bytes 6291460
  266.0 8.3 %copy-start.14 = (f32[8,256,256]{2,1,0:T(8,128)}, f32[8,256,256]{2,1,0:T(8,128)S(1)}, u32[]{:S(2)}) copy-start(f32[8,256,256]{2,1,0:T(8,128)S(1)} %get-tuple-element.23) | copy-start | bytes 6291460
  274.4 14.3 %copy-start.19 = (f32[8,256,256]{2,1,0:T(8,128)}, f32[8,256,256]{2,1,0:T(8,128)S(1)}, u32[]{:S(2)}) copy-start(f32[8,256,256]{2,1,0:T(8,128)S(1)} %get-tuple-element.25) | copy-start | bytes 6291460
  274.4 14.3 %copy-start.20 = (f32[8,256,256]{2,1,0:T(8,128)}, f32[8,256,256]{2,1,0:T(8,128)S(1)}, u32[]{:S(2)}) copy-start(f32[8,256,256]{2,1,0:T(8,128)S(1)} %get-tuple-element.48) | copy-start | bytes 6291460
  274.4 14.3 %collective-permute-start.10 = (f32[1,256,256]{2,1,0:T(8,128)S(1)}, f32[1,256,256]{2,1,0:T(8,128)S(1)}, u32[]{:S(2)}, u32[]{:S(2)}) collective-permute-start(f32[1,256,256]{2,1,0:T(8,128)S(1)} %get-tuple-element.57), channel_id=1, source_target_pairs={{1,0},{2,1},{3,2},{4,3},{5,4},{6,5},{7,6},{8,7},{9,8},{10,9},{11,1... | collective-permute-start | bytes 786440 | tf_op jit(solution)/shard_map/ppermute | solution.py:27
  278.1 10.6 %collective-permute-start.11 = (f32[1,256,256]{2,1,0:T(8,128)S(1)}, f32[1,256,256]{2,1,0:T(8,128)S(1)}, u32[]{:S(2)}, u32[]{:S(2)}) collective-permute-start(f32[1,256,256]{2,1,0:T(8,128)S(1)} %get-tuple-element.58), channel_id=1, source_target_pairs={{0,1},{1,2},{2,3},{3,4},{4,5},{5,6},{6,7},{7,8},{8,9},{9,10},{10,1... | collective-permute-start | bytes 786440 | tf_op jit(solution)/shard_map/ppermute | solution.py:25
  280.2 8.5 %copy-start.5 = (f32[8,256,256]{2,1,0:T(8,128)S(1)}, f32[8,256,256]{2,1,0:T(8,128)}, u32[]{:S(2)}) copy-start(f32[8,256,256]{2,1,0:T(8,128)} %copy-done.4) | copy-start | bytes 6291460
  288.7 16.4 %copy-start.12 = (f32[8,256,256]{2,1,0:T(8,128)S(1)}, f32[8,256,256]{2,1,0:T(8,128)}, u32[]{:S(2)}) copy-start(f32[8,256,256]{2,1,0:T(8,128)} %copy-done.11) | copy-start | bytes 6291460
  315.3 15.8 %copy-start.15 = (f32[8,256,256]{2,1,0:T(8,128)}, f32[8,256,256]{2,1,0:T(8,128)S(1)}, u32[]{:S(2)}) copy-start(f32[8,256,256]{2,1,0:T(8,128)S(1)} %get-tuple-element.15) | copy-start | bytes 6291460
  315.3 15.8 %copy-start.16 = (f32[8,256,256]{2,1,0:T(8,128)}, f32[8,256,256]{2,1,0:T(8,128)S(1)}, u32[]{:S(2)}) copy-start(f32[8,256,256]{2,1,0:T(8,128)S(1)} %get-tuple-element.46) | copy-start | bytes 6291460
  316.7 14.3 %collective-permute-start.12 = (f32[1,256,256]{2,1,0:T(8,128)S(1)}, f32[1,256,256]{2,1,0:T(8,128)S(1)}, u32[]{:S(2)}, u32[]{:S(2)}) collective-permute-start(f32[1,256,256]{2,1,0:T(8,128)S(1)} %get-tuple-element.53), channel_id=1, source_target_pairs={{1,0},{2,1},{3,2},{4,3},{5,4},{6,5},{7,6},{8,7},{9,8},{10,9},{11,1... | collective-permute-start | bytes 786440 | tf_op jit(solution)/shard_map/ppermute | solution.py:27
  320.4 10.7 %collective-permute-start.13 = (f32[1,256,256]{2,1,0:T(8,128)S(1)}, f32[1,256,256]{2,1,0:T(8,128)S(1)}, u32[]{:S(2)}, u32[]{:S(2)}) collective-permute-start(f32[1,256,256]{2,1,0:T(8,128)S(1)} %get-tuple-element.54), channel_id=1, source_target_pairs={{0,1},{1,2},{2,3},{3,4},{4,5},{5,6},{6,7},{7,8},{8,9},{9,10},{10,1... | collective-permute-start | bytes 786440 | tf_op jit(solution)/shard_map/ppermute | solution.py:25
  322.6 8.5 %copy-start.6 = (f32[8,256,256]{2,1,0:T(8,128)S(1)}, f32[8,256,256]{2,1,0:T(8,128)}, u32[]{:S(2)}) copy-start(f32[8,256,256]{2,1,0:T(8,128)} %copy-done.4) | copy-start | bytes 6291460
  423.8 59.4 %copy-start.23 = (f32[1,2,4096]{2,1,0:T(2,128)S(1)}, f32[1,2,4096]{2,1,0:T(2,128)}, u32[]{:S(2)}) copy-start(f32[1,2,4096]{2,1,0:T(2,128)} %copy-done.22) | copy-start | bytes 98308
  423.8 59.4 %copy-start.25 = (f32[2,4096]{1,0:T(2,128)S(1)}, f32[2,4096]{1,0:T(2,128)}, u32[]{:S(2)}) copy-start(f32[2,4096]{1,0:T(2,128)} %copy-done.24) | copy-start | bytes 98308
where the time goes:
time: 494 us; the launch traced here: 486 us
  other arithmetic  180 us (36%)
  local copies, waits for them, and re-layouts  152 us (31%)
  blocking collectives  107 us (22%)
  starting transfers between devices  40.2 us (8%)
  between operations  5.39 us (1%)
    reshape x1, local copies, waits for them, and re-layouts, restrict(): fine.reshape(plane_count // 4, 4, row_count // 4, 4, column_count // 4, 4)  71.4 us
    reshape x1, local copies, waits for them, and re-layouts, prolong(): return cube.reshape(plane_count * 4, row_count, column_count)  56.1 us
    psum x1, blocking collectives, on_device(): lax.psum(jnp.sum(control + multiplier, axis=0), 'scen') / scen_count  41.1 us
    psum x1, blocking collectives, on_device(): total = lax.psum(gradient, 'scen')  38.5 us
    mul x3, other arithmetic, horizontal(): return -advect + DIFF_FLAT * spread - rate * field  37.5 us
    psum x1, blocking collectives, on_device(): lax.psum((jnp.sum(monitor_float * field * field), jnp.sum(monitor_float))...  27.4 us
    add_any x3, other arithmetic, divergence(): product = backward * forward  26.7 us
    neg x3, other arithmetic, divergence(): backward = field - lower_cells  25.5 us
  transfers between devices with their start and end apart: 14, of which 1 were waited for; matrix products, arithmetic and copies ran while one was open for 26% of the time, Pallas kernels for 0%

commit v1 on v0

v1 whole, which is shorter than its diff:
```python
import functools

import jax
import jax.numpy as jnp
from jax import lax
from jax.experimental import pallas as pl
from jax.experimental.pallas import tpu as pltpu
from jax.sharding import PartitionSpec as P

STEPS = 4
EPS_LIMIT = 0.01
TIME_STEP = 0.25
DIFF_FLAT = 0.1
DIFF_VERTICAL = 0.25
BETA_LEVEL = 0.75
SOFT_WIDTH = 0.25

NZ, NX, NY = 8, 256, 256
HP = NX + 8
ZP = 2 * HP
F0 = 8
ROWS = F0 + NZ * ZP + 8
SEG = HP // 8
VERT = TIME_STEP * DIFF_VERTICAL
KEEP = 1.0 - 2.0 * VERT
f32 = jnp.float32
VM = pl.BlockSpec(memory_space=pltpu.VMEM)
HBM = pl.BlockSpec(memory_space=pltpu.HBM)
FIELD = jax.ShapeDtypeStruct((ROWS, 128), f32)
PLANE = jax.ShapeDtypeStruct((NX, NY), f32)


def seg_load(ref, z, h, r):
    return ref[pl.ds(F0 + z * ZP + h * HP + r, 8, stride=SEG), :]


def seg_store(ref, z, h, r, value):
    ref[pl.ds(F0 + z * ZP + h * HP + r, 8, stride=SEG), :] = value


def block_rows(z, h, j):
    return pl.ds(pl.multiple_of(F0 + z * ZP + h * HP + 8 * j, 8), 8)


def zero_pads(ref):
    zeros = jnp.zeros((8, 128), f32)
    ref[0:8, :] = zeros
    ref[ROWS - 8 : ROWS, :] = zeros
    for z in range(NZ):
        for h in range(2):
            start = F0 + z * ZP + h * HP + NX
            ref[start : start + 8, :] = zeros


def limiter(b, f, sb, sf):
    p = b * f
    q = p * p + EPS_LIMIT * EPS_LIMIT
    s = q * lax.rsqrt(q)
    r = lax.rsqrt(sb + sf + EPS_LIMIT)
    w = (p + s) * (r * r)
    return w * (b * (1.0 / 6.0) + f * (1.0 / 3.0))


def limiter_slopes(b, f, sb, sf):
    p = b * f
    q = p * p + EPS_LIMIT * EPS_LIMIT
    rs = lax.rsqrt(q)
    s = q * rs
    r = lax.rsqrt(sb + sf + EPS_LIMIT)
    r = r * r
    w = (p + s) * r
    u = b * (1.0 / 6.0) + f * (1.0 / 3.0)
    r2 = r + r
    slope_b = (f * rs - b * r2) * u + (1.0 / 6.0)
    slope_f = (b * rs - f * r2) * u + (1.0 / 3.0)
    return w, slope_b, slope_f


def lane_masks():
    lane = lax.broadcasted_iota(jnp.int32, (8, 128), 1)
    sub = lax.broadcasted_iota(jnp.int32, (8, 128), 0)
    return lane == 0, lane == 127, sub < 7


def from_left(pair, first, edge):
    rolled = [pltpu.roll(v, 1, 1) for v in pair]
    return [jnp.where(edge, first, rolled[0]), jnp.where(edge, rolled[0], rolled[1])]


def from_right(pair, last, edge):
    rolled = [pltpu.roll(v, 127, 1) for v in pair]
    return [jnp.where(edge, rolled[1], rolled[0]), jnp.where(edge, last, rolled[1])]


def forward_planes(z, unroll, c_ref, ve_ref, vn_ref, co_ref, out_ref):
    at_first, at_last, inside = lane_masks()
    below = jnp.maximum(z - 1, 0)
    above = jnp.minimum(z + 1, NZ - 1)
    has_below = jnp.where(z > 0, VERT, 0.0)
    has_above = jnp.where(z < NZ - 1, VERT, 0.0)

    def flux(v, c, b, f, sb, sf):
        return v * (c + limiter(b, f, sb, sf)) - DIFF_FLAT * f

    def one(r, c, b, sb, before):
        after = [seg_load(c_ref, z, h, r + 1) for h in (0, 1)]
        left = from_left(c, 0.0, at_first)
        right = from_right(c, 0.0, at_last)
        f, sf, gx, gy = [], [], [], []
        for h in (0, 1):
            fx = after[h] - c[h]
            sx = fx * fx
            gx.append(flux(seg_load(ve_ref, z, h, r), c[h], b[h], fx, sb[h], sx))
            by = c[h] - left[h]
            fy = right[h] - c[h]
            gy.append(flux(seg_load(vn_ref, z, h, r), c[h], by, fy, by * by, fy * fy))
            f.append(fx)
            sf.append(sx)
        gl = from_left(gy, -DIFF_FLAT * c[0], at_first)
        for h in (0, 1):
            vertical = has_below * seg_load(c_ref, below, h, r) + has_above * seg_load(c_ref, above, h, r)
            keep = KEEP if co_ref is None else seg_load(co_ref, z, h, r)
            out = keep * c[h] + vertical - TIME_STEP * ((gx[h] - before[h]) + (gy[h] - gl[h]))
            seg_store(out_ref, z, h, r, jnp.where(inside | (r < NX - 7 * SEG), out, 0.0))
        return after, f, sf, gx

    c, b, sb, before = [], [], [], []
    for h in (0, 1):
        m2 = seg_load(c_ref, z, h, -2)
        m1 = seg_load(c_ref, z, h, -1)
        c0 = seg_load(c_ref, z, h, 0)
        bm = m1 - m2
        fm = c0 - m1
        sm = fm * fm
        before.append(flux(seg_load(ve_ref, z, h, -1), m1, bm, fm, bm * bm, sm))
        c.append(c0)
        b.append(fm)
        sb.append(sm)

    def block(i, carry):
        for j in range(unroll):
            carry = one(i * unroll + j, *carry)
        return carry

    lax.fori_loop(0, SEG // unroll, block, (c, b, sb, before))


def first_kernel(start_ref, east_ref, north_ref, c_ref, ve_ref, vn_ref, out_ref, sem):
    def copies(z):
        made = []
        for source, target in ((start_ref, c_ref), (east_ref, ve_ref), (north_ref, vn_ref)):
            for h in (0, 1):
                made.append(
                    pltpu.make_async_copy(
                        source.at[0, z, :, pl.ds(h * 128, 128)],
                        target.at[pl.ds(pl.multiple_of(F0 + z * ZP + h * HP, 8), NX), :],
                        sem.at[z, len(made)],
                    )
                )
        return made

    for z in range(NZ):
        for copy in copies(z):
            copy.start()
    for ref in (c_ref, ve_ref, vn_ref, out_ref):
        zero_pads(ref)
    for copy in copies(0):
        copy.wait()

    def plane(z, unused):
        @pl.when(z < NZ - 1)
        def _():
            for copy in copies(z + 1):
                copy.wait()

        forward_planes(z, 11, c_ref, ve_ref, vn_ref, None, out_ref)
        return unused

    lax.fori_loop(0, NZ, plane, 0)


def step_kernel(c_ref, ve_ref, vn_ref, co_ref, out_ref):
    zero_pads(out_ref)

    def plane(z, unused):
        forward_planes(z, 11, c_ref, ve_ref, vn_ref, co_ref, out_ref)
        return unused

    lax.fori_loop(0, NZ, plane, 0)


def facing():
    z_chip = jnp.where(lax.axis_index("slab") % 2 == 0, NZ - 1, 0)
    return z_chip, NZ - 1 - z_chip


def fix_planes(chip_ref, near_ref, field_ref, target_ref, send_chip_ref, send_near_ref):
    z_chip, z_near = facing()

    def block(j, unused):
        for h in (0, 1):
            lanes = slice(h * 128, h * 128 + 128)
            rows = pl.ds(pl.multiple_of(8 * j, 8), 8)
            for z, halo_ref, send_ref in ((z_chip, chip_ref, send_chip_ref), (z_near, near_ref, send_near_ref)):
                value = field_ref[block_rows(z, h, j), :] + VERT * halo_ref[rows, lanes]
                target_ref[block_rows(z, h, j), :] = value
                if send_ref is not None:
                    send_ref[rows, lanes] = value
        return unused

    lax.fori_loop(0, NX // 8, block, 0, unroll=4)


def fix_kernel(chip_ref, near_ref, field_ref, out_ref, send_chip_ref, send_near_ref):
    fix_planes(chip_ref, near_ref, field_ref, out_ref, send_chip_ref, send_near_ref)


def send_planes(field_ref, send_chip_ref, send_near_ref):
    z_chip, z_near = facing()

    def block(j, unused):
        for h in (0, 1):
            lanes = slice(h * 128, h * 128 + 128)
            rows = pl.ds(pl.multiple_of(8 * j, 8), 8)
            send_chip_ref[rows, lanes] = field_ref[block_rows(z_chip, h, j), :]
            send_near_ref[rows, lanes] = field_ref[block_rows(z_near, h, j), :]
        return unused

    lax.fori_loop(0, NX // 8, block, 0, unroll=4)


def mask_copies(mask_hbm, mask_ref, sem):
    return [
        pltpu.make_async_copy(mask_hbm.at[z], mask_ref.at[z], sem.at[z]) for z in range(NZ)
    ]


def rate_kernel(chip_ref, near_ref, field_ref, c0_ref, cons_ref, wells_hbm, out_ref, send_chip_ref, send_near_ref, co_ref, wells_ref, sem):
    copies = mask_copies(wells_hbm, wells_ref, sem)
    for copy in copies:
        copy.start()
    lane = lax.broadcasted_iota(jnp.int32, (8, 128), 1)
    sub = lax.broadcasted_iota(jnp.int32, (8, 128), 0)
    base = jnp.where(sub < 4, 0, 64) + lane // 4
    zero_pads(co_ref)
    for copy in copies:
        copy.wait()

    def block(j, unused):
        for h in (0, 1):
            for p in (0, 1):
                coarse = cons_ref[pl.ds(p, 1), pl.ds(pl.multiple_of(j * 128, 128), 128)]
                wide = jnp.broadcast_to(coarse * TIME_STEP, (8, 128))
                wide = jnp.take_along_axis(wide, base + 32 * h, axis=1)
                for z in range(4 * p, 4 * p + 4):
                    wells = wells_ref[z, pl.ds(pl.multiple_of(8 * j, 8), 8), h * 128 : h * 128 + 128]
                    rate = wells.astype(f32) * wide
                    at = block_rows(z, h, j)
                    co_ref[at, :] = KEEP - rate
                    out_ref[at, :] = field_ref[at, :] - rate * c0_ref[at, :]
        return unused

    lax.fori_loop(0, NX // 8, block, 0)
    fix_planes(chip_ref, near_ref, out_ref, out_ref, send_chip_ref, send_near_ref)


def seed_kernel(chip_ref, near_ref, ahead_ref, monitors_hbm, final_hbm, adjoint_ref, send_chip_ref, send_near_ref, sums_ref, field_ref, c_ref, monitors_ref, sem, out_sem):
    copies = mask_copies(monitors_hbm, monitors_ref, sem)
    for copy in copies:
        copy.start()
    zero_pads(adjoint_ref)
    fix_planes(chip_ref, near_ref, ahead_ref, field_ref, None, None)
    for copy in copies:
        copy.wait()

    def block(j, sums):
        mass, count = sums
        for z in range(NZ):
            for h in (0, 1):
                rows = pl.ds(pl.multiple_of(8 * j, 8), 8)
                value = field_ref[block_rows(z, h, j), :]
                c_ref[z, rows, h * 128 : h * 128 + 128] = value
                monitor = monitors_ref[z, rows, h * 128 : h * 128 + 128].astype(f32)
                seed = monitor * value
                adjoint_ref[block_rows(z, h, j), :] = seed
                mass = mass + seed * value
                count = count + monitor
        return mass, count

    zeros = jnp.zeros((8, 128), f32)
    mass, count = lax.fori_loop(0, NX // 8, block, (zeros, zeros))
    out = pltpu.make_async_copy(c_ref, final_hbm.at[0], out_sem)
    out.start()
    sums_ref[0:8, :] = jnp.broadcast_to(jnp.sum(jnp.sum(mass, axis=0, keepdims=True), axis=1, keepdims=True), (8, 128))
    sums_ref[8:16, :] = jnp.broadcast_to(jnp.sum(jnp.sum(count, axis=0, keepdims=True), axis=1, keepdims=True), (8, 128))
    send_planes(adjoint_ref, send_chip_ref, send_near_ref)
    out.wait()


def adjoint_planes(z, unroll, c_ref, a_ref, ve_ref, vn_ref, co_ref, rg_in_ref, out_ref, rg_ref):
    at_first, at_last, inside = lane_masks()
    below = jnp.maximum(z - 1, 0)
    above = jnp.minimum(z + 1, NZ - 1)
    has_below = jnp.where(z > 0, VERT, 0.0)
    has_above = jnp.where(z < NZ - 1, VERT, 0.0)

    def parts(v, g, b, f, sb, sf):
        w, slope_b, slope_f = limiter_slopes(b, f, sb, sf)
        direct = v * g
        scaled = direct * w
        return direct, scaled * slope_b, scaled * slope_f - DIFF_FLAT * g

    def along_x(r, c, b, sb, a):
        after = [seg_load(c_ref, z, h, r + 1) for h in (0, 1)]
        next_a = [seg_load(a_ref, z, h, r + 1) for h in (0, 1)]
        f, sf, direct, back, front = [], [], [], [], []
        for h in (0, 1):
            fx = after[h] - c[h]
            sx = fx * fx
            d, k, n = parts(seg_load(ve_ref, z, h, r), next_a[h] - a[h], b[h], fx, sb[h], sx)
            f.append(fx)
            sf.append(sx)
            direct.append(d)
            back.append(k)
            front.append(n)
        return after, f, sf, next_a, direct, back, front

    def along_y(r, c, a):
        left = from_left(c, 0.0, at_first)
        right = from_right(c, 0.0, at_last)
        next_a = from_right(a, 0.0, at_last)
        direct, back, front = [], [], []
        for h in (0, 1):
            by = c[h] - left[h]
            fy = right[h] - c[h]
            d, k, n = parts(seg_load(vn_ref, z, h, r), next_a[h] - a[h], by, fy, by * by, fy * fy)
            direct.append(d)
            back.append(k)
            front.append(n)
        fl = from_left(front, -DIFF_FLAT * a[0], at_first)
        kr = from_right(back, 0.0, at_last)
        return [direct[h] + (back[h] - front[h]) + fl[h] - kr[h] for h in (0, 1)]

    def row(r, c, b, sb, a, before):
        after, f, sf, next_a, direct, back, front = along_x(r, c, b, sb, a)
        flat = along_y(r, c, a)
        pulled = []
        for h in (0, 1):
            vertical = has_below * seg_load(a_ref, below, h, r) + has_above * seg_load(a_ref, above, h, r)
            grad = c[h] * a[h]
            if rg_in_ref is not None:
                grad = grad + seg_load(rg_in_ref, z, h, r)
            seg_store(rg_ref, z, h, r, grad)
            here = flat[h] + direct[h] + (back[h] - front[h]) + before[h]
            pulled.append(seg_load(co_ref, z, h, r) * a[h] + vertical + TIME_STEP * here)
        return after, f, sf, next_a, front, back, pulled

    start_c, start_b, start_s, start_a = [], [], [], []
    for h in (0, 1):
        m2 = seg_load(c_ref, z, h, -2)
        m1 = seg_load(c_ref, z, h, -1)
        bm = m1 - m2
        start_c.append(m1)
        start_b.append(bm)
        start_s.append(bm * bm)
        start_a.append(seg_load(a_ref, z, h, -1))
    c, b, sb, a, _, _, before = along_x(-1, start_c, start_b, start_s, start_a)
    zeros = [jnp.zeros((8, 128), f32)] * 2

    def block(i, carry):
        c, b, sb, a, before, pulled = carry
        for j in range(unroll):
            r = i * unroll + j
            c, b, sb, a, before, back, new = row(r, c, b, sb, a, before)
            for h in (0, 1):
                out = pulled[h] - TIME_STEP * back[h]
                seg_store(out_ref, z, h, r - 1, jnp.where(inside | (r - 1 < NX - 7 * SEG), out, 0.0))
            pulled = new
        return c, b, sb, a, before, pulled

    c, b, sb, a, before, pulled = lax.fori_loop(0, SEG // unroll, block, (c, b, sb, a, before, zeros))
    last = along_x(SEG, c, b, sb, a)
    for h in (0, 1):
        out = pulled[h] - TIME_STEP * last[5][h]
        seg_store(out_ref, z, h, SEG - 1, jnp.where(inside, out, 0.0))


def adjoint_kernel(c_ref, a_ref, ve_ref, vn_ref, co_ref, *rest):
    rg_in_ref = rest[0] if len(rest) == 3 else None
    out_ref, rg_ref = rest[-2:]

    def plane(z, unused):
        adjoint_planes(z, 11, c_ref, a_ref, ve_ref, vn_ref, co_ref, rg_in_ref, out_ref, rg_ref)
        return unused

    lax.fori_loop(0, NZ, plane, 0)
    zero_pads(out_ref)


def restrict_kernel(chip_ref, near_ref, ahead_ref, c0_ref, rg_ref, wells_hbm, out_ref, field_ref, wide_ref, wells_ref, sem):
    copies = mask_copies(wells_hbm, wells_ref, sem)
    for copy in copies:
        copy.start()
    fix_planes(chip_ref, near_ref, ahead_ref, field_ref, None, None)
    for copy in copies:
        copy.wait()

    def block(j, unused):
        for h in (0, 1):
            for p in (0, 1):
                total = jnp.zeros((8, 128), f32)
                for z in range(4 * p, 4 * p + 4):
                    at = block_rows(z, h, j)
                    rows = pl.ds(pl.multiple_of(8 * j, 8), 8)
                    wells = wells_ref[z, rows, h * 128 : h * 128 + 128].astype(f32)
                    total = total + wells * (rg_ref[at, :] + c0_ref[at, :] * field_ref[at, :])
                wide_ref[p, pl.ds(pl.multiple_of(8 * j, 8), 8), h * 128 : h * 128 + 128] = total
        return unused

    lax.fori_loop(0, NX // 8, block, 0)
    fine = lax.broadcasted_iota(jnp.int32, (NY, 128), 0) // 4
    coarse = lax.broadcasted_iota(jnp.int32, (NY, 128), 1) % 64
    sums = jnp.where(fine == coarse, 1.0, 0.0).astype(f32)
    row = lax.broadcasted_iota(jnp.int32, (NX, 128), 0) % 8
    lane = lax.broadcasted_iota(jnp.int32, (NX, 128), 1)
    own = (row < 4) == (lane < 64)
    for p in (0, 1):
        part = jnp.dot(wide_ref[p], sums, precision=lax.Precision.HIGHEST, preferred_element_type=f32)
        part = jnp.where(own, part, 0.0).reshape(NX // 8, 8, 128).sum(axis=1)
        for j in range(NX // 8):
            out_ref[p : p + 1, j * 128 : (j + 1) * 128] = part[j : j + 1, :]


def call(kernel, name, flops, **kwargs):
    return pl.pallas_call(
        kernel,
        name=name,
        compiler_params=pltpu.CompilerParams(vmem_limit_bytes=8 << 20),
        cost_estimate=pl.CostEstimate(flops=flops, bytes_accessed=1 << 20, transcendentals=0),
        **kwargs,
    )


def dma(*shape):
    return pltpu.SemaphoreType.DMA(shape)


def pairs_sum(value, axis, size, steps):
    for step in steps:
        value = value + lax.ppermute(value, axis, [(i, i ^ step) for i in range(size)])
    return value


def scen_sum(value):
    others = [lax.ppermute(value, "scen", [(i, (i & 4) | ((i + k) & 3)) for i in range(8)]) for k in (1, 2, 3)]
    value = (value + others[0]) + (others[1] + others[2])
    return value + lax.ppermute(value, "scen", [(i, i ^ 4) for i in range(8)])


def swap(slab_count, send_chip, send_near):
    near = []
    for i in range(1, slab_count - 1, 2):
        near += [(i, i + 1), (i + 1, i)]
    got_near = lax.ppermute(send_near, "slab", near)
    got_chip = lax.ppermute(send_chip, "slab", [(i, i ^ 1) for i in range(slab_count)])
    return got_chip, got_near


def on_device(start, flow_east, flow_north, wells, monitors, control, multiplier, threshold):
    scen_count = lax.axis_size("scen")
    slab_count = lax.axis_size("slab")
    odd = lax.axis_index("slab") % 2
    in_hbm = functools.partial(pltpu.with_memory_space_constraint, memory_space=pltpu.HBM)
    half = (2, 4096)

    low, high = start[0, 0], start[0, NZ - 1]
    halos = swap(slab_count, jnp.where(odd == 0, high, low), jnp.where(odd == 0, low, high))
    consensus = scen_sum((control + multiplier)[0]) / scen_count

    c0, ve, vn, ahead = call(
        first_kernel, "step0", 3 << 30,
        in_specs=[HBM] * 3, out_specs=[VM] * 4, out_shape=[FIELD] * 4, scratch_shapes=[dma(NZ, 6)],
    )(in_hbm(start), in_hbm(flow_east), in_hbm(flow_north))
    c, send_chip, send_near, co = call(
        rate_kernel, "rate", 1 << 28,
        in_specs=[VM] * 5 + [HBM], out_specs=[VM] * 4, out_shape=[FIELD, PLANE, PLANE, FIELD],
        scratch_shapes=[pltpu.VMEM((NZ, NX, NY), jnp.int32), dma(NZ)],
        input_output_aliases={2: 0},
    )(*halos, ahead, c0, consensus, in_hbm(wells))
    states = [c0, c]
    for k in range(1, STEPS):
        halos = swap(slab_count, send_chip, send_near)
        ahead = call(step_kernel, f"step{k}", 3 << 30, in_specs=[VM] * 4, out_specs=VM, out_shape=FIELD)(c, ve, vn, co)
        if k < STEPS - 1:
            c, send_chip, send_near = call(
                fix_kernel, f"fix{k}", 1 << 26,
                in_specs=[VM] * 3, out_specs=[VM] * 3, out_shape=[FIELD, PLANE, PLANE],
                input_output_aliases={2: 0},
            )(*halos, ahead)
            states.append(c)
    final, adjoint, send_chip, send_near, sums, unused = call(
        seed_kernel, "seed", 1 << 28,
        in_specs=[VM] * 3 + [HBM], out_specs=[HBM] + [VM] * 5,
        out_shape=[jax.ShapeDtypeStruct((1, NZ, NX, NY), f32), FIELD, PLANE, PLANE, jax.ShapeDtypeStruct((16, 128), f32), FIELD],
        input_output_aliases={2: 5},
        scratch_shapes=[pltpu.VMEM((NZ, NX, NY), f32), pltpu.VMEM((NZ, NX, NY), jnp.int32), dma(NZ), pltpu.SemaphoreType.DMA],
    )(*halos, ahead, in_hbm(monitors))
    grads = ()
    rounds = [1, 2, 4, 8]
    for k in range(STEPS - 1, 0, -1):
        halos = swap(slab_count, send_chip, send_near)
        sums = pairs_sum(sums, "slab", slab_count, rounds[:1])
        rounds = rounds[1:]
        ahead, grad = call(
            adjoint_kernel, f"adjoint{k}", 4 << 30,
            in_specs=[VM] * (5 + len(grads)), out_specs=[VM] * 2, out_shape=[FIELD] * 2,
            input_output_aliases={5: 1} if grads else {},
        )(states[k], adjoint, ve, vn, co, *grads)
        sums, ahead, grad = lax.optimization_barrier((sums, ahead, grad))
        grads = (grad,)
        if k > 1:
            adjoint, send_chip, send_near = call(
                fix_kernel, f"back{k}", 1 << 26,
                in_specs=[VM] * 3, out_specs=[VM] * 3, out_shape=[FIELD, PLANE, PLANE],
                input_output_aliases={2: 0},
            )(*halos, ahead)
    coarse, unused = call(
        restrict_kernel, "restrict", 1 << 28,
        in_specs=[VM] * 5 + [HBM], out_specs=[VM] * 2, out_shape=[jax.ShapeDtypeStruct(half, f32), FIELD],
        input_output_aliases={2: 1},
        scratch_shapes=[pltpu.VMEM((2, NX, NY), f32), pltpu.VMEM((NZ, NX, NY), jnp.int32), dma(NZ)],
    )(*halos, ahead, c0, grad, in_hbm(wells))

    sums = pairs_sum(sums, "slab", slab_count, rounds)
    mass, count = sums[0:1], jnp.maximum(sums[8:9], 1.0)
    scaled = (mass / count - threshold[0]) / SOFT_WIDTH
    share = 1.0 / ((1.0 - BETA_LEVEL) * scen_count)
    weight = jax.nn.sigmoid(scaled) * share
    soft_term = SOFT_WIDTH * jax.nn.softplus(scaled) * share
    risk = scen_sum(soft_term)
    coarse_cells = NZ * slab_count * NX * NY / 64.0
    scale = (weight * 2.0 / count * (-TIME_STEP * coarse_cells))[0, 0]
    total = scen_sum(coarse * scale)
    consensus_next = consensus - total
    multiplier_next = multiplier + control - consensus_next[None]
    return (final, consensus_next, multiplier_next, threshold + risk[0, :1])


def solution(mesh):
    placed = (
        P("scen", "slab", None, None),
        P("scen", "slab", None, None),
        P("scen", "slab", None, None),
        P("slab", None, None),
        P("slab", None, None),
        P("scen", "slab", None),
        P("scen", "slab", None),
        P(),
    )
    return jax.shard_map(
        on_device,
        mesh=mesh,
        in_specs=placed,
        out_specs=(P("scen", "slab", None, None), P("slab", None), P("scen", "slab", None), P()),
        check_vma=False,
    )
```

time: 494 us -> 144 us (0.29); the launches traced: 486 us -> 141 us
  other arithmetic: 180 us -> 2.75 us
  local copies, waits for them, and re-layouts: 152 us -> 0 us
  blocking collectives: 107 us -> 0 us
  Pallas kernels: 0 us -> 68.7 us
  waiting for transfers between devices: 1.14 us -> 14.6 us
  starting transfers between devices: 40.2 us -> 52.6 us
    reshape x2 -> x0, local copies, waits for them, and re-layouts: 127 us -> none  [the longest x1 71.4 us: restrict(): fine.reshape(plane_count // 4, 4, row_count // 4, 4, column_count // 4, 4)]
    psum x3 -> x0, blocking collectives: 107 us -> none  [the longest x1 41.1 us: on_device(): lax.psum(jnp.sum(control + multiplier, axis=0), 'scen') / scen_count]
    mul x9 -> x3, other arithmetic: 82.5 us -> 0.08 us  [the longest x1 0.05 us: on_device(): total = scen_sum(coarse * scale)]
    pallas_call x0 -> x14, Pallas kernels: none -> 68.7 us  [the longest x3 27.8 us: on_device(): call(adjoint_kernel, f'adjoint{k}', 4 << 30, in_specs=[VM] * (5 + len(gra...]
    add_any x3 -> x0, other arithmetic: 26.7 us -> none  [divergence(): product = backward * forward]
    reduce_sum x2 -> x0, other arithmetic: 25.8 us -> none  [the longest x1 20.8 us: restrict(): fine.reshape(plane_count // 4, 4, row_count // 4, 4, column_count // 4, 4)]
    neg x3 -> x0, other arithmetic: 25.5 us -> none  [divergence(): backward = field - lower_cells]
    broadcast_in_dim x2 -> x0, local copies, waits for them, and re-layouts: 21.6 us -> none  [prolong(): jnp.broadcast_to(cube, (plane_count, 4, row_count // 4, 4, column_count /...]
  transfers between devices with their start and end apart: 14 -> 30, of which waited for: 1 -> 4; matrix products, arithmetic and copies ran while one was open for 26% -> 1% of each run, Pallas kernels for 0% -> 33%
where the time goes in v1:
time: 144 us; the launch traced here: 141 us
  Pallas kernels  68.7 us (48%)
  starting transfers between devices  52.6 us (37%)
  waiting for transfers between devices  14.6 us (10%)
  between operations  2.84 us (2%)
  other arithmetic  2.75 us (2%)
    pallas_call x3, Pallas kernels, on_device(): call(adjoint_kernel, f'adjoint{k}', 4 << 30, in_specs=[VM] * (5 + len(gra...  27.8 us
    pallas_call x3, Pallas kernels, on_device(): call(step_kernel, f'step{k}', 3 << 30, in_specs=[VM] * 4, out_specs=VM, o...  19.2 us
    ppermute x7, starting transfers between devices, swap(): got_near = lax.ppermute(send_near, 'slab', near)  14.9 us
    ppermute x9, starting transfers between devices, scen_sum(): lax.ppermute(value, 'scen', [(i, i & 4 | i + k & 3) for i in range(8)])  14.8 us
    ppermute x4, starting transfers between devices, pairs_sum(): lax.ppermute(value, axis, [(i, i ^ step) for i in range(size)])  9.52 us
    pallas_call x1, Pallas kernels, on_device(): call(first_kernel, 'step0', 3 << 30, in_specs=[HBM] * 3, out_specs=[VM] *...  8.29 us
    ppermute x7, starting transfers between devices, swap(): lax.ppermute(send_chip, 'slab', [(i, i ^ 1) for i in range(slab_count)])  7.15 us
    ppermute x7, waiting for transfers between devices, swap(): got_near = lax.ppermute(send_near, 'slab', near)  6.59 us
  transfers between devices with their start and end apart: 30, of which 4 were waited for; matrix products, arithmetic and copies ran while one was open for 1% of the time, Pallas kernels for 33%

profile of v1, /device:TPU:2, one launch (start us, length us, event | category | flops | bytes accessed | tf_op | source)
XLA Modules:
  0.0 141.4 jit_solution(3860682493919066689)
XLA Ops:
  0.6 0.8 add.67
  1.4 1.6 %collective-permute-start.2 = (f32[2,4096]{1,0:T(2,128)S(1)}, f32[2,4096]{1,0:T(2,128)S(1)}, u32[]{:S(2)}, u32[]{:S(2)}) collective-permute-start(f32[2,4096]{1,0:T(2,128)S(1)} %bitcast.14), channel_id=1, source_target_pairs={{0,16},{16,32},{32,48},{48,0},{64,80},{80,96},{96,112},{112,64},{1... | collective-permute-start | bytes 98312 | tf_op jit(solution)/shard_map/ppermute | solution.py:455
  3.1 2.9 %collective-permute-start.3 = (f32[2,4096]{1,0:T(2,128)S(1)}, f32[2,4096]{1,0:T(2,128)S(1)}, u32[]{:S(2)}, u32[]{:S(2)}) collective-permute-start(f32[2,4096]{1,0:T(2,128)S(1)} %bitcast.15), channel_id=1, source_target_pairs={{0,32},{16,48},{32,0},{48,16},{64,96},{80,112},{96,64},{112,80},{1... | collective-permute-start | bytes 98312 | tf_op jit(solution)/shard_map/ppermute | solution.py:455
  6.0 1.3 collective-permute-start.4
  7.3 1.1 select_bitcast_fusion
  8.5 2.5 %collective-permute-start.1 = (f32[256,256]{1,0:T(8,128)S(1)}, f32[256,256]{1,0:T(8,128)S(1)}, u32[]{:S(2)}, u32[]{:S(2)}) collective-permute-start(f32[256,256]{1,0:T(8,128)S(1)} %get-tuple-element.90), channel_id=1, source_target_pairs={{1,2},{2,1},{3,4},{4,3},{5,6},{6,5},{7,8},{8,7},{9,10},{10,9},{11,... | collective-permute-start | bytes 786440 | tf_op jit(solution)/shard_map/ppermute | solution.py:464
  11.1 2.5 %collective-permute-start.5 = (f32[2,4096]{1,0:T(2,128)S(1)}, f32[2,4096]{1,0:T(2,128)S(1)}, u32[]{:S(2)}, u32[]{:S(2)}) collective-permute-start(f32[2,4096]{1,0:T(2,128)S(1)} %add_add_fusion.1), channel_id=1, source_target_pairs={{0,64},{16,80},{32,96},{48,112},{64,0},{80,16},{96,32},{112,48},{1... | collective-permute-start | bytes 98312 | tf_op jit(solution)/shard_map/ppermute | solution.py:457
  13.6 8.3 %step0.1 = (f32[4240,128]{1,0:T(8,128)S(1)}, f32[4240,128]{1,0:T(8,128)S(1)}, f32[4240,128]{1,0:T(8,128)S(1)}, f32[4240,128]{1,0:T(8,128)S(1)}) custom-call(f32[1,8,256,256]{3,2,1,0:T(8,128)} %start_ref.1, f32[1,8,256,256]{3,2,1,0:T(8,128)} %east_ref.1, f32[1,8,256,256]{3,2,1,0:T(8,128)} %north_ref.1), custom_call_target="tpu_custom_call" | custom-call | flops 3221225472 | bytes 1048576 | tf_op jit(solution)/shard_map/step0/pallas_call | solution.py:480
  22.0 5.4 %rate.1 = (f32[4240,128]{1,0:T(8,128)S(1)}, f32[256,256]{1,0:T(8,128)S(1)}, f32[256,256]{1,0:T(8,128)S(1)}, f32[4240,128]{1,0:T(8,128)S(1)}) custom-call(f32[256,256]{1,0:T(8,128)S(1)} %collective-permute-done.chip_ref, f32[256,256]{1,0:T(8,128)S(1)} %collective-permute-done.1.near_ref, ...), custom_call_target="tpu_custom_call", output_to_operand_aliasing={{0}: (2, {})} | custom-call | flops 268435456 | bytes 1048576 | tf_op jit(solution)/shard_map/rate/pallas_call | solution.py:484
  27.4 1.2 collective-permute-start.6
  28.6 2.0 %collective-permute-start.7 = (f32[256,256]{1,0:T(8,128)S(1)}, f32[256,256]{1,0:T(8,128)S(1)}, u32[]{:S(2)}, u32[]{:S(2)}) collective-permute-start(f32[256,256]{1,0:T(8,128)S(1)} %get-tuple-element.48), channel_id=1, source_target_pairs={{1,2},{2,1},{3,4},{4,3},{5,6},{6,5},{7,8},{8,7},{9,10},{10,9},{11,... | collective-permute-start | bytes 786440 | tf_op jit(solution)/shard_map/ppermute | solution.py:464
  30.6 6.4 %step1.1.field_ref = f32[4240,128]{1,0:T(8,128)S(1)} custom-call(f32[4240,128]{1,0:T(8,128)S(1)} %get-tuple-element.49.c_ref, f32[4240,128]{1,0:T(8,128)S(1)} %get-tuple-element.50.ve_ref, f32[4240,128]{1,0:T(8,128)S(1)} %get-tuple-element.51.vn_ref, f32[4240,128]{1,0:T(8,128)S(1)} %get-tuple-element.52.co_ref), custom_call_target="tpu_custom_call" | custom-call | flops 3221225472 | bytes 1048576 | tf_op jit(solution)/shard_map/step1/pallas_call | solution.py:493
  37.0 0.3 fix1.1
  37.3 2.8 %collective-permute-start.8 = (f32[256,256]{1,0:T(8,128)S(1)}, f32[256,256]{1,0:T(8,128)S(1)}, u32[]{:S(2)}, u32[]{:S(2)}) collective-permute-start(f32[256,256]{1,0:T(8,128)S(1)} %get-tuple-element.53), channel_id=1, source_target_pairs={{0,1},{1,0},{2,3},{3,2},{4,5},{5,4},{6,7},{7,6},{8,9},{9,8},{10,11... | collective-permute-start | bytes 786440 | tf_op jit(solution)/shard_map/ppermute | solution.py:465
  40.1 1.9 %collective-permute-start.9 = (f32[256,256]{1,0:T(8,128)S(1)}, f32[256,256]{1,0:T(8,128)S(1)}, u32[]{:S(2)}, u32[]{:S(2)}) collective-permute-start(f32[256,256]{1,0:T(8,128)S(1)} %get-tuple-element.54), channel_id=1, source_target_pairs={{1,2},{2,1},{3,4},{4,3},{5,6},{6,5},{7,8},{8,7},{9,10},{10,9},{11,... | collective-permute-start | bytes 786440 | tf_op jit(solution)/shard_map/ppermute | solution.py:464
  42.1 6.4 %step2.1.field_ref = f32[4240,128]{1,0:T(8,128)S(1)} custom-call(f32[4240,128]{1,0:T(8,128)S(1)} %get-tuple-element.55.c_ref, f32[4240,128]{1,0:T(8,128)S(1)} %get-tuple-element.50.ve_ref, f32[4240,128]{1,0:T(8,128)S(1)} %get-tuple-element.51.vn_ref, f32[4240,128]{1,0:T(8,128)S(1)} %get-tuple-element.52.co_ref), custom_call_target="tpu_custom_call" | custom-call | flops 3221225472 | bytes 1048576 | tf_op jit(solution)/shard_map/step2/pallas_call | solution.py:493
  48.5 0.3 fix2.1
  48.8 2.7 %collective-permute-start.10 = (f32[256,256]{1,0:T(8,128)S(1)}, f32[256,256]{1,0:T(8,128)S(1)}, u32[]{:S(2)}, u32[]{:S(2)}) collective-permute-start(f32[256,256]{1,0:T(8,128)S(1)} %get-tuple-element.56), channel_id=1, source_target_pairs={{0,1},{1,0},{2,3},{3,2},{4,5},{5,4},{6,7},{7,6},{8,9},{9,8},{10,11... | collective-permute-start | bytes 786440 | tf_op jit(solution)/shard_map/ppermute | solution.py:465
  51.5 1.9 %collective-permute-start.11 = (f32[256,256]{1,0:T(8,128)S(1)}, f32[256,256]{1,0:T(8,128)S(1)}, u32[]{:S(2)}, u32[]{:S(2)}) collective-permute-start(f32[256,256]{1,0:T(8,128)S(1)} %get-tuple-element.57), channel_id=1, source_target_pairs={{1,2},{2,1},{3,4},{4,3},{5,6},{6,5},{7,8},{8,7},{9,10},{10,9},{11,... | collective-permute-start | bytes 786440 | tf_op jit(solution)/shard_map/ppermute | solution.py:464
  53.4 6.4 %step3.1.ahead_ref = f32[4240,128]{1,0:T(8,128)S(1)} custom-call(f32[4240,128]{1,0:T(8,128)S(1)} %get-tuple-element.58.c_ref, f32[4240,128]{1,0:T(8,128)S(1)} %get-tuple-element.50.ve_ref, f32[4240,128]{1,0:T(8,128)S(1)} %get-tuple-element.51.vn_ref, f32[4240,128]{1,0:T(8,128)S(1)} %get-tuple-element.52.co_ref), custom_call_target="tpu_custom_call" | custom-call | flops 3221225472 | bytes 1048576 | tf_op jit(solution)/shard_map/step3/pallas_call | solution.py:493
  59.8 3.6 %seed.1 = (f32[1,8,256,256]{3,2,1,0:T(8,128)}, f32[4240,128]{1,0:T(8,128)S(1)}, f32[256,256]{1,0:T(8,128)S(1)}, f32[256,256]{1,0:T(8,128)S(1)}, f32[16,128]{1,0:T(8,128)S(1)}, /*index=5*/f32[4240,128]{1,0:T(8,128)S(1)}) custom-call(f32[256,256]{1,0:T(8,128)S(1)} %collective-permute-done.10.chip_ref, ...), custom_call_target="tpu_custom_call", output_to_operand_aliasing={{5}: (2, {})} | custom-call | flops 268435456 | bytes 1048576 | tf_op jit(solution)/shard_map/seed/pallas_call | solution.py:501
  63.5 3.0 %collective-permute-start.14 = (f32[16,128]{1,0:T(8,128)S(1)}, f32[16,128]{1,0:T(8,128)S(1)}, u32[]{:S(2)}, u32[]{:S(2)}) collective-permute-start(f32[16,128]{1,0:T(8,128)S(1)} %get-tuple-element.62), channel_id=1, source_target_pairs={{0,1},{1,0},{2,3},{3,2},{4,5},{5,4},{6,7},{7,6},{8,9},{9,8},{10,11... | collective-permute-start | bytes 24584 | tf_op jit(solution)/shard_map/ppermute | solution.py:450
  66.5 0.1 collective-permute-start.12
  66.6 1.9 %collective-permute-start.13 = (f32[256,256]{1,0:T(8,128)S(1)}, f32[256,256]{1,0:T(8,128)S(1)}, u32[]{:S(2)}, u32[]{:S(2)}) collective-permute-start(f32[256,256]{1,0:T(8,128)S(1)} %get-tuple-element.61), channel_id=1, source_target_pairs={{1,2},{2,1},{3,4},{4,3},{5,6},{6,5},{7,8},{8,7},{9,10},{10,9},{11,... | collective-permute-start | bytes 786440 | tf_op jit(solution)/shard_map/ppermute | solution.py:464
  68.6 9.3 %adjoint3.1 = (f32[4240,128]{1,0:T(8,128)S(1)}, f32[4240,128]{1,0:T(8,128)S(1)}) custom-call(f32[4240,128]{1,0:T(8,128)S(1)} %get-tuple-element.58.c_ref, f32[4240,128]{1,0:T(8,128)S(1)} %get-tuple-element.63.a_ref, f32[4240,128]{1,0:T(8,128)S(1)} %get-tuple-element.50.ve_ref, f32[4240,128]{1,0:T(8,128)S(1)} %get-tuple-element.51.vn_ref, ...), custom_call_target="tpu_custom_call" | custom-call | flops 4294967296 | bytes 1048576 | tf_op jit(solution)/shard_map/adjoint3/pallas_call | solution.py:514
  78.0 3.6 %collective-permute-done.17 = f32[16,128]{1,0:T(8,128)S(1)} collective-permute-done((f32[16,128]{1,0:T(8,128)S(1)}, f32[16,128]{1,0:T(8,128)S(1)}, u32[]{:S(2)}, u32[]{:S(2)}) %collective-permute-start.17) | collective-permute-done | bytes 8224 | tf_op jit(solution)/shard_map/ppermute | solution.py:450
  81.6 0.3 back3.1
  82.0 0.2 collective-permute-start.15
  82.2 2.4 %collective-permute-start.16 = (f32[256,256]{1,0:T(8,128)S(1)}, f32[256,256]{1,0:T(8,128)S(1)}, u32[]{:S(2)}, u32[]{:S(2)}) collective-permute-start(f32[256,256]{1,0:T(8,128)S(1)} %get-tuple-element.68), channel_id=1, source_target_pairs={{1,2},{2,1},{3,4},{4,3},{5,6},{6,5},{7,8},{8,7},{9,10},{10,9},{11,... | collective-permute-start | bytes 786440 | tf_op jit(solution)/shard_map/ppermute | solution.py:464
  84.6 9.3 %adjoint2.1 = (f32[4240,128]{1,0:T(8,128)S(1)}, f32[4240,128]{1,0:T(8,128)S(1)}) custom-call(f32[4240,128]{1,0:T(8,128)S(1)} %get-tuple-element.55.c_ref, f32[4240,128]{1,0:T(8,128)S(1)} %get-tuple-element.70.a_ref, f32[4240,128]{1,0:T(8,128)S(1)} %get-tuple-element.50.ve_ref, ...), custom_call_target="tpu_custom_call", output_to_operand_aliasing={{1}: (5, {})} | custom-call | flops 4294967296 | bytes 1048576 | tf_op jit(solution)/shard_map/adjoint2/pallas_call | solution.py:514
  93.8 3.1 %collective-permute-start.20 = (f32[16,128]{1,0:T(8,128)S(1)}, f32[16,128]{1,0:T(8,128)S(1)}, u32[]{:S(2)}, u32[]{:S(2)}) collective-permute-start(f32[16,128]{1,0:T(8,128)S(1)} %add.73), channel_id=1, source_target_pairs={{0,4},{1,5},{2,6},{3,7},{4,0},{5,1},{6,2},{7,3},{8,12},{9,13},{10,... | collective-permute-start | bytes 24584 | tf_op jit(solution)/shard_map/ppermute | solution.py:450
  96.9 1.6 %collective-permute-done.20 = f32[16,128]{1,0:T(8,128)S(1)} collective-permute-done((f32[16,128]{1,0:T(8,128)S(1)}, f32[16,128]{1,0:T(8,128)S(1)}, u32[]{:S(2)}, u32[]{:S(2)}) %collective-permute-start.20) | collective-permute-done | bytes 8224 | tf_op jit(solution)/shard_map/ppermute | solution.py:450
  98.6 0.3 back2.1
  98.9 9.3 %adjoint1.1 = (f32[4240,128]{1,0:T(8,128)S(1)}, f32[4240,128]{1,0:T(8,128)S(1)}) custom-call(f32[4240,128]{1,0:T(8,128)S(1)} %get-tuple-element.49.c_ref, f32[4240,128]{1,0:T(8,128)S(1)} %get-tuple-element.78.a_ref, f32[4240,128]{1,0:T(8,128)S(1)} %get-tuple-element.50.ve_ref, ...), custom_call_target="tpu_custom_call", output_to_operand_aliasing={{1}: (5, {})} | custom-call | flops 4294967296 | bytes 1048576 | tf_op jit(solution)/shard_map/adjoint1/pallas_call | solution.py:514
  108.2 3.3 %collective-permute-start.21 = (f32[16,128]{1,0:T(8,128)S(1)}, f32[16,128]{1,0:T(8,128)S(1)}, u32[]{:S(2)}, u32[]{:S(2)}) collective-permute-start(f32[16,128]{1,0:T(8,128)S(1)} %add.74), channel_id=1, source_target_pairs={{0,8},{1,9},{2,10},{3,11},{4,12},{5,13},{6,14},{7,15},{8,0},{9,1},... | collective-permute-start | bytes 24584 | tf_op jit(solution)/shard_map/ppermute | solution.py:450
  112.2 2.3 %collective-permute-start.19 = (f32[256,256]{1,0:T(8,128)S(1)}, f32[256,256]{1,0:T(8,128)S(1)}, u32[]{:S(2)}, u32[]{:S(2)}) collective-permute-start(f32[256,256]{1,0:T(8,128)S(1)} %get-tuple-element.76), channel_id=1, source_target_pairs={{1,2},{2,1},{3,4},{4,3},{5,6},{6,5},{7,8},{8,7},{9,10},{10,9},{11,... | collective-permute-start | bytes 786440 | tf_op jit(solution)/shard_map/ppermute | solution.py:464
  114.6 6.6 %collective-permute-done.19.near_ref = f32[256,256]{1,0:T(8,128)S(1)} collective-permute-done((f32[256,256]{1,0:T(8,128)S(1)}, f32[256,256]{1,0:T(8,128)S(1)}, u32[]{:S(2)}, u32[]{:S(2)}) %collective-permute-start.19) | collective-permute-done | bytes 262176 | tf_op jit(solution)/shard_map/ppermute | solution.py:464
  121.2 3.0 %restrict.1 = (f32[2,4096]{1,0:T(2,128)S(1)}, f32[4240,128]{1,0:T(8,128)S(1)}) custom-call(f32[256,256]{1,0:T(8,128)S(1)} %collective-permute-done.18.chip_ref, f32[256,256]{1,0:T(8,128)S(1)} %collective-permute-done.19.near_ref, f32[4240,128]{1,0:T(8,128)S(1)} %get-tuple-element.82.ahead_ref, ...), custom_call_target="tpu_custom_call", output_to_operand_aliasing={{1}: (2, {})} | custom-call | flops 268435456 | bytes 1048576 | tf_op jit(solution)/shard_map/restrict/pallas_call | solution.py:527
  124.2 0.7 collective-permute-start.22
  125.0 1.7 %collective-permute-start.23 = (f32[2,4096]{1,0:T(2,128)S(1)}, f32[2,4096]{1,0:T(2,128)S(1)}, u32[]{:S(2)}, u32[]{:S(2)}) collective-permute-start(f32[2,4096]{1,0:T(2,128)S(1)} %broadcast_multiply_fusion), channel_id=1, source_target_pairs={{0,32},{16,48},{32,0},{48,16},{64,96},{80,112},{96,64},{112,80},{1... | collective-permute-start | bytes 98312 | tf_op jit(solution)/shard_map/ppermute | solution.py:455
  126.7 1.1 collective-permute-start.24
  127.7 1.0 collective-permute-start.26
  128.7 1.8 %collective-permute-start.27 = (f32[1,128]{1,0:T(1,128)S(1)}, f32[1,128]{1,0:T(1,128)S(1)}, u32[]{:S(2)}, u32[]{:S(2)}) collective-permute-start(f32[1,128]{1,0:T(1,128)S(1)} %get-tuple-element.86), channel_id=1, source_target_pairs={{0,32},{16,48},{32,0},{48,16},{64,96},{80,112},{96,64},{112,80},{1... | collective-permute-start | bytes 1544 | tf_op jit(solution)/shard_map/ppermute | solution.py:455
  130.5 2.6 %collective-permute-start.28 = (f32[1,128]{1,0:T(1,128)S(1)}, f32[1,128]{1,0:T(1,128)S(1)}, u32[]{:S(2)}, u32[]{:S(2)}) collective-permute-start(f32[1,128]{1,0:T(1,128)S(1)} %get-tuple-element.86), channel_id=1, source_target_pairs={{0,48},{16,0},{32,16},{48,32},{64,112},{80,64},{96,80},{112,96},{1... | collective-permute-start | bytes 1544 | tf_op jit(solution)/shard_map/ppermute | solution.py:455
  133.2 1.2 collective-permute-start.25
  134.4 2.5 %collective-permute-start.29 = (f32[1,128]{1,0:T(1,128)S(1)}, f32[1,128]{1,0:T(1,128)S(1)}, u32[]{:S(2)}, u32[]{:S(2)}) collective-permute-start(f32[1,128]{1,0:T(1,128)S(1)} %add_add_fusion.2), channel_id=1, source_target_pairs={{0,64},{16,80},{32,96},{48,112},{64,0},{80,16},{96,32},{112,48},{1... | collective-permute-start | bytes 1544 | tf_op jit(solution)/shard_map/ppermute | solution.py:457
  136.9 2.7 %collective-permute-done.29 = f32[1,128]{1,0:T(1,128)S(1)} collective-permute-done((f32[1,128]{1,0:T(1,128)S(1)}, f32[1,128]{1,0:T(1,128)S(1)}, u32[]{:S(2)}, u32[]{:S(2)}) %collective-permute-start.29) | collective-permute-done | bytes 544 | tf_op jit(solution)/shard_map/ppermute | solution.py:457
  139.6 0.7 bitcast_subtract_fusion
  (41 shorter events, 0.6 us)
Async XLA Ops:
  1.4 9.6 %collective-permute-start.2 = (f32[2,4096]{1,0:T(2,128)S(1)}, f32[2,4096]{1,0:T(2,128)S(1)}, u32[]{:S(2)}, u32[]{:S(2)}) collective-permute-start(f32[2,4096]{1,0:T(2,128)S(1)} %bitcast.14), channel_id=1, source_target_pairs={{0,16},{16,32},{32,48},{48,0},{64,80},{80,96},{96,112},{112,64},{1... | collective-permute-start | bytes 98312 | tf_op jit(solution)/shard_map/ppermute | solution.py:455
  3.1 8.0 %collective-permute-start.3 = (f32[2,4096]{1,0:T(2,128)S(1)}, f32[2,4096]{1,0:T(2,128)S(1)}, u32[]{:S(2)}, u32[]{:S(2)}) collective-permute-start(f32[2,4096]{1,0:T(2,128)S(1)} %bitcast.15), channel_id=1, source_target_pairs={{0,32},{16,48},{32,0},{48,16},{64,96},{80,112},{96,64},{112,80},{1... | collective-permute-start | bytes 98312 | tf_op jit(solution)/shard_map/ppermute | solution.py:455
  6.0 5.1 %collective-permute-start.4 = (f32[2,4096]{1,0:T(2,128)S(1)}, f32[2,4096]{1,0:T(2,128)S(1)}, u32[]{:S(2)}, u32[]{:S(2)}) collective-permute-start(f32[2,4096]{1,0:T(2,128)S(1)} %bitcast.16), channel_id=1, source_target_pairs={{0,48},{16,0},{32,16},{48,32},{64,112},{80,64},{96,80},{112,96},{1... | collective-permute-start | bytes 98312 | tf_op jit(solution)/shard_map/ppermute | solution.py:455
  8.4 13.5 %collective-permute-start = (f32[256,256]{1,0:T(8,128)S(1)}, f32[256,256]{1,0:T(8,128)S(1)}, u32[]{:S(2)}, u32[]{:S(2)}) collective-permute-start(f32[256,256]{1,0:T(8,128)S(1)} %get-tuple-element.91), channel_id=1, source_target_pairs={{0,1},{1,0},{2,3},{3,2},{4,5},{5,4},{6,7},{7,6},{8,9},{9,8},{10,11... | collective-permute-start | bytes 786440 | tf_op jit(solution)/shard_map/ppermute | solution.py:465
  8.5 13.5 %collective-permute-start.1 = (f32[256,256]{1,0:T(8,128)S(1)}, f32[256,256]{1,0:T(8,128)S(1)}, u32[]{:S(2)}, u32[]{:S(2)}) collective-permute-start(f32[256,256]{1,0:T(8,128)S(1)} %get-tuple-element.90), channel_id=1, source_target_pairs={{1,2},{2,1},{3,4},{4,3},{5,6},{6,5},{7,8},{8,7},{9,10},{10,9},{11,... | collective-permute-start | bytes 786440 | tf_op jit(solution)/shard_map/ppermute | solution.py:464
  11.1 10.8 %collective-permute-start.5 = (f32[2,4096]{1,0:T(2,128)S(1)}, f32[2,4096]{1,0:T(2,128)S(1)}, u32[]{:S(2)}, u32[]{:S(2)}) collective-permute-start(f32[2,4096]{1,0:T(2,128)S(1)} %add_add_fusion.1), channel_id=1, source_target_pairs={{0,64},{16,80},{32,96},{48,112},{64,0},{80,16},{96,32},{112,48},{1... | collective-permute-start | bytes 98312 | tf_op jit(solution)/shard_map/ppermute | solution.py:457
  27.4 9.6 %collective-permute-start.6 = (f32[256,256]{1,0:T(8,128)S(1)}, f32[256,256]{1,0:T(8,128)S(1)}, u32[]{:S(2)}, u32[]{:S(2)}) collective-permute-start(f32[256,256]{1,0:T(8,128)S(1)} %get-tuple-element.47), channel_id=1, source_target_pairs={{0,1},{1,0},{2,3},{3,2},{4,5},{5,4},{6,7},{7,6},{8,9},{9,8},{10,11... | collective-permute-start | bytes 786440 | tf_op jit(solution)/shard_map/ppermute | solution.py:465
  28.6 8.4 %collective-permute-start.7 = (f32[256,256]{1,0:T(8,128)S(1)}, f32[256,256]{1,0:T(8,128)S(1)}, u32[]{:S(2)}, u32[]{:S(2)}) collective-permute-start(f32[256,256]{1,0:T(8,128)S(1)} %get-tuple-element.48), channel_id=1, source_target_pairs={{1,2},{2,1},{3,4},{4,3},{5,6},{6,5},{7,8},{8,7},{9,10},{10,9},{11,... | collective-permute-start | bytes 786440 | tf_op jit(solution)/shard_map/ppermute | solution.py:464
  37.3 11.1 %collective-permute-start.8 = (f32[256,256]{1,0:T(8,128)S(1)}, f32[256,256]{1,0:T(8,128)S(1)}, u32[]{:S(2)}, u32[]{:S(2)}) collective-permute-start(f32[256,256]{1,0:T(8,128)S(1)} %get-tuple-element.53), channel_id=1, source_target_pairs={{0,1},{1,0},{2,3},{3,2},{4,5},{5,4},{6,7},{7,6},{8,9},{9,8},{10,11... | collective-permute-start | bytes 786440 | tf_op jit(solution)/shard_map/ppermute | solution.py:465
  40.1 8.3 %collective-permute-start.9 = (f32[256,256]{1,0:T(8,128)S(1)}, f32[256,256]{1,0:T(8,128)S(1)}, u32[]{:S(2)}, u32[]{:S(2)}) collective-permute-start(f32[256,256]{1,0:T(8,128)S(1)} %get-tuple-element.54), channel_id=1, source_target_pairs={{1,2},{2,1},{3,4},{4,3},{5,6},{6,5},{7,8},{8,7},{9,10},{10,9},{11,... | collective-permute-start | bytes 786440 | tf_op jit(solution)/shard_map/ppermute | solution.py:464
  48.8 11.0 %collective-permute-start.10 = (f32[256,256]{1,0:T(8,128)S(1)}, f32[256,256]{1,0:T(8,128)S(1)}, u32[]{:S(2)}, u32[]{:S(2)}) collective-permute-start(f32[256,256]{1,0:T(8,128)S(1)} %get-tuple-element.56), channel_id=1, source_target_pairs={{0,1},{1,0},{2,3},{3,2},{4,5},{5,4},{6,7},{7,6},{8,9},{9,8},{10,11... | collective-permute-start | bytes 786440 | tf_op jit(solution)/shard_map/ppermute | solution.py:465
  51.5 8.3 %collective-permute-start.11 = (f32[256,256]{1,0:T(8,128)S(1)}, f32[256,256]{1,0:T(8,128)S(1)}, u32[]{:S(2)}, u32[]{:S(2)}) collective-permute-start(f32[256,256]{1,0:T(8,128)S(1)} %get-tuple-element.57), channel_id=1, source_target_pairs={{1,2},{2,1},{3,4},{4,3},{5,6},{6,5},{7,8},{8,7},{9,10},{10,9},{11,... | collective-permute-start | bytes 786440 | tf_op jit(solution)/shard_map/ppermute | solution.py:464
  63.5 14.4 %collective-permute-start.14 = (f32[16,128]{1,0:T(8,128)S(1)}, f32[16,128]{1,0:T(8,128)S(1)}, u32[]{:S(2)}, u32[]{:S(2)}) collective-permute-start(f32[16,128]{1,0:T(8,128)S(1)} %get-tuple-element.62), channel_id=1, source_target_pairs={{0,1},{1,0},{2,3},{3,2},{4,5},{5,4},{6,7},{7,6},{8,9},{9,8},{10,11... | collective-permute-start | bytes 24584 | tf_op jit(solution)/shard_map/ppermute | solution.py:450
  66.5 15.1 %collective-permute-start.12 = (f32[256,256]{1,0:T(8,128)S(1)}, f32[256,256]{1,0:T(8,128)S(1)}, u32[]{:S(2)}, u32[]{:S(2)}) collective-permute-start(f32[256,256]{1,0:T(8,128)S(1)} %get-tuple-element.60), channel_id=1, source_target_pairs={{0,1},{1,0},{2,3},{3,2},{4,5},{5,4},{6,7},{7,6},{8,9},{9,8},{10,11... | collective-permute-start | bytes 786440 | tf_op jit(solution)/shard_map/ppermute | solution.py:465
  66.6 15.0 %collective-permute-start.13 = (f32[256,256]{1,0:T(8,128)S(1)}, f32[256,256]{1,0:T(8,128)S(1)}, u32[]{:S(2)}, u32[]{:S(2)}) collective-permute-start(f32[256,256]{1,0:T(8,128)S(1)} %get-tuple-element.61), channel_id=1, source_target_pairs={{1,2},{2,1},{3,4},{4,3},{5,6},{6,5},{7,8},{8,7},{9,10},{10,9},{11,... | collective-permute-start | bytes 786440 | tf_op jit(solution)/shard_map/ppermute | solution.py:464
  77.9 3.7 %collective-permute-start.17 = (f32[16,128]{1,0:T(8,128)S(1)}, f32[16,128]{1,0:T(8,128)S(1)}, u32[]{:S(2)}, u32[]{:S(2)}) collective-permute-start(f32[16,128]{1,0:T(8,128)S(1)} %add.72), channel_id=1, source_target_pairs={{0,2},{1,3},{2,0},{3,1},{4,6},{5,7},{6,4},{7,5},{8,10},{9,11},{10,... | collective-permute-start | bytes 24584 | tf_op jit(solution)/shard_map/ppermute | solution.py:450
  82.0 16.6 %collective-permute-start.15 = (f32[256,256]{1,0:T(8,128)S(1)}, f32[256,256]{1,0:T(8,128)S(1)}, u32[]{:S(2)}, u32[]{:S(2)}) collective-permute-start(f32[256,256]{1,0:T(8,128)S(1)} %get-tuple-element.67), channel_id=1, source_target_pairs={{0,1},{1,0},{2,3},{3,2},{4,5},{5,4},{6,7},{7,6},{8,9},{9,8},{10,11... | collective-permute-start | bytes 786440 | tf_op jit(solution)/shard_map/ppermute | solution.py:465
  82.2 16.4 %collective-permute-start.16 = (f32[256,256]{1,0:T(8,128)S(1)}, f32[256,256]{1,0:T(8,128)S(1)}, u32[]{:S(2)}, u32[]{:S(2)}) collective-permute-start(f32[256,256]{1,0:T(8,128)S(1)} %get-tuple-element.68), channel_id=1, source_target_pairs={{1,2},{2,1},{3,4},{4,3},{5,6},{6,5},{7,8},{8,7},{9,10},{10,9},{11,... | collective-permute-start | bytes 786440 | tf_op jit(solution)/shard_map/ppermute | solution.py:464
  93.8 4.7 %collective-permute-start.20 = (f32[16,128]{1,0:T(8,128)S(1)}, f32[16,128]{1,0:T(8,128)S(1)}, u32[]{:S(2)}, u32[]{:S(2)}) collective-permute-start(f32[16,128]{1,0:T(8,128)S(1)} %add.73), channel_id=1, source_target_pairs={{0,4},{1,5},{2,6},{3,7},{4,0},{5,1},{6,2},{7,3},{8,12},{9,13},{10,... | collective-permute-start | bytes 24584 | tf_op jit(solution)/shard_map/ppermute | solution.py:450
  108.2 6.4 %collective-permute-start.21 = (f32[16,128]{1,0:T(8,128)S(1)}, f32[16,128]{1,0:T(8,128)S(1)}, u32[]{:S(2)}, u32[]{:S(2)}) collective-permute-start(f32[16,128]{1,0:T(8,128)S(1)} %add.74), channel_id=1, source_target_pairs={{0,8},{1,9},{2,10},{3,11},{4,12},{5,13},{6,14},{7,15},{8,0},{9,1},... | collective-permute-start | bytes 24584 | tf_op jit(solution)/shard_map/ppermute | solution.py:450
  112.1 2.5 %collective-permute-start.18 = (f32[256,256]{1,0:T(8,128)S(1)}, f32[256,256]{1,0:T(8,128)S(1)}, u32[]{:S(2)}, u32[]{:S(2)}) collective-permute-start(f32[256,256]{1,0:T(8,128)S(1)} %get-tuple-element.75), channel_id=1, source_target_pairs={{0,1},{1,0},{2,3},{3,2},{4,5},{5,4},{6,7},{7,6},{8,9},{9,8},{10,11... | collective-permute-start | bytes 786440 | tf_op jit(solution)/shard_map/ppermute | solution.py:465
  112.2 9.0 %collective-permute-start.19 = (f32[256,256]{1,0:T(8,128)S(1)}, f32[256,256]{1,0:T(8,128)S(1)}, u32[]{:S(2)}, u32[]{:S(2)}) collective-permute-start(f32[256,256]{1,0:T(8,128)S(1)} %get-tuple-element.76), channel_id=1, source_target_pairs={{1,2},{2,1},{3,4},{4,3},{5,6},{6,5},{7,8},{8,7},{9,10},{10,9},{11,... | collective-permute-start | bytes 786440 | tf_op jit(solution)/shard_map/ppermute | solution.py:464
  124.2 6.3 %collective-permute-start.22 = (f32[2,4096]{1,0:T(2,128)S(1)}, f32[2,4096]{1,0:T(2,128)S(1)}, u32[]{:S(2)}, u32[]{:S(2)}) collective-permute-start(f32[2,4096]{1,0:T(2,128)S(1)} %broadcast_multiply_fusion), channel_id=1, source_target_pairs={{0,16},{16,32},{32,48},{48,0},{64,80},{80,96},{96,112},{112,64},{1... | collective-permute-start | bytes 98312 | tf_op jit(solution)/shard_map/ppermute | solution.py:455
  125.0 8.1 %collective-permute-start.23 = (f32[2,4096]{1,0:T(2,128)S(1)}, f32[2,4096]{1,0:T(2,128)S(1)}, u32[]{:S(2)}, u32[]{:S(2)}) collective-permute-start(f32[2,4096]{1,0:T(2,128)S(1)} %broadcast_multiply_fusion), channel_id=1, source_target_pairs={{0,32},{16,48},{32,0},{48,16},{64,96},{80,112},{96,64},{112,80},{1... | collective-permute-start | bytes 98312 | tf_op jit(solution)/shard_map/ppermute | solution.py:455
  126.7 6.4 %collective-permute-start.24 = (f32[2,4096]{1,0:T(2,128)S(1)}, f32[2,4096]{1,0:T(2,128)S(1)}, u32[]{:S(2)}, u32[]{:S(2)}) collective-permute-start(f32[2,4096]{1,0:T(2,128)S(1)} %broadcast_multiply_fusion), channel_id=1, source_target_pairs={{0,48},{16,0},{32,16},{48,32},{64,112},{80,64},{96,80},{112,96},{1... | collective-permute-start | bytes 98312 | tf_op jit(solution)/shard_map/ppermute | solution.py:455
  127.7 6.6 %collective-permute-start.26 = (f32[1,128]{1,0:T(1,128)S(1)}, f32[1,128]{1,0:T(1,128)S(1)}, u32[]{:S(2)}, u32[]{:S(2)}) collective-permute-start(f32[1,128]{1,0:T(1,128)S(1)} %get-tuple-element.86), channel_id=1, source_target_pairs={{0,16},{16,32},{32,48},{48,0},{64,80},{80,96},{96,112},{112,64},{1... | collective-permute-start | bytes 1544 | tf_op jit(solution)/shard_map/ppermute | solution.py:455
  128.7 5.7 %collective-permute-start.27 = (f32[1,128]{1,0:T(1,128)S(1)}, f32[1,128]{1,0:T(1,128)S(1)}, u32[]{:S(2)}, u32[]{:S(2)}) collective-permute-start(f32[1,128]{1,0:T(1,128)S(1)} %get-tuple-element.86), channel_id=1, source_target_pairs={{0,32},{16,48},{32,0},{48,16},{64,96},{80,112},{96,64},{112,80},{1... | collective-permute-start | bytes 1544 | tf_op jit(solution)/shard_map/ppermute | solution.py:455
  130.5 3.9 %collective-permute-start.28 = (f32[1,128]{1,0:T(1,128)S(1)}, f32[1,128]{1,0:T(1,128)S(1)}, u32[]{:S(2)}, u32[]{:S(2)}) collective-permute-start(f32[1,128]{1,0:T(1,128)S(1)} %get-tuple-element.86), channel_id=1, source_target_pairs={{0,48},{16,0},{32,16},{48,32},{64,112},{80,64},{96,80},{112,96},{1... | collective-permute-start | bytes 1544 | tf_op jit(solution)/shard_map/ppermute | solution.py:455
  133.2 6.4 %collective-permute-start.25 = (f32[2,4096]{1,0:T(2,128)S(1)}, f32[2,4096]{1,0:T(2,128)S(1)}, u32[]{:S(2)}, u32[]{:S(2)}) collective-permute-start(f32[2,4096]{1,0:T(2,128)S(1)} %add_add_fusion), channel_id=1, source_target_pairs={{0,64},{16,80},{32,96},{48,112},{64,0},{80,16},{96,32},{112,48},{1... | collective-permute-start | bytes 98312 | tf_op jit(solution)/shard_map/ppermute | solution.py:457
  134.4 5.1 %collective-permute-start.29 = (f32[1,128]{1,0:T(1,128)S(1)}, f32[1,128]{1,0:T(1,128)S(1)}, u32[]{:S(2)}, u32[]{:S(2)}) collective-permute-start(f32[1,128]{1,0:T(1,128)S(1)} %add_add_fusion.2), channel_id=1, source_target_pairs={{0,64},{16,80},{32,96},{48,112},{64,0},{80,16},{96,32},{112,48},{1... | collective-permute-start | bytes 1544 | tf_op jit(solution)/shard_map/ppermute | solution.py:457

commit v2 on v1

v2 whole, which is shorter than its diff:
```python
import functools

import jax
import jax.numpy as jnp
from jax import lax
from jax.experimental import pallas as pl
from jax.experimental.pallas import tpu as pltpu
from jax.sharding import PartitionSpec as P


STEPS = 4
EPS_LIMIT = 0.01
TIME_STEP = 0.25
DIFF_FLAT = 0.1
DIFF_VERTICAL = 0.25
BETA_LEVEL = 0.75
SOFT_WIDTH = 0.25

NZ, NX, NY = 8, 256, 256
HP = NX + 8
ZP = 2 * HP
F0 = 8
ROWS = F0 + NZ * ZP + 8
SEG = HP // 8
VERT = TIME_STEP * DIFF_VERTICAL
KEEP = 1.0 - 2.0 * VERT
f32 = jnp.float32
VM = pl.BlockSpec(memory_space=pltpu.VMEM)
HBM = pl.BlockSpec(memory_space=pltpu.HBM)
FIELD = jax.ShapeDtypeStruct((ROWS, 128), f32)
PLANE = jax.ShapeDtypeStruct((NX, NY), f32)


def seg_load(ref, z, h, r):
    return ref[pl.ds(F0 + z * ZP + h * HP + r, 8, stride=SEG), :]


def seg_store(ref, z, h, r, value):
    ref[pl.ds(F0 + z * ZP + h * HP + r, 8, stride=SEG), :] = value


def block_rows(z, h, j):
    return pl.ds(pl.multiple_of(F0 + z * ZP + h * HP + 8 * j, 8), 8)


def zero_plane_pads(ref, z):
    for h in range(2):
        ref[pl.ds(pl.multiple_of(F0 + z * ZP + h * HP + NX, 8), 8), :] = jnp.zeros((8, 128), f32)


def zero_pads(ref):
    zeros = jnp.zeros((8, 128), f32)
    ref[0:8, :] = zeros
    ref[ROWS - 8 : ROWS, :] = zeros
    for z in range(NZ):
        for h in range(2):
            start = F0 + z * ZP + h * HP + NX
            ref[start : start + 8, :] = zeros


def limiter(b, f, sb, sf):
    p = b * f
    q = p * p + EPS_LIMIT * EPS_LIMIT
    s = q * lax.rsqrt(q)
    r = lax.rsqrt(sb + sf + EPS_LIMIT)
    return ((p + s) * (r * r)) * ((b + f) + f)


def limiter_slopes(b, f, sb, sf):
    p = b * f
    q = p * p + EPS_LIMIT * EPS_LIMIT
    rs = lax.rsqrt(q)
    s = q * rs
    r = lax.rsqrt(sb + sf + EPS_LIMIT)
    r = r * r
    w = (p + s) * r
    u = (b + f) + f
    r2 = r + r
    slope_b = (f * rs - b * r2) * u + 1.0
    slope_f = (b * rs - f * r2) * u + 2.0
    return w, u, slope_b, slope_f


def lane_masks():
    lane = lax.broadcasted_iota(jnp.int32, (8, 128), 1)
    return lane == 0, lane == 127


def from_left(pair, first, edge):
    rolled = [pltpu.roll(v, 1, 1) for v in pair]
    return [jnp.where(edge, first, rolled[0]), jnp.where(edge, rolled[0], rolled[1])]


def from_right(pair, last, edge):
    rolled = [pltpu.roll(v, 127, 1) for v in pair]
    return [jnp.where(edge, rolled[1], rolled[0]), jnp.where(edge, last, rolled[1])]


def vertical_sum(ref, z, h, r):
    if isinstance(z, int) and z == 0:
        return seg_load(ref, 1, h, r)
    if isinstance(z, int) and z == NZ - 1:
        return seg_load(ref, NZ - 2, h, r)
    return seg_load(ref, z - 1, h, r) + seg_load(ref, z + 1, h, r)


def forward_plane(z, unroll, c_ref, ve_ref, vn_ref, co_ref, out_ref, slope_refs):
    at_first, at_last = lane_masks()

    def flux(v, c6, b, f, sb, sf, refs, h, r):
        if refs is None:
            corrected = v * (c6 + limiter(b, f, sb, sf))
        else:
            w, u, slope_b, slope_f = limiter_slopes(b, f, sb, sf)
            vw = v * w
            seg_store(refs[0], z, h, r, vw * slope_b)
            seg_store(refs[1], z, h, r, vw * slope_f - 6.0 * DIFF_FLAT)
            corrected = v * c6 + vw * u
        return corrected - (6.0 * DIFF_FLAT) * f

    def one(r, c, b, sb, before):
        after = [seg_load(c_ref, z, h, r + 1) for h in (0, 1)]
        left = from_left(c, 0.0, at_first)
        right = from_right(c, 0.0, at_last)
        f, sf, gx, gy = [], [], [], []
        for h in (0, 1):
            c6 = 6.0 * c[h]
            fx = after[h] - c[h]
            sx = fx * fx
            gx.append(flux(seg_load(ve_ref, z, h, r), c6, b[h], fx, sb[h], sx, slope_refs and slope_refs[:2], h, r))
            by = c[h] - left[h]
            fy = right[h] - c[h]
            gy.append(flux(seg_load(vn_ref, z, h, r), c6, by, fy, by * by, fy * fy, slope_refs and slope_refs[2:], h, r))
            f.append(fx)
            sf.append(sx)
        gl = from_left(gy, (-6.0 * DIFF_FLAT) * c[0], at_first)
        for h in (0, 1):
            vertical = VERT * vertical_sum(c_ref, z, h, r)
            keep = KEEP if co_ref is None else seg_load(co_ref, z, h, r)
            flow = (gx[h] - before[h]) + (gy[h] - gl[h])
            seg_store(out_ref, z, h, r, keep * c[h] + vertical - (TIME_STEP / 6.0) * flow)
        return after, f, sf, gx

    c, b, sb, before = [], [], [], []
    for h in (0, 1):
        m2 = seg_load(c_ref, z, h, -2)
        m1 = seg_load(c_ref, z, h, -1)
        c0 = seg_load(c_ref, z, h, 0)
        bm = m1 - m2
        fm = c0 - m1
        sm = fm * fm
        before.append(flux(seg_load(ve_ref, z, h, -1), 6.0 * m1, bm, fm, bm * bm, sm, None, h, -1))
        c.append(c0)
        b.append(fm)
        sb.append(sm)

    def block(i, carry):
        for j in range(unroll):
            carry = one(i * unroll + j, *carry)
        return carry

    lax.fori_loop(0, SEG // unroll, block, (c, b, sb, before))
    zero_plane_pads(out_ref, z)


def over_planes(plane):
    plane(0)

    def inner(z, unused):
        plane(z)
        return unused

    lax.fori_loop(1, NZ - 1, inner, 0)
    plane(NZ - 1)


def first_kernel(start_ref, east_ref, north_ref, c_ref, ve_ref, vn_ref, out_ref, sem):
    def copies(z):
        made = []
        for source, target in ((start_ref, c_ref), (east_ref, ve_ref), (north_ref, vn_ref)):
            for h in (0, 1):
                made.append(
                    pltpu.make_async_copy(
                        source.at[0, z, :, pl.ds(h * 128, 128)],
                        target.at[pl.ds(pl.multiple_of(F0 + z * ZP + h * HP, 8), NX), :],
                        sem.at[z, len(made)],
                    )
                )
        return made

    ahead = 3
    for z in range(ahead):
        for copy in copies(z):
            copy.start()
    for ref in (c_ref, ve_ref, vn_ref, out_ref):
        zero_pads(ref)
    for copy in copies(0):
        copy.wait()

    def plane(z):
        if isinstance(z, int) and z == NZ - 1:
            pass
        else:
            for copy in copies(z + 1):
                copy.wait()

            @pl.when(z + ahead < NZ)
            def _():
                for copy in copies(z + ahead):
                    copy.start()

        forward_plane(z, 11, c_ref, ve_ref, vn_ref, None, out_ref, None)

    over_planes(plane)


def step_kernel(c_ref, ve_ref, vn_ref, co_ref, out_ref, *slope_refs):
    zero_pads(out_ref)
    for i, ref in enumerate(slope_refs):
        ref[0:F0, :] = jnp.full((F0, 128), -6.0 * DIFF_FLAT if i % 2 else 0.0, f32)
    over_planes(lambda z: forward_plane(z, 11, c_ref, ve_ref, vn_ref, co_ref, out_ref, slope_refs))


def facing():
    z_chip = jnp.where(lax.axis_index("slab") % 2 == 0, NZ - 1, 0)
    return z_chip, NZ - 1 - z_chip


def fix_planes(chip_ref, near_ref, field_ref, target_ref, send_chip_ref=None, send_near_ref=None, prior_ref=None):
    z_chip, z_near = facing()
    slab = lax.axis_index("slab")
    near_share = jnp.where((slab > 0) & (slab < lax.axis_size("slab") - 1), VERT, 0.0)

    def block(j, unused):
        for h in (0, 1):
            lanes = slice(h * 128, h * 128 + 128)
            rows = pl.ds(pl.multiple_of(8 * j, 8), 8)
            for z, halo_ref, send_ref, share in (
                (z_chip, chip_ref, send_chip_ref, VERT),
                (z_near, near_ref, send_near_ref, near_share),
            ):
                at = block_rows(z, h, j)
                halo = halo_ref[rows, lanes]
                if prior_ref is not None:
                    halo = halo + share * prior_ref[at, :]
                value = field_ref[at, :] + VERT * halo
                target_ref[at, :] = value
                if send_ref is not None:
                    send_ref[rows, lanes] = value
        return unused

    lax.fori_loop(0, NX // 8, block, 0, unroll=4)


def fix_kernel(chip_ref, near_ref, field_ref, out_ref, send_chip_ref, send_near_ref):
    fix_planes(chip_ref, near_ref, field_ref, out_ref, send_chip_ref, send_near_ref)


def send_planes(field_ref, send_chip_ref, send_near_ref):
    z_chip, z_near = facing()

    def block(j, unused):
        for h in (0, 1):
            lanes = slice(h * 128, h * 128 + 128)
            rows = pl.ds(pl.multiple_of(8 * j, 8), 8)
            send_chip_ref[rows, lanes] = field_ref[block_rows(z_chip, h, j), :]
            send_near_ref[rows, lanes] = field_ref[block_rows(z_near, h, j), :]
        return unused

    lax.fori_loop(0, NX // 8, block, 0, unroll=4)


def rate_kernel(chip_ref, near_ref, field_ref, c0_ref, cons_ref, wells_ref, out_ref, send_chip_ref, send_near_ref, co_ref, wide_ref):
    lane = lax.broadcasted_iota(jnp.int32, (8, 128), 1)
    sub = lax.broadcasted_iota(jnp.int32, (8, 128), 0)
    base = jnp.where(sub < 4, 0, 64) + lane // 4
    zero_pads(co_ref)

    def prolong(j, unused):
        for p in (0, 1):
            coarse = cons_ref[pl.ds(p, 1), pl.ds(pl.multiple_of(j * 128, 128), 128)]
            coarse = jnp.broadcast_to(coarse * TIME_STEP, (8, 128))
            for h in (0, 1):
                wide_ref[p, pl.ds(pl.multiple_of(8 * j, 8), 8), h * 128 : h * 128 + 128] = jnp.take_along_axis(
                    coarse, base + 32 * h, axis=1
                )
        return unused

    lax.fori_loop(0, NX // 8, prolong, 0, unroll=8)

    def block(j, unused):
        rows = pl.ds(pl.multiple_of(8 * j, 8), 8)
        for h in (0, 1):
            lanes = slice(h * 128, h * 128 + 128)
            for p in (0, 1):
                wide = wide_ref[p, rows, lanes]
                for z in range(4 * p, 4 * p + 4):
                    rate = wells_ref[z, rows, lanes].astype(f32) * wide
                    at = block_rows(z, h, j)
                    co_ref[at, :] = KEEP - rate
                    out_ref[at, :] = field_ref[at, :] - rate * c0_ref[at, :]
        return unused

    lax.fori_loop(0, NX // 8, block, 0, unroll=2)
    fix_planes(chip_ref, near_ref, out_ref, out_ref, send_chip_ref, send_near_ref)


def seed_kernel(chip_ref, near_ref, ahead_ref, monitors_ref, final_ref, adjoint_ref, send_chip_ref, send_near_ref, field_ref):
    zero_pads(adjoint_ref)
    fix_planes(chip_ref, near_ref, ahead_ref, field_ref)

    def block(j, sums):
        mass, count = sums
        rows = pl.ds(pl.multiple_of(8 * j, 8), 8)
        for z in range(NZ):
            for h in (0, 1):
                lanes = slice(h * 128, h * 128 + 128)
                value = field_ref[block_rows(z, h, j), :]
                final_ref[0, z, rows, lanes] = value
                monitor = monitors_ref[z, rows, lanes].astype(f32)
                seed = monitor * value
                adjoint_ref[block_rows(z, h, j), :] = seed
                mass[z % 4] = mass[z % 4] + seed * value
                count[z % 4] = count[z % 4] + monitor
        return mass, count

    zeros = [jnp.zeros((8, 128), f32)] * 4
    mass, count = lax.fori_loop(0, NX // 8, block, (list(zeros), list(zeros)))
    for part, start in ((mass, 0), (count, 128)):
        part = (part[0] + part[1]) + (part[2] + part[3])
        part = jnp.sum(jnp.sum(part, axis=0, keepdims=True), axis=1, keepdims=True)
        send_chip_ref[NX : NX + 8, start : start + 128] = jnp.broadcast_to(part, (8, 128))
    send_planes(adjoint_ref, send_chip_ref, send_near_ref)


def adjoint_plane(z, unroll, fields, rg_in_ref, out_ref, rg_ref):
    a_ref, c_ref, ve_ref, vn_ref, co_ref, xb_ref, xf_ref, yb_ref, yf_ref = fields
    at_first, at_last = lane_masks()

    def one(r, a, next_a, vg, behind, front):
        far_a = [seg_load(a_ref, z, h, r + 2) for h in (0, 1)]
        right = from_right(a, 0.0, at_last)
        vy, back_y, front_y = [], [], []
        for h in (0, 1):
            g = right[h] - a[h]
            vy.append(seg_load(vn_ref, z, h, r) * g)
            back_y.append(seg_load(yb_ref, z, h, r) * g)
            front_y.append(seg_load(yf_ref, z, h, r) * g)
        fl = from_left(front_y, (-6.0 * DIFF_FLAT) * a[0], at_first)
        kr = from_right(back_y, 0.0, at_last)
        new_vg, new_behind, new_front = [], [], []
        for h in (0, 1):
            g = far_a[h] - next_a[h]
            ahead = seg_load(xb_ref, z, h, r + 1) * g + front[h]
            new_vg.append(seg_load(ve_ref, z, h, r + 1) * g)
            new_front.append(seg_load(xf_ref, z, h, r + 1) * g)
            new_behind.append(ahead)
            here = ((back_y[h] - front_y[h]) + (fl[h] - kr[h])) + (behind[h] - ahead) + 6.0 * (vg[h] + vy[h])
            vertical = VERT * vertical_sum(a_ref, z, h, r)
            out = seg_load(co_ref, z, h, r) * a[h] + vertical + (TIME_STEP / 6.0) * here
            seg_store(out_ref, z, h, r, out)
            grad = seg_load(c_ref, z, h, r) * a[h]
            if rg_in_ref is not None:
                grad = grad + seg_load(rg_in_ref, z, h, r)
            seg_store(rg_ref, z, h, r, grad)
        return next_a, far_a, new_vg, new_behind, new_front

    a, next_a, vg, behind, front = [], [], [], [], []
    for h in (0, 1):
        am = seg_load(a_ref, z, h, -1)
        a0 = seg_load(a_ref, z, h, 0)
        a1 = seg_load(a_ref, z, h, 1)
        gm = a0 - am
        g0 = a1 - a0
        a.append(a0)
        next_a.append(a1)
        vg.append(seg_load(ve_ref, z, h, 0) * g0)
        behind.append(seg_load(xb_ref, z, h, 0) * g0 + seg_load(xf_ref, z, h, -1) * gm)
        front.append(seg_load(xf_ref, z, h, 0) * g0)

    def block(i, carry):
        for j in range(unroll):
            carry = one(i * unroll + j, *carry)
        return carry

    lax.fori_loop(0, SEG // unroll, block, (a, next_a, vg, behind, front))
    zero_plane_pads(out_ref, z)


def edge_planes(fields, rg_in_ref, out_ref, rg_ref, send_chip_ref, send_near_ref):
    zero_pads(out_ref)
    for z in (0, NZ - 1):
        adjoint_plane(z, 11, fields, rg_in_ref, out_ref, rg_ref)
    send_planes(out_ref, send_chip_ref, send_near_ref)


def edge_kernel(*refs):
    edge_planes(refs[:9], None, *refs[9:])


def turn_kernel(chip_ref, near_ref, ahead_ref, *refs):
    rest, rg_in_ref, (a_ref, out_ref, rg_ref, send_chip_ref, send_near_ref) = refs[:8], refs[8], refs[9:]
    fix_planes(chip_ref, near_ref, ahead_ref, a_ref)
    edge_planes((a_ref,) + rest, rg_in_ref, out_ref, rg_ref, send_chip_ref, send_near_ref)


def inner_kernel(has_grad, *refs):
    fields, (out_in_ref, rg_in_ref, out_ref, rg_ref) = refs[:9], refs[9:]

    def inner(z, unused):
        adjoint_plane(z, 11, fields, rg_in_ref if has_grad else None, out_ref, rg_ref)
        return unused

    lax.fori_loop(1, NZ - 1, inner, 0)


def last_kernel(chip_ref, near_ref, prior_ref, ahead_ref, *refs):
    rest, rg_in_ref, (a_ref, out_ref, rg_ref) = refs[:8], refs[8], refs[9:]
    fix_planes(chip_ref, near_ref, ahead_ref, a_ref, prior_ref=prior_ref)
    zero_pads(out_ref)
    over_planes(lambda z: adjoint_plane(z, 11, (a_ref,) + rest, rg_in_ref, out_ref, rg_ref))


def restrict_kernel(share, cells, limit_ref, chip_ref, near_ref, prior_ref, ahead_ref, c0_ref, rg_ref, wells_ref, sums_ref, out_ref, field_ref, wide_ref):
    fix_planes(chip_ref, near_ref, ahead_ref, field_ref, prior_ref=prior_ref)
    count = jnp.maximum(sums_ref[0:8, 128:256], 1.0)
    scaled = (sums_ref[0:8, 0:128] / count - limit_ref[0]) / SOFT_WIDTH
    small = jnp.exp(-jnp.abs(scaled))
    weight = jnp.where(scaled >= 0.0, 1.0, small) / (1.0 + small) * share
    soft = SOFT_WIDTH * (jnp.maximum(scaled, 0.0) + jnp.log1p(small)) * share
    out_ref[0:2, NX * 16 : NX * 16 + 128] = soft[0:2, :]
    scale = weight * 2.0 / count * (-TIME_STEP * cells)

    def block(j, unused):
        rows = pl.ds(pl.multiple_of(8 * j, 8), 8)
        for h in (0, 1):
            lanes = slice(h * 128, h * 128 + 128)
            for p in (0, 1):
                parts = []
                for z in range(4 * p, 4 * p + 4):
                    at = block_rows(z, h, j)
                    parts.append(wells_ref[z, rows, lanes].astype(f32) * (rg_ref[at, :] + c0_ref[at, :] * field_ref[at, :]))
                wide_ref[p, rows, lanes] = ((parts[0] + parts[1]) + (parts[2] + parts[3])) * scale
        return unused

    lax.fori_loop(0, NX // 8, block, 0, unroll=2)
    fine = lax.broadcasted_iota(jnp.int32, (NY, 128), 0) // 4
    coarse = lax.broadcasted_iota(jnp.int32, (NY, 128), 1) % 64
    sums = jnp.where(fine == coarse, 1.0, 0.0).astype(f32)
    row = lax.broadcasted_iota(jnp.int32, (NX, 128), 0) % 8
    lane = lax.broadcasted_iota(jnp.int32, (NX, 128), 1)
    own = (row < 4) == (lane < 64)
    for p in (0, 1):
        part = jnp.dot(wide_ref[p], sums, precision=lax.Precision.HIGHEST, preferred_element_type=f32)
        part = jnp.where(own, part, 0.0).reshape(NX // 8, 8, 128).sum(axis=1)
        for j in range(NX // 8):
            out_ref[p : p + 1, j * 128 : (j + 1) * 128] = part[j : j + 1, :]


def call(kernel, flops, **kwargs):
    return pl.pallas_call(
        kernel,
        compiler_params=pltpu.CompilerParams(vmem_limit_bytes=8 << 20),
        cost_estimate=pl.CostEstimate(flops=flops, bytes_accessed=1 << 20, transcendentals=0),
        **kwargs,
    )


def dma(*shape):
    return pltpu.SemaphoreType.DMA(shape)


def pair_sum(value, axis, size, step):
    return value + lax.ppermute(value, axis, [(i, i ^ step) for i in range(size)])


def scen_sum(value):
    others = [lax.ppermute(value, "scen", [(i, (i & 4) | ((i + k) & 3)) for i in range(8)]) for k in (1, 2, 3)]
    value = (value + others[0]) + (others[1] + others[2])
    return pair_sum(value, "scen", 8, 4)


def swap(slab_count, send_chip, send_near):
    near = []
    for i in range(1, slab_count - 1, 2):
        near += [(i, i + 1), (i + 1, i)]
    got_near = lax.ppermute(send_near, "slab", near)
    got_chip = lax.ppermute(send_chip, "slab", [(i, i ^ 1) for i in range(slab_count)])
    return got_chip, got_near


def on_device(start, flow_east, flow_north, wells, monitors, control, multiplier, threshold):
    scen_count = lax.axis_size("scen")
    slab_count = lax.axis_size("slab")
    odd = lax.axis_index("slab") % 2
    in_hbm = functools.partial(pltpu.with_memory_space_constraint, memory_space=pltpu.HBM)

    low, high = start[0, 0], start[0, NZ - 1]
    halos = swap(slab_count, jnp.where(odd == 0, high, low), jnp.where(odd == 0, low, high))
    consensus = scen_sum((control + multiplier)[0]) / scen_count

    c0, ve, vn, ahead = call(
        first_kernel, 3 << 30,
        in_specs=[HBM] * 3, out_specs=[VM] * 4, out_shape=[FIELD] * 4, scratch_shapes=[dma(NZ, 6)],
    )(in_hbm(start), in_hbm(flow_east), in_hbm(flow_north))
    c, send_chip, send_near, co = call(
        rate_kernel, 1 << 28,
        in_specs=[VM] * 6, out_specs=[VM] * 4, out_shape=[FIELD, PLANE, PLANE, FIELD],
        scratch_shapes=[pltpu.VMEM((2, NX, NY), f32)],
        input_output_aliases={2: 0},
    )(*halos, ahead, c0, consensus, wells)
    states = [c0, c]
    slopes = [()]
    for k in range(1, STEPS):
        halos = swap(slab_count, send_chip, send_near)
        ahead, *made = call(step_kernel, 3 << 30, in_specs=[VM] * 4, out_specs=[VM] * 5, out_shape=[FIELD] * 5)(c, ve, vn, co)
        slopes.append(tuple(made))
        if k < STEPS - 1:
            c, send_chip, send_near = call(
                fix_kernel, 1 << 26,
                in_specs=[VM] * 3, out_specs=[VM] * 3, out_shape=[FIELD, PLANE, PLANE],
                input_output_aliases={2: 0},
            )(*halos, ahead)
            states.append(c)
    final, seed, send_chip, send_near, _ = call(
        seed_kernel, 1 << 28,
        in_specs=[VM] * 4, out_specs=[VM] * 5,
        out_shape=[
            jax.ShapeDtypeStruct((1, NZ, NX, NY), f32), FIELD, jax.ShapeDtypeStruct((NX + 8, NY), f32), PLANE, FIELD,
        ],
        input_output_aliases={2: 4},
    )(*halos, ahead, monitors)

    def rest(k):
        return (states[k], ve, vn, co) + slopes[k]

    def inner(k, adjoint, ahead, grad):
        return call(
            functools.partial(inner_kernel, k < STEPS - 1), 2 << 30,
            in_specs=[VM] * 11, out_specs=[VM] * 2, out_shape=[FIELD] * 2, input_output_aliases={9: 0, 10: 1},
        )(adjoint, *rest(k), ahead, grad)

    halos4 = swap(slab_count, send_chip, send_near)
    ahead, grad, send_chip5, send_near5 = call(
        edge_kernel, 1 << 30,
        in_specs=[VM] * 9, out_specs=[VM] * 4, out_shape=[FIELD, FIELD, PLANE, PLANE],
    )(seed, *rest(3))
    halos5 = swap(slab_count, send_chip5, send_near5)
    sums = send_chip[NX:] + halos4[0][NX:]
    sums = pair_sum(sums, "slab", slab_count, 2)
    ahead, grad = inner(3, seed, ahead, grad)
    adjoint3, ahead, grad, send_chip, send_near = call(
        turn_kernel, 1 << 30,
        in_specs=[VM] * 12, out_specs=[VM] * 5, out_shape=[FIELD, FIELD, FIELD, PLANE, PLANE],
        input_output_aliases={2: 0, 11: 2},
    )(*halos4, ahead, *rest(2), grad)
    halos6 = swap(slab_count, send_chip, send_near)
    sums = pair_sum(sums, "slab", slab_count, 4)
    ahead, grad = inner(2, adjoint3, ahead, grad)
    sums = pair_sum(sums, "slab", slab_count, 8)
    _, ahead, grad = call(
        last_kernel, 3 << 30,
        in_specs=[VM] * 13, out_specs=[VM] * 3, out_shape=[FIELD] * 3, input_output_aliases={3: 0, 12: 2},
    )(*halos5, seed, ahead, *rest(1), grad)
    share = 1.0 / ((1.0 - BETA_LEVEL) * scen_count)
    coarse_cells = NZ * slab_count * NX * NY / 64.0
    coarse, _ = call(
        functools.partial(restrict_kernel, share, coarse_cells), 1 << 28,
        in_specs=[pl.BlockSpec(memory_space=pltpu.SMEM)] + [VM] * 8, out_specs=[VM] * 2,
        out_shape=[jax.ShapeDtypeStruct((2, 4096 + 128), f32), FIELD],
        scratch_shapes=[pltpu.VMEM((2, NX, NY), f32)],
        input_output_aliases={4: 1},
    )(threshold, *halos6, adjoint3, ahead, c0, grad, wells, sums)
    total = scen_sum(coarse)
    consensus_next = consensus - total[:, :4096]
    multiplier_next = multiplier + control - consensus_next[None]
    return (final, consensus_next, multiplier_next, threshold + total[0, 4096:4097])


def solution(mesh):
    placed = (
        P("scen", "slab", None, None),
        P("scen", "slab", None, None),
        P("scen", "slab", None, None),
        P("slab", None, None),
        P("slab", None, None),
        P("scen", "slab", None),
        P("scen", "slab", None),
        P(),
    )
    return jax.shard_map(
        on_device,
        mesh=mesh,
        in_specs=placed,
        out_specs=(P("scen", "slab", None, None), P("slab", None), P("scen", "slab", None), P()),
        check_vma=False,
    )
```

time: 144 us -> 112 us (0.78); the launches traced: 141 us -> 111 us
  Pallas kernels: 68.7 us -> 54.5 us
  starting transfers between devices: 52.6 us -> 41.8 us
  waiting for transfers between devices: 14.6 us -> 7.94 us
    pallas_call x14, Pallas kernels: 68.7 us -> 54.5 us  [the longest x3 23.6 us: on_device(): call(step_kernel, 3 << 30, in_specs=[VM] * 4, out_specs=[VM] * 5, out_sha...]
    ppermute x7 -> x5, starting transfers between devices: 15.7 us -> 6.61 us  [pair_sum(): lax.ppermute(value, axis, [(i, i ^ step) for i in range(size)])]
    ppermute x7, waiting for transfers between devices: 6.59 us -> 0.02 us  [swap(): got_near = lax.ppermute(send_near, 'slab', near)]
    ppermute x9 -> x6, starting transfers between devices: 14.8 us -> 9.41 us  [scen_sum(): lax.ppermute(value, 'scen', [(i, i & 4 | i + k & 3) for i in range(8)])]
    ppermute x7 -> x5, waiting for transfers between devices: 7.93 us -> 4.98 us  [pair_sum(): lax.ppermute(value, axis, [(i, i ^ step) for i in range(size)])]
    ppermute x7, starting transfers between devices: 7.15 us -> 10.1 us  [swap(): lax.ppermute(send_chip, 'slab', [(i, i ^ 1) for i in range(slab_count)])]
    ppermute x9 -> x6, waiting for transfers between devices: 0.04 us -> 2.92 us  [scen_sum(): lax.ppermute(value, 'scen', [(i, i & 4 | i + k & 3) for i in range(8)])]
  transfers between devices with their start and end apart: 30 -> 25, of which waited for: 4 -> 4; matrix products, arithmetic and copies ran while one was open for 1% -> 1% of each run, Pallas kernels for 33% -> 43%
where the time goes in v2:
time: 112 us; the launch traced here: 111 us
  Pallas kernels  54.5 us (49%)
  starting transfers between devices  41.8 us (37%)
  waiting for transfers between devices  7.94 us (7%)
  between operations  3.51 us (3%)
  other arithmetic  2.64 us (2%)
    pallas_call x3, Pallas kernels, on_device(): call(step_kernel, 3 << 30, in_specs=[VM] * 4, out_specs=[VM] * 5, out_sha...  23.6 us
    ppermute x7, starting transfers between devices, swap(): got_near = lax.ppermute(send_near, 'slab', near)  15.7 us
    ppermute x7, starting transfers between devices, swap(): lax.ppermute(send_chip, 'slab', [(i, i ^ 1) for i in range(slab_count)])  10.1 us
    ppermute x6, starting transfers between devices, scen_sum(): lax.ppermute(value, 'scen', [(i, i & 4 | i + k & 3) for i in range(8)])  9.41 us
    pallas_call x1, Pallas kernels, on_device(): call(first_kernel, 3 << 30, in_specs=[HBM] * 3, out_specs=[VM] * 4, out_s...  7.89 us
    pallas_call x2, Pallas kernels, inner(): call(functools.partial(inner_kernel, k < STEPS - 1), 2 << 30, in_specs=[V...  7.67 us
    ppermute x5, starting transfers between devices, pair_sum(): lax.ppermute(value, axis, [(i, i ^ step) for i in range(size)])  6.61 us
    pallas_call x1, Pallas kernels, on_device(): call(last_kernel, 3 << 30, in_specs=[VM] * 13, out_specs=[VM] * 3, out_sh...  5.45 us
  transfers between devices with their start and end apart: 25, of which 4 were waited for; matrix products, arithmetic and copies ran while one was open for 1% of the time, Pallas kernels for 43%

profile of v2, /device:TPU:2, one launch (start us, length us, event | category | flops | bytes accessed | tf_op | source)
XLA Modules:
  0.0 110.9 jit_solution(3383628078570352739)
XLA Ops:
  0.6 0.8 add.48
  1.4 1.6 %collective-permute-start.2 = (f32[2,4096]{1,0:T(2,128)S(1)}, f32[2,4096]{1,0:T(2,128)S(1)}, u32[]{:S(2)}, u32[]{:S(2)}) collective-permute-start(f32[2,4096]{1,0:T(2,128)S(1)} %bitcast.9), channel_id=1, source_target_pairs={{0,16},{16,32},{32,48},{48,0},{64,80},{80,96},{96,112},{112,64},{1... | collective-permute-start | bytes 98312 | tf_op jit(solution)/shard_map/ppermute | solution.py:478
  3.1 2.9 %collective-permute-start.3 = (f32[2,4096]{1,0:T(2,128)S(1)}, f32[2,4096]{1,0:T(2,128)S(1)}, u32[]{:S(2)}, u32[]{:S(2)}) collective-permute-start(f32[2,4096]{1,0:T(2,128)S(1)} %bitcast.10), channel_id=1, source_target_pairs={{0,32},{16,48},{32,0},{48,16},{64,96},{80,112},{96,64},{112,80},{1... | collective-permute-start | bytes 98312 | tf_op jit(solution)/shard_map/ppermute | solution.py:478
  6.0 1.3 %collective-permute-start.4 = (f32[2,4096]{1,0:T(2,128)S(1)}, f32[2,4096]{1,0:T(2,128)S(1)}, u32[]{:S(2)}, u32[]{:S(2)}) collective-permute-start(f32[2,4096]{1,0:T(2,128)S(1)} %bitcast.11), channel_id=1, source_target_pairs={{0,48},{16,0},{32,16},{48,32},{64,112},{80,64},{96,80},{112,96},{1... | collective-permute-start | bytes 98312 | tf_op jit(solution)/shard_map/ppermute | solution.py:478
  7.3 1.1 select_bitcast_fusion
  8.4 0.1 collective-permute-start
  8.5 2.5 %collective-permute-start.1 = (f32[256,256]{1,0:T(8,128)S(1)}, f32[256,256]{1,0:T(8,128)S(1)}, u32[]{:S(2)}, u32[]{:S(2)}) collective-permute-start(f32[256,256]{1,0:T(8,128)S(1)} %get-tuple-element.104), channel_id=1, source_target_pairs={{1,2},{2,1},{3,4},{4,3},{5,6},{6,5},{7,8},{8,7},{9,10},{10,9},{11,... | collective-permute-start | bytes 786440 | tf_op jit(solution)/shard_map/ppermute | solution.py:487
  11.1 0.0 copy-start
  11.1 2.5 %collective-permute-start.5 = (f32[2,4096]{1,0:T(2,128)S(1)}, f32[2,4096]{1,0:T(2,128)S(1)}, u32[]{:S(2)}, u32[]{:S(2)}) collective-permute-start(f32[2,4096]{1,0:T(2,128)S(1)} %add_add_fusion.1), channel_id=1, source_target_pairs={{0,64},{16,80},{32,96},{48,112},{64,0},{80,16},{96,32},{112,48},{1... | collective-permute-start | bytes 98312 | tf_op jit(solution)/shard_map/ppermute | solution.py:474
  13.6 7.9 %shard_map.111 = (f32[4240,128]{1,0:T(8,128)S(1)}, f32[4240,128]{1,0:T(8,128)S(1)}, f32[4240,128]{1,0:T(8,128)S(1)}, f32[4240,128]{1,0:T(8,128)S(1)}) custom-call(f32[1,8,256,256]{3,2,1,0:T(8,128)} %start_ref.1, f32[1,8,256,256]{3,2,1,0:T(8,128)} %east_ref.1, f32[1,8,256,256]{3,2,1,0:T(8,128)} %north_ref.1), custom_call_target="tpu_custom_call" | custom-call | flops 3221225472 | bytes 1048576 | tf_op jit(solution)/shard_map/pallas_call | solution.py:502
  22.2 2.3 %shard_map.112 = (f32[4240,128]{1,0:T(8,128)S(1)}, f32[256,256]{1,0:T(8,128)S(1)}, f32[256,256]{1,0:T(8,128)S(1)}, f32[4240,128]{1,0:T(8,128)S(1)}) custom-call(f32[256,256]{1,0:T(8,128)S(1)} %collective-permute-done.chip_ref, f32[256,256]{1,0:T(8,128)S(1)} %collective-permute-done.1.near_ref, ...), custom_call_target="tpu_custom_call", output_to_operand_aliasing={{0}: (2, {})} | custom-call | flops 268435456 | bytes 1048576 | tf_op jit(solution)/shard_map/pallas_call | solution.py:506
  24.5 1.2 %collective-permute-start.6 = (f32[256,256]{1,0:T(8,128)S(1)}, f32[256,256]{1,0:T(8,128)S(1)}, u32[]{:S(2)}, u32[]{:S(2)}) collective-permute-start(f32[256,256]{1,0:T(8,128)S(1)} %get-tuple-element.55), channel_id=1, source_target_pairs={{0,1},{1,0},{2,3},{3,2},{4,5},{5,4},{6,7},{7,6},{8,9},{9,8},{10,11... | collective-permute-start | bytes 786440 | tf_op jit(solution)/shard_map/ppermute | solution.py:488
  25.7 2.0 %collective-permute-start.7 = (f32[256,256]{1,0:T(8,128)S(1)}, f32[256,256]{1,0:T(8,128)S(1)}, u32[]{:S(2)}, u32[]{:S(2)}) collective-permute-start(f32[256,256]{1,0:T(8,128)S(1)} %get-tuple-element.56), channel_id=1, source_target_pairs={{1,2},{2,1},{3,4},{4,3},{5,6},{6,5},{7,8},{8,7},{9,10},{10,9},{11,... | collective-permute-start | bytes 786440 | tf_op jit(solution)/shard_map/ppermute | solution.py:487
  27.7 7.9 %shard_map.113 = (f32[4240,128]{1,0:T(8,128)S(1)}, f32[4240,128]{1,0:T(8,128)S(1)}, f32[4240,128]{1,0:T(8,128)S(1)}, f32[4240,128]{1,0:T(8,128)S(1)}, f32[4240,128]{1,0:T(8,128)S(1)}) custom-call(f32[4240,128]{1,0:T(8,128)S(1)} %get-tuple-element.57.c_ref.refs_0_, f32[4240,128]{1,0:T(8,128)S(1)} %get-tuple-element.58.ve_ref.refs_2_.refs_1_, ...), custom_call_target="tpu_custom_call" | custom-call | flops 3221225472 | bytes 1048576 | tf_op jit(solution)/shard_map/pallas_call | solution.py:516
  35.6 0.3 shard_map.114
  35.9 1.9 %collective-permute-start.8 = (f32[256,256]{1,0:T(8,128)S(1)}, f32[256,256]{1,0:T(8,128)S(1)}, u32[]{:S(2)}, u32[]{:S(2)}) collective-permute-start(f32[256,256]{1,0:T(8,128)S(1)} %get-tuple-element.62), channel_id=1, source_target_pairs={{0,1},{1,0},{2,3},{3,2},{4,5},{5,4},{6,7},{7,6},{8,9},{9,8},{10,11... | collective-permute-start | bytes 786440 | tf_op jit(solution)/shard_map/ppermute | solution.py:488
  37.9 1.9 %collective-permute-start.9 = (f32[256,256]{1,0:T(8,128)S(1)}, f32[256,256]{1,0:T(8,128)S(1)}, u32[]{:S(2)}, u32[]{:S(2)}) collective-permute-start(f32[256,256]{1,0:T(8,128)S(1)} %get-tuple-element.63), channel_id=1, source_target_pairs={{1,2},{2,1},{3,4},{4,3},{5,6},{6,5},{7,8},{8,7},{9,10},{10,9},{11,... | collective-permute-start | bytes 786440 | tf_op jit(solution)/shard_map/ppermute | solution.py:487
  39.8 7.9 %shard_map.115 = (f32[4240,128]{1,0:T(8,128)S(1)}, f32[4240,128]{1,0:T(8,128)S(1)}, f32[4240,128]{1,0:T(8,128)S(1)}, f32[4240,128]{1,0:T(8,128)S(1)}, f32[4240,128]{1,0:T(8,128)S(1)}) custom-call(f32[4240,128]{1,0:T(8,128)S(1)} %get-tuple-element.64.c_ref.refs_0_.refs_1_, f32[4240,128]{1,0:T(8,128)S(1)} %get-tuple-element.58.ve_ref.refs_2_.refs_1_, ...), custom_call_target="tpu_custom_call" | custom-call | flops 3221225472 | bytes 1048576 | tf_op jit(solution)/shard_map/pallas_call | solution.py:516
  47.7 0.3 shard_map.116
  48.1 1.8 %collective-permute-start.10 = (f32[256,256]{1,0:T(8,128)S(1)}, f32[256,256]{1,0:T(8,128)S(1)}, u32[]{:S(2)}, u32[]{:S(2)}) collective-permute-start(f32[256,256]{1,0:T(8,128)S(1)} %get-tuple-element.66), channel_id=1, source_target_pairs={{0,1},{1,0},{2,3},{3,2},{4,5},{5,4},{6,7},{7,6},{8,9},{9,8},{10,11... | collective-permute-start | bytes 786440 | tf_op jit(solution)/shard_map/ppermute | solution.py:488
  49.8 2.0 %collective-permute-start.11 = (f32[256,256]{1,0:T(8,128)S(1)}, f32[256,256]{1,0:T(8,128)S(1)}, u32[]{:S(2)}, u32[]{:S(2)}) collective-permute-start(f32[256,256]{1,0:T(8,128)S(1)} %get-tuple-element.67), channel_id=1, source_target_pairs={{1,2},{2,1},{3,4},{4,3},{5,6},{6,5},{7,8},{8,7},{9,10},{10,9},{11,... | collective-permute-start | bytes 786440 | tf_op jit(solution)/shard_map/ppermute | solution.py:487
  51.8 7.9 %shard_map.117 = (f32[4240,128]{1,0:T(8,128)S(1)}, f32[4240,128]{1,0:T(8,128)S(1)}, f32[4240,128]{1,0:T(8,128)S(1)}, f32[4240,128]{1,0:T(8,128)S(1)}, f32[4240,128]{1,0:T(8,128)S(1)}) custom-call(f32[4240,128]{1,0:T(8,128)S(1)} %get-tuple-element.68.c_ref.refs_1_, f32[4240,128]{1,0:T(8,128)S(1)} %get-tuple-element.58.ve_ref.refs_2_.refs_1_, ...), custom_call_target="tpu_custom_call" | custom-call | flops 3221225472 | bytes 1048576 | tf_op jit(solution)/shard_map/pallas_call | solution.py:516
  59.7 2.4 %shard_map.118 = (f32[1,8,256,256]{3,2,1,0:T(8,128)}, f32[4240,128]{1,0:T(8,128)S(1)}, f32[264,256]{1,0:T(8,128)S(1)}, f32[256,256]{1,0:T(8,128)S(1)}, f32[4240,128]{1,0:T(8,128)S(1)}) custom-call(f32[256,256]{1,0:T(8,128)S(1)} %collective-permute-done.10.chip_ref, f32[256,256]{1,0:T(8,128)S(1)} %collective-permute-done.11.near_ref, ...), custom_call_target="tpu_custom_call", output_to_operand_aliasing={{4}: (2, {})} | custom-call | flops 268435456 | bytes 1048576 | tf_op jit(solution)/shard_map/pallas_call | solution.py:525
  62.1 1.8 %collective-permute-start.12 = (f32[264,256]{1,0:T(8,128)S(1)}, f32[264,256]{1,0:T(8,128)S(1)}, u32[]{:S(2)}, u32[]{:S(2)}) collective-permute-start(f32[264,256]{1,0:T(8,128)S(1)} %get-tuple-element.71), channel_id=1, source_target_pairs={{0,1},{1,0},{2,3},{3,2},{4,5},{5,4},{6,7},{7,6},{8,9},{9,8},{10,11... | collective-permute-start | bytes 811016 | tf_op jit(solution)/shard_map/ppermute | solution.py:488
  63.9 1.9 %collective-permute-start.13 = (f32[256,256]{1,0:T(8,128)S(1)}, f32[256,256]{1,0:T(8,128)S(1)}, u32[]{:S(2)}, u32[]{:S(2)}) collective-permute-start(f32[256,256]{1,0:T(8,128)S(1)} %get-tuple-element.72), channel_id=1, source_target_pairs={{1,2},{2,1},{3,4},{4,3},{5,6},{6,5},{7,8},{8,7},{9,10},{10,9},{11,... | collective-permute-start | bytes 786440 | tf_op jit(solution)/shard_map/ppermute | solution.py:487
  65.8 1.3 %shard_map.119 = (f32[4240,128]{1,0:T(8,128)S(1)}, f32[4240,128]{1,0:T(8,128)S(1)}, f32[256,256]{1,0:T(8,128)S(1)}, f32[256,256]{1,0:T(8,128)S(1)}) custom-call(f32[4240,128]{1,0:T(8,128)S(1)} %get-tuple-element.73.refs_0_.prior_ref, f32[4240,128]{1,0:T(8,128)S(1)} %get-tuple-element.68.c_ref.refs_1_, ...), custom_call_target="tpu_custom_call" | custom-call | flops 1073741824 | bytes 1048576 | tf_op jit(solution)/shard_map/pallas_call | solution.py:544
  67.2 1.6 %collective-permute-start.16 = (f32[256,256]{1,0:T(8,128)S(1)}, f32[256,256]{1,0:T(8,128)S(1)}, u32[]{:S(2)}, u32[]{:S(2)}) collective-permute-start(f32[256,256]{1,0:T(8,128)S(1)} %get-tuple-element.89), channel_id=1, source_target_pairs={{0,1},{1,0},{2,3},{3,2},{4,5},{5,4},{6,7},{7,6},{8,9},{9,8},{10,11... | collective-permute-start | bytes 786440 | tf_op jit(solution)/shard_map/ppermute | solution.py:488
  68.7 2.2 %collective-permute-start.17 = (f32[256,256]{1,0:T(8,128)S(1)}, f32[256,256]{1,0:T(8,128)S(1)}, u32[]{:S(2)}, u32[]{:S(2)}) collective-permute-start(f32[256,256]{1,0:T(8,128)S(1)} %get-tuple-element.90), channel_id=1, source_target_pairs={{1,2},{2,1},{3,4},{4,3},{5,6},{6,5},{7,8},{8,7},{9,10},{10,9},{11,... | collective-permute-start | bytes 786440 | tf_op jit(solution)/shard_map/ppermute | solution.py:487
  70.9 3.8 %shard_map.120 = (f32[4240,128]{1,0:T(8,128)S(1)}, f32[4240,128]{1,0:T(8,128)S(1)}) custom-call(f32[4240,128]{1,0:T(8,128)S(1)} %get-tuple-element.73.refs_0_.prior_ref, f32[4240,128]{1,0:T(8,128)S(1)} %get-tuple-element.68.c_ref.refs_1_, f32[4240,128]{1,0:T(8,128)S(1)} %get-tuple-element.58.ve_ref.refs_2_.refs_1_, ...), custom_call_target="tpu_custom_call", output_to_operand_aliasing={{0}: (9, {}), {1}: (10, {})} | custom-call | flops 2147483648 | bytes 1048576 | tf_op jit(solution)/shard_map/pallas_call | solution.py:538
  74.8 0.1 collective-permute-start.18
  74.9 1.7 %shard_map.121 = (f32[4240,128]{1,0:T(8,128)S(1)}, f32[4240,128]{1,0:T(8,128)S(1)}, f32[4240,128]{1,0:T(8,128)S(1)}, f32[256,256]{1,0:T(8,128)S(1)}, f32[256,256]{1,0:T(8,128)S(1)}) custom-call(f32[264,256]{1,0:T(8,128)S(1)} %collective-permute-done.12.chip_ref, ...), custom_call_target="tpu_custom_call", output_to_operand_aliasing={{0}: (2, {}), {2}: (11, {})} | custom-call | flops 1073741824 | bytes 1048576 | tf_op jit(solution)/shard_map/pallas_call | solution.py:552
  76.6 1.7 %collective-permute-start.14 = (f32[256,256]{1,0:T(8,128)S(1)}, f32[256,256]{1,0:T(8,128)S(1)}, u32[]{:S(2)}, u32[]{:S(2)}) collective-permute-start(f32[256,256]{1,0:T(8,128)S(1)} %get-tuple-element.86), channel_id=1, source_target_pairs={{0,1},{1,0},{2,3},{3,2},{4,5},{5,4},{6,7},{7,6},{8,9},{9,8},{10,11... | collective-permute-start | bytes 786440 | tf_op jit(solution)/shard_map/ppermute | solution.py:488
  78.3 3.2 %collective-permute-start.15 = (f32[256,256]{1,0:T(8,128)S(1)}, f32[256,256]{1,0:T(8,128)S(1)}, u32[]{:S(2)}, u32[]{:S(2)}) collective-permute-start(f32[256,256]{1,0:T(8,128)S(1)} %get-tuple-element.87), channel_id=1, source_target_pairs={{1,2},{2,1},{3,4},{4,3},{5,6},{6,5},{7,8},{8,7},{9,10},{10,9},{11,... | collective-permute-start | bytes 786440 | tf_op jit(solution)/shard_map/ppermute | solution.py:487
  81.6 1.1 collective-permute-start.19
  82.7 3.8 %shard_map.122 = (f32[4240,128]{1,0:T(8,128)S(1)}, f32[4240,128]{1,0:T(8,128)S(1)}) custom-call(f32[4240,128]{1,0:T(8,128)S(1)} %get-tuple-element.88.refs_0_.prior_ref, f32[4240,128]{1,0:T(8,128)S(1)} %get-tuple-element.64.c_ref.refs_0_.refs_1_, ...), custom_call_target="tpu_custom_call", output_to_operand_aliasing={{0}: (9, {}), {1}: (10, {})} | custom-call | flops 2147483648 | bytes 1048576 | tf_op jit(solution)/shard_map/pallas_call | solution.py:538
  86.5 2.4 %collective-permute-start.20 = (f32[8,256]{1,0:T(8,128)S(1)}, f32[8,256]{1,0:T(8,128)S(1)}, u32[]{:S(2)}, u32[]{:S(2)}) collective-permute-start(f32[8,256]{1,0:T(8,128)S(1)} %add.55), channel_id=1, source_target_pairs={{0,8},{1,9},{2,10},{3,11},{4,12},{5,13},{6,14},{7,15},{8,0},{9,1},... | collective-permute-start | bytes 24584 | tf_op jit(solution)/shard_map/ppermute | solution.py:474
  89.0 5.4 %shard_map.123 = (f32[4240,128]{1,0:T(8,128)S(1)}, f32[4240,128]{1,0:T(8,128)S(1)}, f32[4240,128]{1,0:T(8,128)S(1)}) custom-call(f32[256,256]{1,0:T(8,128)S(1)} %collective-permute-done.16.chip_ref, f32[256,256]{1,0:T(8,128)S(1)} %collective-permute-done.17.near_ref, ...), custom_call_target="tpu_custom_call", output_to_operand_aliasing={{0}: (3, {}), {2}: (12, {})} | custom-call | flops 3221225472 | bytes 1048576 | tf_op jit(solution)/shard_map/pallas_call | solution.py:561
  94.5 1.5 %shard_map.124 = (f32[2,4224]{1,0:T(2,128)S(1)}, f32[4240,128]{1,0:T(8,128)S(1)}) custom-call(f32[1]{0:T(128)S(6)} %copy.38.limit_ref, f32[256,256]{1,0:T(8,128)S(1)} %collective-permute-done.14.chip_ref, f32[256,256]{1,0:T(8,128)S(1)} %collective-permute-done.15.near_ref, ...), custom_call_target="tpu_custom_call", output_to_operand_aliasing={{1}: (4, {})} | custom-call | flops 268435456 | bytes 1048576 | tf_op jit(solution)/shard_map/pallas_call | solution.py:567
  96.0 0.7 collective-permute-start.21
  96.7 1.7 %collective-permute-start.22 = (f32[2,4224]{1,0:T(2,128)S(1)}, f32[2,4224]{1,0:T(2,128)S(1)}, u32[]{:S(2)}, u32[]{:S(2)}) collective-permute-start(f32[2,4224]{1,0:T(2,128)S(1)} %get-tuple-element.101), channel_id=1, source_target_pairs={{0,32},{16,48},{32,0},{48,16},{64,96},{80,112},{96,64},{112,80},{1... | collective-permute-start | bytes 101384 | tf_op jit(solution)/shard_map/ppermute | solution.py:478
  98.4 1.1 collective-permute-start.23
  99.5 1.7 %collective-permute-done.21 = f32[2,4224]{1,0:T(2,128)S(1)} collective-permute-done((f32[2,4224]{1,0:T(2,128)S(1)}, f32[2,4224]{1,0:T(2,128)S(1)}, u32[]{:S(2)}, u32[]{:S(2)}) %collective-permute-start.21) | collective-permute-done | bytes 33824 | tf_op jit(solution)/shard_map/ppermute | solution.py:478
  101.2 1.0 collective-permute-done.22
  102.2 0.2 collective-permute-done.23
  102.4 0.5 collective-permute-start.24
  103.0 5.0 %collective-permute-done.24 = f32[2,4224]{1,0:T(2,128)S(1)} collective-permute-done((f32[2,4224]{1,0:T(2,128)S(1)}, f32[2,4224]{1,0:T(2,128)S(1)}, u32[]{:S(2)}, u32[]{:S(2)}) %collective-permute-start.24) | collective-permute-done | bytes 33824 | tf_op jit(solution)/shard_map/ppermute | solution.py:474
  108.0 0.7 bitcast_subtract_fusion
  108.6 0.5 slice.26
  (40 shorter events, 0.2 us)
Async XLA Ops:
  1.4 9.6 %collective-permute-start.2 = (f32[2,4096]{1,0:T(2,128)S(1)}, f32[2,4096]{1,0:T(2,128)S(1)}, u32[]{:S(2)}, u32[]{:S(2)}) collective-permute-start(f32[2,4096]{1,0:T(2,128)S(1)} %bitcast.9), channel_id=1, source_target_pairs={{0,16},{16,32},{32,48},{48,0},{64,80},{80,96},{96,112},{112,64},{1... | collective-permute-start | bytes 98312 | tf_op jit(solution)/shard_map/ppermute | solution.py:478
  3.1 8.0 %collective-permute-start.3 = (f32[2,4096]{1,0:T(2,128)S(1)}, f32[2,4096]{1,0:T(2,128)S(1)}, u32[]{:S(2)}, u32[]{:S(2)}) collective-permute-start(f32[2,4096]{1,0:T(2,128)S(1)} %bitcast.10), channel_id=1, source_target_pairs={{0,32},{16,48},{32,0},{48,16},{64,96},{80,112},{96,64},{112,80},{1... | collective-permute-start | bytes 98312 | tf_op jit(solution)/shard_map/ppermute | solution.py:478
  6.0 5.1 %collective-permute-start.4 = (f32[2,4096]{1,0:T(2,128)S(1)}, f32[2,4096]{1,0:T(2,128)S(1)}, u32[]{:S(2)}, u32[]{:S(2)}) collective-permute-start(f32[2,4096]{1,0:T(2,128)S(1)} %bitcast.11), channel_id=1, source_target_pairs={{0,48},{16,0},{32,16},{48,32},{64,112},{80,64},{96,80},{112,96},{1... | collective-permute-start | bytes 98312 | tf_op jit(solution)/shard_map/ppermute | solution.py:478
  8.4 13.8 %collective-permute-start = (f32[256,256]{1,0:T(8,128)S(1)}, f32[256,256]{1,0:T(8,128)S(1)}, u32[]{:S(2)}, u32[]{:S(2)}) collective-permute-start(f32[256,256]{1,0:T(8,128)S(1)} %get-tuple-element.105), channel_id=1, source_target_pairs={{0,1},{1,0},{2,3},{3,2},{4,5},{5,4},{6,7},{7,6},{8,9},{9,8},{10,11... | collective-permute-start | bytes 786440 | tf_op jit(solution)/shard_map/ppermute | solution.py:488
  8.5 13.7 %collective-permute-start.1 = (f32[256,256]{1,0:T(8,128)S(1)}, f32[256,256]{1,0:T(8,128)S(1)}, u32[]{:S(2)}, u32[]{:S(2)}) collective-permute-start(f32[256,256]{1,0:T(8,128)S(1)} %get-tuple-element.104), channel_id=1, source_target_pairs={{1,2},{2,1},{3,4},{4,3},{5,6},{6,5},{7,8},{8,7},{9,10},{10,9},{11,... | collective-permute-start | bytes 786440 | tf_op jit(solution)/shard_map/ppermute | solution.py:487
  11.1 11.1 %copy-start = (s32[8,256,256]{2,1,0:T(8,128)S(1)}, s32[8,256,256]{2,1,0:T(8,128)}, u32[]{:S(2)}) copy-start(s32[8,256,256]{2,1,0:T(8,128)} %wells_ref.3) | copy-start | bytes 6291460
  11.1 11.0 %collective-permute-start.5 = (f32[2,4096]{1,0:T(2,128)S(1)}, f32[2,4096]{1,0:T(2,128)S(1)}, u32[]{:S(2)}, u32[]{:S(2)}) collective-permute-start(f32[2,4096]{1,0:T(2,128)S(1)} %add_add_fusion.1), channel_id=1, source_target_pairs={{0,64},{16,80},{32,96},{48,112},{64,0},{80,16},{96,32},{112,48},{1... | collective-permute-start | bytes 98312 | tf_op jit(solution)/shard_map/ppermute | solution.py:474
  24.5 11.1 %collective-permute-start.6 = (f32[256,256]{1,0:T(8,128)S(1)}, f32[256,256]{1,0:T(8,128)S(1)}, u32[]{:S(2)}, u32[]{:S(2)}) collective-permute-start(f32[256,256]{1,0:T(8,128)S(1)} %get-tuple-element.55), channel_id=1, source_target_pairs={{0,1},{1,0},{2,3},{3,2},{4,5},{5,4},{6,7},{7,6},{8,9},{9,8},{10,11... | collective-permute-start | bytes 786440 | tf_op jit(solution)/shard_map/ppermute | solution.py:488
  25.7 9.9 %collective-permute-start.7 = (f32[256,256]{1,0:T(8,128)S(1)}, f32[256,256]{1,0:T(8,128)S(1)}, u32[]{:S(2)}, u32[]{:S(2)}) collective-permute-start(f32[256,256]{1,0:T(8,128)S(1)} %get-tuple-element.56), channel_id=1, source_target_pairs={{1,2},{2,1},{3,4},{4,3},{5,6},{6,5},{7,8},{8,7},{9,10},{10,9},{11,... | collective-permute-start | bytes 786440 | tf_op jit(solution)/shard_map/ppermute | solution.py:487
  35.6 12.1 %copy-start.1 = (f32[4240,128]{1,0:T(8,128)}, f32[4240,128]{1,0:T(8,128)S(1)}, u32[]{:S(2)}) copy-start(f32[4240,128]{1,0:T(8,128)S(1)} %get-tuple-element.95.refs_5_) | copy-start | bytes 6512644
  35.6 12.1 %copy-start.3 = (f32[4240,128]{1,0:T(8,128)}, f32[4240,128]{1,0:T(8,128)S(1)}, u32[]{:S(2)}) copy-start(f32[4240,128]{1,0:T(8,128)S(1)} %get-tuple-element.96.refs_6_) | copy-start | bytes 6512644
  35.9 11.8 %collective-permute-start.8 = (f32[256,256]{1,0:T(8,128)S(1)}, f32[256,256]{1,0:T(8,128)S(1)}, u32[]{:S(2)}, u32[]{:S(2)}) collective-permute-start(f32[256,256]{1,0:T(8,128)S(1)} %get-tuple-element.62), channel_id=1, source_target_pairs={{0,1},{1,0},{2,3},{3,2},{4,5},{5,4},{6,7},{7,6},{8,9},{9,8},{10,11... | collective-permute-start | bytes 786440 | tf_op jit(solution)/shard_map/ppermute | solution.py:488
  37.9 9.9 %collective-permute-start.9 = (f32[256,256]{1,0:T(8,128)S(1)}, f32[256,256]{1,0:T(8,128)S(1)}, u32[]{:S(2)}, u32[]{:S(2)}) collective-permute-start(f32[256,256]{1,0:T(8,128)S(1)} %get-tuple-element.63), channel_id=1, source_target_pairs={{1,2},{2,1},{3,4},{4,3},{5,6},{6,5},{7,8},{8,7},{9,10},{10,9},{11,... | collective-permute-start | bytes 786440 | tf_op jit(solution)/shard_map/ppermute | solution.py:487
  48.1 11.6 %collective-permute-start.10 = (f32[256,256]{1,0:T(8,128)S(1)}, f32[256,256]{1,0:T(8,128)S(1)}, u32[]{:S(2)}, u32[]{:S(2)}) collective-permute-start(f32[256,256]{1,0:T(8,128)S(1)} %get-tuple-element.66), channel_id=1, source_target_pairs={{0,1},{1,0},{2,3},{3,2},{4,5},{5,4},{6,7},{7,6},{8,9},{9,8},{10,11... | collective-permute-start | bytes 786440 | tf_op jit(solution)/shard_map/ppermute | solution.py:488
  49.8 9.9 %collective-permute-start.11 = (f32[256,256]{1,0:T(8,128)S(1)}, f32[256,256]{1,0:T(8,128)S(1)}, u32[]{:S(2)}, u32[]{:S(2)}) collective-permute-start(f32[256,256]{1,0:T(8,128)S(1)} %get-tuple-element.67), channel_id=1, source_target_pairs={{1,2},{2,1},{3,4},{4,3},{5,6},{6,5},{7,8},{8,7},{9,10},{10,9},{11,... | collective-permute-start | bytes 786440 | tf_op jit(solution)/shard_map/ppermute | solution.py:487
  51.8 7.9 %copy-start.5 = (s32[8,256,256]{2,1,0:T(8,128)S(1)}, s32[8,256,256]{2,1,0:T(8,128)}, u32[]{:S(2)}) copy-start(s32[8,256,256]{2,1,0:T(8,128)} %monitors_ref.1) | copy-start | bytes 6291460
  62.1 12.7 %collective-permute-start.12 = (f32[264,256]{1,0:T(8,128)S(1)}, f32[264,256]{1,0:T(8,128)S(1)}, u32[]{:S(2)}, u32[]{:S(2)}) collective-permute-start(f32[264,256]{1,0:T(8,128)S(1)} %get-tuple-element.71), channel_id=1, source_target_pairs={{0,1},{1,0},{2,3},{3,2},{4,5},{5,4},{6,7},{7,6},{8,9},{9,8},{10,11... | collective-permute-start | bytes 811016 | tf_op jit(solution)/shard_map/ppermute | solution.py:488
  63.9 11.0 %collective-permute-start.13 = (f32[256,256]{1,0:T(8,128)S(1)}, f32[256,256]{1,0:T(8,128)S(1)}, u32[]{:S(2)}, u32[]{:S(2)}) collective-permute-start(f32[256,256]{1,0:T(8,128)S(1)} %get-tuple-element.72), channel_id=1, source_target_pairs={{1,2},{2,1},{3,4},{4,3},{5,6},{6,5},{7,8},{8,7},{9,10},{10,9},{11,... | collective-permute-start | bytes 786440 | tf_op jit(solution)/shard_map/ppermute | solution.py:487
  67.2 21.7 %collective-permute-start.16 = (f32[256,256]{1,0:T(8,128)S(1)}, f32[256,256]{1,0:T(8,128)S(1)}, u32[]{:S(2)}, u32[]{:S(2)}) collective-permute-start(f32[256,256]{1,0:T(8,128)S(1)} %get-tuple-element.89), channel_id=1, source_target_pairs={{0,1},{1,0},{2,3},{3,2},{4,5},{5,4},{6,7},{7,6},{8,9},{9,8},{10,11... | collective-permute-start | bytes 786440 | tf_op jit(solution)/shard_map/ppermute | solution.py:488
  68.7 20.2 %collective-permute-start.17 = (f32[256,256]{1,0:T(8,128)S(1)}, f32[256,256]{1,0:T(8,128)S(1)}, u32[]{:S(2)}, u32[]{:S(2)}) collective-permute-start(f32[256,256]{1,0:T(8,128)S(1)} %get-tuple-element.90), channel_id=1, source_target_pairs={{1,2},{2,1},{3,4},{4,3},{5,6},{6,5},{7,8},{8,7},{9,10},{10,9},{11,... | collective-permute-start | bytes 786440 | tf_op jit(solution)/shard_map/ppermute | solution.py:487
  74.8 6.8 %collective-permute-start.18 = (f32[8,256]{1,0:T(8,128)S(1)}, f32[8,256]{1,0:T(8,128)S(1)}, u32[]{:S(2)}, u32[]{:S(2)}) collective-permute-start(f32[8,256]{1,0:T(8,128)S(1)} %slice_add_fusion), channel_id=1, source_target_pairs={{0,2},{1,3},{2,0},{3,1},{4,6},{5,7},{6,4},{7,5},{8,10},{9,11},{10,... | collective-permute-start | bytes 24584 | tf_op jit(solution)/shard_map/ppermute | solution.py:474
  76.6 17.9 %collective-permute-start.14 = (f32[256,256]{1,0:T(8,128)S(1)}, f32[256,256]{1,0:T(8,128)S(1)}, u32[]{:S(2)}, u32[]{:S(2)}) collective-permute-start(f32[256,256]{1,0:T(8,128)S(1)} %get-tuple-element.86), channel_id=1, source_target_pairs={{0,1},{1,0},{2,3},{3,2},{4,5},{5,4},{6,7},{7,6},{8,9},{9,8},{10,11... | collective-permute-start | bytes 786440 | tf_op jit(solution)/shard_map/ppermute | solution.py:488
  78.3 16.1 %collective-permute-start.15 = (f32[256,256]{1,0:T(8,128)S(1)}, f32[256,256]{1,0:T(8,128)S(1)}, u32[]{:S(2)}, u32[]{:S(2)}) collective-permute-start(f32[256,256]{1,0:T(8,128)S(1)} %get-tuple-element.87), channel_id=1, source_target_pairs={{1,2},{2,1},{3,4},{4,3},{5,6},{6,5},{7,8},{8,7},{9,10},{10,9},{11,... | collective-permute-start | bytes 786440 | tf_op jit(solution)/shard_map/ppermute | solution.py:487
  81.6 4.9 %collective-permute-start.19 = (f32[8,256]{1,0:T(8,128)S(1)}, f32[8,256]{1,0:T(8,128)S(1)}, u32[]{:S(2)}, u32[]{:S(2)}) collective-permute-start(f32[8,256]{1,0:T(8,128)S(1)} %add.54), channel_id=1, source_target_pairs={{0,4},{1,5},{2,6},{3,7},{4,0},{5,1},{6,2},{7,3},{8,12},{9,13},{10,... | collective-permute-start | bytes 24584 | tf_op jit(solution)/shard_map/ppermute | solution.py:474
  82.7 6.3 %copy-start.2 = (f32[4240,128]{1,0:T(8,128)S(1)}, f32[4240,128]{1,0:T(8,128)}, u32[]{:S(2)}) copy-start(f32[4240,128]{1,0:T(8,128)} %copy-done.1) | copy-start | bytes 6512644
  82.7 6.3 %copy-start.4 = (f32[4240,128]{1,0:T(8,128)S(1)}, f32[4240,128]{1,0:T(8,128)}, u32[]{:S(2)}) copy-start(f32[4240,128]{1,0:T(8,128)} %copy-done.3) | copy-start | bytes 6512644
  86.5 7.9 %collective-permute-start.20 = (f32[8,256]{1,0:T(8,128)S(1)}, f32[8,256]{1,0:T(8,128)S(1)}, u32[]{:S(2)}, u32[]{:S(2)}) collective-permute-start(f32[8,256]{1,0:T(8,128)S(1)} %add.55), channel_id=1, source_target_pairs={{0,8},{1,9},{2,10},{3,11},{4,12},{5,13},{6,14},{7,15},{8,0},{9,1},... | collective-permute-start | bytes 24584 | tf_op jit(solution)/shard_map/ppermute | solution.py:474
  96.0 5.2 %collective-permute-start.21 = (f32[2,4224]{1,0:T(2,128)S(1)}, f32[2,4224]{1,0:T(2,128)S(1)}, u32[]{:S(2)}, u32[]{:S(2)}) collective-permute-start(f32[2,4224]{1,0:T(2,128)S(1)} %get-tuple-element.101), channel_id=1, source_target_pairs={{0,16},{16,32},{32,48},{48,0},{64,80},{80,96},{96,112},{112,64},{1... | collective-permute-start | bytes 101384 | tf_op jit(solution)/shard_map/ppermute | solution.py:478
  96.7 5.4 %collective-permute-start.22 = (f32[2,4224]{1,0:T(2,128)S(1)}, f32[2,4224]{1,0:T(2,128)S(1)}, u32[]{:S(2)}, u32[]{:S(2)}) collective-permute-start(f32[2,4224]{1,0:T(2,128)S(1)} %get-tuple-element.101), channel_id=1, source_target_pairs={{0,32},{16,48},{32,0},{48,16},{64,96},{80,112},{96,64},{112,80},{1... | collective-permute-start | bytes 101384 | tf_op jit(solution)/shard_map/ppermute | solution.py:478
  98.4 4.0 %collective-permute-start.23 = (f32[2,4224]{1,0:T(2,128)S(1)}, f32[2,4224]{1,0:T(2,128)S(1)}, u32[]{:S(2)}, u32[]{:S(2)}) collective-permute-start(f32[2,4224]{1,0:T(2,128)S(1)} %get-tuple-element.101), channel_id=1, source_target_pairs={{0,48},{16,0},{32,16},{48,32},{64,112},{80,64},{96,80},{112,96},{1... | collective-permute-start | bytes 101384 | tf_op jit(solution)/shard_map/ppermute | solution.py:478
  102.4 5.5 %collective-permute-start.24 = (f32[2,4224]{1,0:T(2,128)S(1)}, f32[2,4224]{1,0:T(2,128)S(1)}, u32[]{:S(2)}, u32[]{:S(2)}) collective-permute-start(f32[2,4224]{1,0:T(2,128)S(1)} %add_add_fusion), channel_id=1, source_target_pairs={{0,64},{16,80},{32,96},{48,112},{64,0},{80,16},{96,32},{112,48},{1... | collective-permute-start | bytes 101384 | tf_op jit(solution)/shard_map/ppermute | solution.py:474

commit v3 on v2

--- a/solution.py
+++ b/solution.py
@@ -22,6 +22,7 @@
 F0 = 8
 ROWS = F0 + NZ * ZP + 8
 SEG = HP // 8
+UNROLL = 11
 VERT = TIME_STEP * DIFF_VERTICAL
 KEEP = 1.0 - 2.0 * VERT
 f32 = jnp.float32
@@ -104,8 +105,28 @@
     return seg_load(ref, z - 1, h, r) + seg_load(ref, z + 1, h, r)
 
 
-def forward_plane(z, unroll, c_ref, ve_ref, vn_ref, co_ref, out_ref, slope_refs):
+def stage_rolls(stage_ref, ref, z, r, j, both):
     at_first, at_last = lane_masks()
+    pair = [seg_load(ref, z, h, r) for h in (0, 1)]
+    made = from_right(pair, 0.0, at_last) + (from_left(pair, 0.0, at_first) if both else [])
+    for n, value in enumerate(made):
+        start = (j * len(made) + n) * 8
+        stage_ref[start : start + 8, :] = value
+
+
+def staged(stage_ref, j, both):
+    count = 4 if both else 2
+    made = [stage_ref[(j * count + n) * 8 : (j * count + n) * 8 + 8, :] for n in range(count)]
+    return made[:2], made[2:]
+
+
+def next_block(z, next_z, i, unroll):
+    last = i == SEG // unroll - 1
+    return jnp.where(last, next_z, z), jnp.where(last, 0, (i + 1) * unroll)
+
+
+def forward_plane(z, next_z, unroll, stage_ref, c_ref, ve_ref, vn_ref, co_ref, out_ref, slope_refs):
+    at_first, _ = lane_masks()
 
     def flux(v, c6, b, f, sb, sf, refs, h, r):
         if refs is None:
@@ -118,10 +139,10 @@
             corrected = v * c6 + vw * u
         return corrected - (6.0 * DIFF_FLAT) * f
 
-    def one(r, c, b, sb, before):
+    def one(r, j, following, c, b, sb, before):
         after = [seg_load(c_ref, z, h, r + 1) for h in (0, 1)]
-        left = from_left(c, 0.0, at_first)
-        right = from_right(c, 0.0, at_last)
+        right, left = staged(stage_ref, j, True)
+        stage_rolls(stage_ref, c_ref, following[0], following[1] + j, j, True)
         f, sf, gx, gy = [], [], [], []
         for h in (0, 1):
             c6 = 6.0 * c[h]
@@ -155,26 +176,32 @@
         sb.append(sm)
 
     def block(i, carry):
+        following = next_block(z, next_z, i, unroll)
         for j in range(unroll):
-            carry = one(i * unroll + j, *carry)
+            carry = one(i * unroll + j, j, following, *carry)
         return carry
 
     lax.fori_loop(0, SEG // unroll, block, (c, b, sb, before))
     zero_plane_pads(out_ref, z)
 
 
+def stage_first(stage_ref, ref, z, unroll, both):
+    for j in range(unroll):
+        stage_rolls(stage_ref, ref, z, j, j, both)
+
+
 def over_planes(plane):
-    plane(0)
+    plane(0, 1)
 
     def inner(z, unused):
-        plane(z)
+        plane(z, z + 1)
         return unused
 
     lax.fori_loop(1, NZ - 1, inner, 0)
-    plane(NZ - 1)
-
-
-def first_kernel(start_ref, east_ref, north_ref, c_ref, ve_ref, vn_ref, out_ref, sem):
+    plane(NZ - 1, NZ - 1)
+
+
+def first_kernel(start_ref, east_ref, north_ref, c_ref, ve_ref, vn_ref, out_ref, stage_ref, sem):
     def copies(z):
         made = []
         for source, target in ((start_ref, c_ref), (east_ref, ve_ref), (north_ref, vn_ref)):
@@ -196,8 +223,9 @@
         zero_pads(ref)
     for copy in copies(0):
         copy.wait()
-
-    def plane(z):
+    stage_first(stage_ref, c_ref, 0, UNROLL, True)
+
+    def plane(z, next_z):
         if isinstance(z, int) and z == NZ - 1:
             pass
         else:
@@ -209,16 +237,20 @@
                 for copy in copies(z + ahead):
                     copy.start()
 
-        forward_plane(z, 11, c_ref, ve_ref, vn_ref, None, out_ref, None)
+        forward_plane(z, next_z, UNROLL, stage_ref, c_ref, ve_ref, vn_ref, None, out_ref, None)
 
     over_planes(plane)
 
 
-def step_kernel(c_ref, ve_ref, vn_ref, co_ref, out_ref, *slope_refs):
+def step_kernel(c_ref, ve_ref, vn_ref, co_ref, out_ref, *rest):
+    slope_refs, stage_ref = rest[:4], rest[4]
     zero_pads(out_ref)
+    stage_first(stage_ref, c_ref, 0, UNROLL, True)
     for i, ref in enumerate(slope_refs):
         ref[0:F0, :] = jnp.full((F0, 128), -6.0 * DIFF_FLAT if i % 2 else 0.0, f32)
-    over_planes(lambda z: forward_plane(z, 11, c_ref, ve_ref, vn_ref, co_ref, out_ref, slope_refs))
+    over_planes(
+        lambda z, next_z: forward_plane(z, next_z, UNROLL, stage_ref, c_ref, ve_ref, vn_ref, co_ref, out_ref, slope_refs)
+    )
 
 
 def facing():
@@ -231,22 +263,23 @@
     slab = lax.axis_index("slab")
     near_share = jnp.where((slab > 0) & (slab < lax.axis_size("slab") - 1), VERT, 0.0)
 
+    sides = ((z_chip, chip_ref, send_chip_ref, VERT), (z_near, near_ref, send_near_ref, near_share))
+
     def block(j, unused):
+        rows = pl.ds(pl.multiple_of(8 * j, 8), 8)
+        made = []
         for h in (0, 1):
             lanes = slice(h * 128, h * 128 + 128)
-            rows = pl.ds(pl.multiple_of(8 * j, 8), 8)
-            for z, halo_ref, send_ref, share in (
-                (z_chip, chip_ref, send_chip_ref, VERT),
-                (z_near, near_ref, send_near_ref, near_share),
-            ):
+            for z, halo_ref, send_ref, share in sides:
                 at = block_rows(z, h, j)
                 halo = halo_ref[rows, lanes]
                 if prior_ref is not None:
                     halo = halo + share * prior_ref[at, :]
-                value = field_ref[at, :] + VERT * halo
-                target_ref[at, :] = value
-                if send_ref is not None:
-                    send_ref[rows, lanes] = value
+                made.append((at, lanes, send_ref, field_ref[at, :] + VERT * halo))
+        for at, lanes, send_ref, value in made:
+            target_ref[at, :] = value
+            if send_ref is not None:
+                send_ref[rows, lanes] = value
         return unused
 
     lax.fori_loop(0, NX // 8, block, 0, unroll=4)
@@ -260,11 +293,14 @@
     z_chip, z_near = facing()
 
     def block(j, unused):
+        rows = pl.ds(pl.multiple_of(8 * j, 8), 8)
+        made = []
         for h in (0, 1):
             lanes = slice(h * 128, h * 128 + 128)
-            rows = pl.ds(pl.multiple_of(8 * j, 8), 8)
-            send_chip_ref[rows, lanes] = field_ref[block_rows(z_chip, h, j), :]
-            send_near_ref[rows, lanes] = field_ref[block_rows(z_near, h, j), :]
+            made.append((send_chip_ref, lanes, field_ref[block_rows(z_chip, h, j), :]))
+            made.append((send_near_ref, lanes, field_ref[block_rows(z_near, h, j), :]))
+        for send_ref, lanes, value in made:
+            send_ref[rows, lanes] = value
         return unused
 
     lax.fori_loop(0, NX // 8, block, 0, unroll=4)
@@ -292,54 +328,55 @@
         rows = pl.ds(pl.multiple_of(8 * j, 8), 8)
         for h in (0, 1):
             lanes = slice(h * 128, h * 128 + 128)
-            for p in (0, 1):
-                wide = wide_ref[p, rows, lanes]
-                for z in range(4 * p, 4 * p + 4):
-                    rate = wells_ref[z, rows, lanes].astype(f32) * wide
-                    at = block_rows(z, h, j)
-                    co_ref[at, :] = KEEP - rate
-                    out_ref[at, :] = field_ref[at, :] - rate * c0_ref[at, :]
+            rates = [wells_ref[z, rows, lanes].astype(f32) * wide_ref[z // 4, rows, lanes] for z in range(NZ)]
+            values = [
+                field_ref[block_rows(z, h, j), :] - rates[z] * c0_ref[block_rows(z, h, j), :] for z in range(NZ)
+            ]
+            for z in range(NZ):
+                co_ref[block_rows(z, h, j), :] = KEEP - rates[z]
+                out_ref[block_rows(z, h, j), :] = values[z]
         return unused
 
     lax.fori_loop(0, NX // 8, block, 0, unroll=2)
     fix_planes(chip_ref, near_ref, out_ref, out_ref, send_chip_ref, send_near_ref)
 
 
-def seed_kernel(chip_ref, near_ref, ahead_ref, monitors_ref, final_ref, adjoint_ref, send_chip_ref, send_near_ref, field_ref):
+def seed_kernel(chip_ref, near_ref, ahead_ref, monitors_ref, adjoint_ref, send_chip_ref, send_near_ref, field_ref):
     zero_pads(adjoint_ref)
     fix_planes(chip_ref, near_ref, ahead_ref, field_ref)
 
     def block(j, sums):
         mass, count = sums
         rows = pl.ds(pl.multiple_of(8 * j, 8), 8)
-        for z in range(NZ):
-            for h in (0, 1):
-                lanes = slice(h * 128, h * 128 + 128)
+        made = []
+        for h in (0, 1):
+            lanes = slice(h * 128, h * 128 + 128)
+            for z in range(NZ):
                 value = field_ref[block_rows(z, h, j), :]
-                final_ref[0, z, rows, lanes] = value
                 monitor = monitors_ref[z, rows, lanes].astype(f32)
                 seed = monitor * value
-                adjoint_ref[block_rows(z, h, j), :] = seed
+                made.append((block_rows(z, h, j), seed))
                 mass[z % 4] = mass[z % 4] + seed * value
                 count[z % 4] = count[z % 4] + monitor
+        for at, seed in made:
+            adjoint_ref[at, :] = seed
         return mass, count
 
     zeros = [jnp.zeros((8, 128), f32)] * 4
     mass, count = lax.fori_loop(0, NX // 8, block, (list(zeros), list(zeros)))
-    for part, start in ((mass, 0), (count, 128)):
-        part = (part[0] + part[1]) + (part[2] + part[3])
-        part = jnp.sum(jnp.sum(part, axis=0, keepdims=True), axis=1, keepdims=True)
-        send_chip_ref[NX : NX + 8, start : start + 128] = jnp.broadcast_to(part, (8, 128))
+    send_chip_ref[NX : NX + 8, 0:128] = (mass[0] + mass[1]) + (mass[2] + mass[3])
+    send_chip_ref[NX : NX + 8, 128:256] = (count[0] + count[1]) + (count[2] + count[3])
     send_planes(adjoint_ref, send_chip_ref, send_near_ref)
 
 
-def adjoint_plane(z, unroll, fields, rg_in_ref, out_ref, rg_ref):
+def adjoint_plane(z, next_z, unroll, stage_ref, fields, rg_in_ref, out_ref, rg_ref):
     a_ref, c_ref, ve_ref, vn_ref, co_ref, xb_ref, xf_ref, yb_ref, yf_ref = fields
     at_first, at_last = lane_masks()
 
-    def one(r, a, next_a, vg, behind, front):
+    def one(r, j, following, a, next_a, vg, behind, front):
         far_a = [seg_load(a_ref, z, h, r + 2) for h in (0, 1)]
-        right = from_right(a, 0.0, at_last)
+        right, _ = staged(stage_ref, j, False)
+        stage_rolls(stage_ref, a_ref, following[0], following[1] + j, j, False)
         vy, back_y, front_y = [], [], []
         for h in (0, 1):
             g = right[h] - a[h]
@@ -379,52 +416,78 @@
         front.append(seg_load(xf_ref, z, h, 0) * g0)
 
     def block(i, carry):
+        following = next_block(z, next_z, i, unroll)
         for j in range(unroll):
-            carry = one(i * unroll + j, *carry)
+            carry = one(i * unroll + j, j, following, *carry)
         return carry
 
     lax.fori_loop(0, SEG // unroll, block, (a, next_a, vg, behind, front))
     zero_plane_pads(out_ref, z)
 
 
-def edge_planes(fields, rg_in_ref, out_ref, rg_ref, send_chip_ref, send_near_ref):
+def edge_planes(stage_ref, fields, rg_in_ref, out_ref, rg_ref, send_chip_ref, send_near_ref):
     zero_pads(out_ref)
+    stage_first(stage_ref, fields[0], 0, UNROLL, False)
     for z in (0, NZ - 1):
-        adjoint_plane(z, 11, fields, rg_in_ref, out_ref, rg_ref)
+        adjoint_plane(z, NZ - 1, UNROLL, stage_ref, fields, rg_in_ref, out_ref, rg_ref)
     send_planes(out_ref, send_chip_ref, send_near_ref)
 
 
 def edge_kernel(*refs):
-    edge_planes(refs[:9], None, *refs[9:])
+    edge_planes(refs[-1], refs[:9], None, *refs[9:-1])
 
 
 def turn_kernel(chip_ref, near_ref, ahead_ref, *refs):
-    rest, rg_in_ref, (a_ref, out_ref, rg_ref, send_chip_ref, send_near_ref) = refs[:8], refs[8], refs[9:]
+    rest, rg_in_ref, (a_ref, out_ref, rg_ref, send_chip_ref, send_near_ref, stage_ref) = refs[:8], refs[8], refs[9:]
     fix_planes(chip_ref, near_ref, ahead_ref, a_ref)
-    edge_planes((a_ref,) + rest, rg_in_ref, out_ref, rg_ref, send_chip_ref, send_near_ref)
+    edge_planes(stage_ref, (a_ref,) + rest, rg_in_ref, out_ref, rg_ref, send_chip_ref, send_near_ref)
+
+
+def leave_kernel(*refs):
+    c_ref, final_ref, sem = refs[11], refs[-3], refs[-1]
+    copies = [
+        pltpu.make_async_copy(
+            c_ref.at[pl.ds(F0 + z * ZP + h * HP, NX), :], final_ref.at[0, z, :, pl.ds(h * 128, 128)], sem.at[z, h]
+        )
+        for z in range(NZ)
+        for h in (0, 1)
+    ]
+    for copy in copies:
+        copy.start()
+    inner_kernel(False, *refs[:11], *refs[12:14], refs[-2])
+    for copy in copies:
+        copy.wait()
 
 
 def inner_kernel(has_grad, *refs):
-    fields, (out_in_ref, rg_in_ref, out_ref, rg_ref) = refs[:9], refs[9:]
+    fields, (out_in_ref, rg_in_ref, out_ref, rg_ref, stage_ref) = refs[:9], refs[9:]
+    stage_first(stage_ref, fields[0], 1, UNROLL, False)
 
     def inner(z, unused):
-        adjoint_plane(z, 11, fields, rg_in_ref if has_grad else None, out_ref, rg_ref)
+        adjoint_plane(z, z + 1, UNROLL, stage_ref, fields, rg_in_ref if has_grad else None, out_ref, rg_ref)
         return unused
 
     lax.fori_loop(1, NZ - 1, inner, 0)
 
 
 def last_kernel(chip_ref, near_ref, prior_ref, ahead_ref, *refs):
-    rest, rg_in_ref, (a_ref, out_ref, rg_ref) = refs[:8], refs[8], refs[9:]
+    rest, rg_in_ref, (a_ref, out_ref, rg_ref, stage_ref) = refs[:8], refs[8], refs[9:]
     fix_planes(chip_ref, near_ref, ahead_ref, a_ref, prior_ref=prior_ref)
     zero_pads(out_ref)
-    over_planes(lambda z: adjoint_plane(z, 11, (a_ref,) + rest, rg_in_ref, out_ref, rg_ref))
+    stage_first(stage_ref, a_ref, 0, UNROLL, False)
+    over_planes(
+        lambda z, next_z: adjoint_plane(z, next_z, UNROLL, stage_ref, (a_ref,) + rest, rg_in_ref, out_ref, rg_ref)
+    )
 
 
 def restrict_kernel(share, cells, limit_ref, chip_ref, near_ref, prior_ref, ahead_ref, c0_ref, rg_ref, wells_ref, sums_ref, out_ref, field_ref, wide_ref):
     fix_planes(chip_ref, near_ref, ahead_ref, field_ref, prior_ref=prior_ref)
-    count = jnp.maximum(sums_ref[0:8, 128:256], 1.0)
-    scaled = (sums_ref[0:8, 0:128] / count - limit_ref[0]) / SOFT_WIDTH
+
+    def all_of(value):
+        return jnp.broadcast_to(jnp.sum(jnp.sum(value, axis=0, keepdims=True), axis=1, keepdims=True), (8, 128))
+
+    count = jnp.maximum(all_of(sums_ref[0:8, 128:256]), 1.0)
+    scaled = (all_of(sums_ref[0:8, 0:128]) / count - limit_ref[0]) / SOFT_WIDTH
     small = jnp.exp(-jnp.abs(scaled))
     weight = jnp.where(scaled >= 0.0, 1.0, small) / (1.0 + small) * share
     soft = SOFT_WIDTH * (jnp.maximum(scaled, 0.0) + jnp.log1p(small)) * share
@@ -440,7 +503,7 @@
                 for z in range(4 * p, 4 * p + 4):
                     at = block_rows(z, h, j)
                     parts.append(wells_ref[z, rows, lanes].astype(f32) * (rg_ref[at, :] + c0_ref[at, :] * field_ref[at, :]))
-                wide_ref[p, rows, lanes] = ((parts[0] + parts[1]) + (parts[2] + parts[3])) * scale
+                wide_ref[p, rows, lanes] = (parts[0] + parts[1]) + (parts[2] + parts[3])
         return unused
 
     lax.fori_loop(0, NX // 8, block, 0, unroll=2)
@@ -452,7 +515,7 @@
     own = (row < 4) == (lane < 64)
     for p in (0, 1):
         part = jnp.dot(wide_ref[p], sums, precision=lax.Precision.HIGHEST, preferred_element_type=f32)
-        part = jnp.where(own, part, 0.0).reshape(NX // 8, 8, 128).sum(axis=1)
+        part = jnp.where(own, part, 0.0).reshape(NX // 8, 8, 128).sum(axis=1) * scale[0:1, :]
         for j in range(NX // 8):
             out_ref[p : p + 1, j * 128 : (j + 1) * 128] = part[j : j + 1, :]
 
@@ -466,6 +529,10 @@
     )
 
 
+def stage(count):
+    return pltpu.VMEM((UNROLL * count * 8, 128), f32)
+
+
 def dma(*shape):
     return pltpu.SemaphoreType.DMA(shape)
 
@@ -474,10 +541,8 @@
     return value + lax.ppermute(value, axis, [(i, i ^ step) for i in range(size)])
 
 
-def scen_sum(value):
-    others = [lax.ppermute(value, "scen", [(i, (i & 4) | ((i + k) & 3)) for i in range(8)]) for k in (1, 2, 3)]
-    value = (value + others[0]) + (others[1] + others[2])
-    return pair_sum(value, "scen", 8, 4)
+def scen_others(value, steps):
+    return [lax.ppermute(value, "scen", [(i, i ^ k) for i in range(8)]) for k in steps]
 
 
 def swap(slab_count, send_chip, send_near):
@@ -497,11 +562,14 @@
 
     low, high = start[0, 0], start[0, NZ - 1]
     halos = swap(slab_count, jnp.where(odd == 0, high, low), jnp.where(odd == 0, low, high))
-    consensus = scen_sum((control + multiplier)[0]) / scen_count
+    own = (control + multiplier)[0]
+    near = scen_others(own, (1, 2, 3))
+    own = (own + near[0]) + (near[1] + near[2])
+    consensus = pair_sum(own, "scen", scen_count, 4) / scen_count
 
     c0, ve, vn, ahead = call(
         first_kernel, 3 << 30,
-        in_specs=[HBM] * 3, out_specs=[VM] * 4, out_shape=[FIELD] * 4, scratch_shapes=[dma(NZ, 6)],
+        in_specs=[HBM] * 3, out_specs=[VM] * 4, out_shape=[FIELD] * 4, scratch_shapes=[stage(4), dma(NZ, 6)],
     )(in_hbm(start), in_hbm(flow_east), in_hbm(flow_north))
     c, send_chip, send_near, co = call(
         rate_kernel, 1 << 28,
@@ -513,7 +581,7 @@
     slopes = [()]
     for k in range(1, STEPS):
         halos = swap(slab_count, send_chip, send_near)
-        ahead, *made = call(step_kernel, 3 << 30, in_specs=[VM] * 4, out_specs=[VM] * 5, out_shape=[FIELD] * 5)(c, ve, vn, co)
+        ahead, *made = call(step_kernel, 3 << 30, in_specs=[VM] * 4, out_specs=[VM] * 5, out_shape=[FIELD] * 5, scratch_shapes=[stage(4)])(c, ve, vn, co)
         slopes.append(tuple(made))
         if k < STEPS - 1:
             c, send_chip, send_near = call(
@@ -522,45 +590,46 @@
                 input_output_aliases={2: 0},
             )(*halos, ahead)
             states.append(c)
-    final, seed, send_chip, send_near, _ = call(
+    seed, send_chip, send_near, last = call(
         seed_kernel, 1 << 28,
-        in_specs=[VM] * 4, out_specs=[VM] * 5,
-        out_shape=[
-            jax.ShapeDtypeStruct((1, NZ, NX, NY), f32), FIELD, jax.ShapeDtypeStruct((NX + 8, NY), f32), PLANE, FIELD,
-        ],
-        input_output_aliases={2: 4},
+        in_specs=[VM] * 4, out_specs=[VM] * 4,
+        out_shape=[FIELD, jax.ShapeDtypeStruct((NX + 8, NY), f32), PLANE, FIELD],
+        input_output_aliases={2: 3},
     )(*halos, ahead, monitors)
 
     def rest(k):
         return (states[k], ve, vn, co) + slopes[k]
-
-    def inner(k, adjoint, ahead, grad):
-        return call(
-            functools.partial(inner_kernel, k < STEPS - 1), 2 << 30,
-            in_specs=[VM] * 11, out_specs=[VM] * 2, out_shape=[FIELD] * 2, input_output_aliases={9: 0, 10: 1},
-        )(adjoint, *rest(k), ahead, grad)
 
     halos4 = swap(slab_count, send_chip, send_near)
     ahead, grad, send_chip5, send_near5 = call(
         edge_kernel, 1 << 30,
-        in_specs=[VM] * 9, out_specs=[VM] * 4, out_shape=[FIELD, FIELD, PLANE, PLANE],
+        in_specs=[VM] * 9, out_specs=[VM] * 4, out_shape=[FIELD, FIELD, PLANE, PLANE], scratch_shapes=[stage(2)],
     )(seed, *rest(3))
     halos5 = swap(slab_count, send_chip5, send_near5)
     sums = send_chip[NX:] + halos4[0][NX:]
     sums = pair_sum(sums, "slab", slab_count, 2)
-    ahead, grad = inner(3, seed, ahead, grad)
+    ahead, grad, final = call(
+        leave_kernel, 2 << 30,
+        in_specs=[VM] * 12, out_specs=[VM, VM, HBM],
+        out_shape=[FIELD, FIELD, jax.ShapeDtypeStruct((1, NZ, NX, NY), f32)],
+        input_output_aliases={9: 0, 10: 1}, scratch_shapes=[stage(2), dma(NZ, 2)],
+    )(seed, *rest(3), ahead, grad, last)
     adjoint3, ahead, grad, send_chip, send_near = call(
         turn_kernel, 1 << 30,
         in_specs=[VM] * 12, out_specs=[VM] * 5, out_shape=[FIELD, FIELD, FIELD, PLANE, PLANE],
-        input_output_aliases={2: 0, 11: 2},
+        input_output_aliases={2: 0, 11: 2}, scratch_shapes=[stage(2)],
     )(*halos4, ahead, *rest(2), grad)
     halos6 = swap(slab_count, send_chip, send_near)
     sums = pair_sum(sums, "slab", slab_count, 4)
-    ahead, grad = inner(2, adjoint3, ahead, grad)
+    ahead, grad = call(
+        functools.partial(inner_kernel, True), 2 << 30,
+        in_specs=[VM] * 11, out_specs=[VM] * 2, out_shape=[FIELD] * 2,
+        input_output_aliases={9: 0, 10: 1}, scratch_shapes=[stage(2)],
+    )(adjoint3, *rest(2), ahead, grad)
     sums = pair_sum(sums, "slab", slab_count, 8)
     _, ahead, grad = call(
         last_kernel, 3 << 30,
-        in_specs=[VM] * 13, out_specs=[VM] * 3, out_shape=[FIELD] * 3, input_output_aliases={3: 0, 12: 2},
+        in_specs=[VM] * 13, out_specs=[VM] * 3, out_shape=[FIELD] * 3, input_output_aliases={3: 0, 12: 2}, scratch_shapes=[stage(2)],
     )(*halos5, seed, ahead, *rest(1), grad)
     share = 1.0 / ((1.0 - BETA_LEVEL) * scen_count)
     coarse_cells = NZ * slab_count * NX * NY / 64.0
@@ -571,7 +640,9 @@
         scratch_shapes=[pltpu.VMEM((2, NX, NY), f32)],
         input_output_aliases={4: 1},
     )(threshold, *halos6, adjoint3, ahead, c0, grad, wells, sums)
-    total = scen_sum(coarse)
+    near = scen_others(coarse, (1, 2, 3))
+    total = (coarse + near[0]) + (near[1] + near[2])
+    total = pair_sum(total, "scen", scen_count, 4)
     consensus_next = consensus - total[:, :4096]
     multiplier_next = multiplier + control - consensus_next[None]
     return (final, consensus_next, multiplier_next, threshold + total[0, 4096:4097])

time: 112 us -> 105 us (0.938)
  Pallas kernels: 54.5 us -> 45.3 us
  starting transfers between devices: 41.8 us -> 43.2 us
    pallas_call x3, Pallas kernels: 23.6 us -> 20.7 us  [on_device(): call(step_kernel, 3 << 30, in_specs=[VM] * 4, out_specs=[VM] * 5, out_sha...]
    pallas_call x3, Pallas kernels: 10 us -> 7.33 us  [the longest x1 3.35 us: on_device(): call(leave_kernel, 2 << 30, in_specs=[VM] * 12, out_specs=[VM, VM, HBM],...]
    ppermute x6, waiting for transfers between devices: 2.92 us -> 4.44 us  [scen_others(): lax.ppermute(value, 'scen', [(i, i ^ k) for i in range(8)])]
    pallas_call x1, Pallas kernels: 2.29 us -> 1.15 us  [on_device(): call(rate_kernel, 1 << 28, in_specs=[VM] * 6, out_specs=[VM] * 4, out_sha...]
  transfers between devices with their start and end apart: 25 -> 25, of which waited for: 4 -> 4; matrix products, arithmetic and copies ran while one was open for 1% -> 1% of each run, Pallas kernels for 43% -> 40%
where the time goes in v3:
time: 105 us; the launch traced here: 104 us
  Pallas kernels  45.3 us (43%)
  starting transfers between devices  43.2 us (41%)
  waiting for transfers between devices  8.8 us (8%)
  between operations  3.49 us (3%)
  other arithmetic  2.64 us (3%)
    pallas_call x3, Pallas kernels, on_device(): call(step_kernel, 3 << 30, in_specs=[VM] * 4, out_specs=[VM] * 5, out_sha...  20.7 us
    ppermute x7, starting transfers between devices, swap(): got_near = lax.ppermute(send_near, 'slab', near)  15.9 us
    ppermute x7, starting transfers between devices, swap(): lax.ppermute(send_chip, 'slab', [(i, i ^ 1) for i in range(slab_count)])  11.1 us
    ppermute x6, starting transfers between devices, scen_others(): lax.ppermute(value, 'scen', [(i, i ^ k) for i in range(8)])  9.11 us
    pallas_call x1, Pallas kernels, on_device(): call(first_kernel, 3 << 30, in_specs=[HBM] * 3, out_specs=[VM] * 4, out_s...  7.12 us
    ppermute x5, starting transfers between devices, pair_sum(): lax.ppermute(value, axis, [(i, i ^ step) for i in range(size)])  7.02 us
    pallas_call x1, Pallas kernels, on_device(): call(last_kernel, 3 << 30, in_specs=[VM] * 13, out_specs=[VM] * 3, out_sh...  4.46 us
    ppermute x6, waiting for transfers between devices, scen_others(): lax.ppermute(value, 'scen', [(i, i ^ k) for i in range(8)])  4.44 us
  transfers between devices with their start and end apart: 25, of which 4 were waited for; matrix products, arithmetic and copies ran while one was open for 1% of the time, Pallas kernels for 40%

profile of v3, /device:TPU:2, one launch (start us, length us, event | category | flops | bytes accessed | tf_op | source)
XLA Modules:
  0.0 103.9 jit_solution(3233624838199056410)
XLA Ops:
  0.6 0.8 add.48
  1.4 3.3 %collective-permute-start.3 = (f32[2,4096]{1,0:T(2,128)S(1)}, f32[2,4096]{1,0:T(2,128)S(1)}, u32[]{:S(2)}, u32[]{:S(2)}) collective-permute-start(f32[2,4096]{1,0:T(2,128)S(1)} %bitcast.9), channel_id=1, source_target_pairs={{0,32},{16,48},{32,0},{48,16},{64,96},{80,112},{96,64},{112,80},{1... | collective-permute-start | bytes 98312 | tf_op jit(solution)/shard_map/ppermute | solution.py:545
  4.7 1.1 %collective-permute-start.4 = (f32[2,4096]{1,0:T(2,128)S(1)}, f32[2,4096]{1,0:T(2,128)S(1)}, u32[]{:S(2)}, u32[]{:S(2)}) collective-permute-start(f32[2,4096]{1,0:T(2,128)S(1)} %bitcast.10), channel_id=1, source_target_pairs={{0,48},{16,32},{32,16},{48,0},{64,112},{80,96},{96,80},{112,64},{1... | collective-permute-start | bytes 98312 | tf_op jit(solution)/shard_map/ppermute | solution.py:545
  5.8 1.1 %select_bitcast_fusion = (f32[256,256]{1,0:T(8,128)S(1)}, f32[256,256]{1,0:T(8,128)S(1)}) fusion(f32[1,8,256,256]{3,2,1,0:T(8,128)} %start_ref.1, pred[]{:T(512)S(6)} %eq.6), kind=kLoop, calls=%fused_computation | loop fusion | flops 131072 | bytes 1048577 | tf_op jit(solution)/shard_map/jit(_where)/select_n | solution.py:564
  6.8 0.1 collective-permute-start
  6.9 2.5 %collective-permute-start.1 = (f32[256,256]{1,0:T(8,128)S(1)}, f32[256,256]{1,0:T(8,128)S(1)}, u32[]{:S(2)}, u32[]{:S(2)}) collective-permute-start(f32[256,256]{1,0:T(8,128)S(1)} %get-tuple-element.106), channel_id=1, source_target_pairs={{1,2},{2,1},{3,4},{4,3},{5,6},{6,5},{7,8},{8,7},{9,10},{10,9},{11,... | collective-permute-start | bytes 786440 | tf_op jit(solution)/shard_map/ppermute | solution.py:552
  9.5 0.0 collective-permute-done.3
  9.5 0.4 collective-permute-done.4
  9.9 0.0 copy-start
  9.9 2.2 %collective-permute-start.5 = (f32[2,4096]{1,0:T(2,128)S(1)}, f32[2,4096]{1,0:T(2,128)S(1)}, u32[]{:S(2)}, u32[]{:S(2)}) collective-permute-start(f32[2,4096]{1,0:T(2,128)S(1)} %add_add_fusion.1), channel_id=1, source_target_pairs={{0,64},{16,80},{32,96},{48,112},{64,0},{80,16},{96,32},{112,48},{1... | collective-permute-start | bytes 98312 | tf_op jit(solution)/shard_map/ppermute | solution.py:541
  12.1 7.1 %shard_map.111 = (f32[4240,128]{1,0:T(8,128)S(1)}, f32[4240,128]{1,0:T(8,128)S(1)}, f32[4240,128]{1,0:T(8,128)S(1)}, f32[4240,128]{1,0:T(8,128)S(1)}) custom-call(f32[1,8,256,256]{3,2,1,0:T(8,128)} %start_ref.1, f32[1,8,256,256]{3,2,1,0:T(8,128)} %east_ref.1, f32[1,8,256,256]{3,2,1,0:T(8,128)} %north_ref.1), custom_call_target="tpu_custom_call" | custom-call | flops 3221225472 | bytes 1048576 | tf_op jit(solution)/shard_map/pallas_call | solution.py:570
  19.9 1.1 %shard_map.112 = (f32[4240,128]{1,0:T(8,128)S(1)}, f32[256,256]{1,0:T(8,128)S(1)}, f32[256,256]{1,0:T(8,128)S(1)}, f32[4240,128]{1,0:T(8,128)S(1)}) custom-call(f32[256,256]{1,0:T(8,128)S(1)} %collective-permute-done.chip_ref, f32[256,256]{1,0:T(8,128)S(1)} %collective-permute-done.1.near_ref, ...), custom_call_target="tpu_custom_call", output_to_operand_aliasing={{0}: (2, {})} | custom-call | flops 268435456 | bytes 1048576 | tf_op jit(solution)/shard_map/pallas_call | solution.py:574
  21.1 1.1 %collective-permute-start.6 = (f32[256,256]{1,0:T(8,128)S(1)}, f32[256,256]{1,0:T(8,128)S(1)}, u32[]{:S(2)}, u32[]{:S(2)}) collective-permute-start(f32[256,256]{1,0:T(8,128)S(1)} %get-tuple-element.56), channel_id=1, source_target_pairs={{0,1},{1,0},{2,3},{3,2},{4,5},{5,4},{6,7},{7,6},{8,9},{9,8},{10,11... | collective-permute-start | bytes 786440 | tf_op jit(solution)/shard_map/ppermute | solution.py:553
  22.2 2.4 %collective-permute-start.7 = (f32[256,256]{1,0:T(8,128)S(1)}, f32[256,256]{1,0:T(8,128)S(1)}, u32[]{:S(2)}, u32[]{:S(2)}) collective-permute-start(f32[256,256]{1,0:T(8,128)S(1)} %get-tuple-element.57), channel_id=1, source_target_pairs={{1,2},{2,1},{3,4},{4,3},{5,6},{6,5},{7,8},{8,7},{9,10},{10,9},{11,... | collective-permute-start | bytes 786440 | tf_op jit(solution)/shard_map/ppermute | solution.py:552
  24.6 6.9 %shard_map.113 = (f32[4240,128]{1,0:T(8,128)S(1)}, f32[4240,128]{1,0:T(8,128)S(1)}, f32[4240,128]{1,0:T(8,128)S(1)}, f32[4240,128]{1,0:T(8,128)S(1)}, f32[4240,128]{1,0:T(8,128)S(1)}) custom-call(f32[4240,128]{1,0:T(8,128)S(1)} %get-tuple-element.58.c_ref.refs_0_, f32[4240,128]{1,0:T(8,128)S(1)} %get-tuple-element.59.ve_ref.refs_2_.refs_1_, ...), custom_call_target="tpu_custom_call" | custom-call | flops 3221225472 | bytes 1048576 | tf_op jit(solution)/shard_map/pallas_call | solution.py:584
  31.6 0.2 shard_map.114
  31.8 1.9 %collective-permute-start.8 = (f32[256,256]{1,0:T(8,128)S(1)}, f32[256,256]{1,0:T(8,128)S(1)}, u32[]{:S(2)}, u32[]{:S(2)}) collective-permute-start(f32[256,256]{1,0:T(8,128)S(1)} %get-tuple-element.63), channel_id=1, source_target_pairs={{0,1},{1,0},{2,3},{3,2},{4,5},{5,4},{6,7},{7,6},{8,9},{9,8},{10,11... | collective-permute-start | bytes 786440 | tf_op jit(solution)/shard_map/ppermute | solution.py:553
  33.7 1.9 %collective-permute-start.9 = (f32[256,256]{1,0:T(8,128)S(1)}, f32[256,256]{1,0:T(8,128)S(1)}, u32[]{:S(2)}, u32[]{:S(2)}) collective-permute-start(f32[256,256]{1,0:T(8,128)S(1)} %get-tuple-element.64), channel_id=1, source_target_pairs={{1,2},{2,1},{3,4},{4,3},{5,6},{6,5},{7,8},{8,7},{9,10},{10,9},{11,... | collective-permute-start | bytes 786440 | tf_op jit(solution)/shard_map/ppermute | solution.py:552
  35.6 6.9 %shard_map.115 = (f32[4240,128]{1,0:T(8,128)S(1)}, f32[4240,128]{1,0:T(8,128)S(1)}, f32[4240,128]{1,0:T(8,128)S(1)}, f32[4240,128]{1,0:T(8,128)S(1)}, f32[4240,128]{1,0:T(8,128)S(1)}) custom-call(f32[4240,128]{1,0:T(8,128)S(1)} %get-tuple-element.65.c_ref.refs_0_.refs_1_, f32[4240,128]{1,0:T(8,128)S(1)} %get-tuple-element.59.ve_ref.refs_2_.refs_1_, ...), custom_call_target="tpu_custom_call" | custom-call | flops 3221225472 | bytes 1048576 | tf_op jit(solution)/shard_map/pallas_call | solution.py:584
  42.5 0.2 shard_map.116
  42.7 2.2 %collective-permute-start.10 = (f32[256,256]{1,0:T(8,128)S(1)}, f32[256,256]{1,0:T(8,128)S(1)}, u32[]{:S(2)}, u32[]{:S(2)}) collective-permute-start(f32[256,256]{1,0:T(8,128)S(1)} %get-tuple-element.67), channel_id=1, source_target_pairs={{0,1},{1,0},{2,3},{3,2},{4,5},{5,4},{6,7},{7,6},{8,9},{9,8},{10,11... | collective-permute-start | bytes 786440 | tf_op jit(solution)/shard_map/ppermute | solution.py:553
  44.9 1.9 %collective-permute-start.11 = (f32[256,256]{1,0:T(8,128)S(1)}, f32[256,256]{1,0:T(8,128)S(1)}, u32[]{:S(2)}, u32[]{:S(2)}) collective-permute-start(f32[256,256]{1,0:T(8,128)S(1)} %get-tuple-element.68), channel_id=1, source_target_pairs={{1,2},{2,1},{3,4},{4,3},{5,6},{6,5},{7,8},{8,7},{9,10},{10,9},{11,... | collective-permute-start | bytes 786440 | tf_op jit(solution)/shard_map/ppermute | solution.py:552
  46.8 0.0 copy-start.3
  46.8 6.9 %shard_map.117 = (f32[4240,128]{1,0:T(8,128)S(1)}, f32[4240,128]{1,0:T(8,128)S(1)}, f32[4240,128]{1,0:T(8,128)S(1)}, f32[4240,128]{1,0:T(8,128)S(1)}, f32[4240,128]{1,0:T(8,128)S(1)}) custom-call(f32[4240,128]{1,0:T(8,128)S(1)} %get-tuple-element.69.c_ref.refs_1_, f32[4240,128]{1,0:T(8,128)S(1)} %get-tuple-element.59.ve_ref.refs_2_.refs_1_, ...), custom_call_target="tpu_custom_call" | custom-call | flops 3221225472 | bytes 1048576 | tf_op jit(solution)/shard_map/pallas_call | solution.py:584
  53.7 0.8 shard_map.118
  54.5 2.2 %collective-permute-start.12 = (f32[264,256]{1,0:T(8,128)S(1)}, f32[264,256]{1,0:T(8,128)S(1)}, u32[]{:S(2)}, u32[]{:S(2)}) collective-permute-start(f32[264,256]{1,0:T(8,128)S(1)} %get-tuple-element.80), channel_id=1, source_target_pairs={{0,1},{1,0},{2,3},{3,2},{4,5},{5,4},{6,7},{7,6},{8,9},{9,8},{10,11... | collective-permute-start | bytes 811016 | tf_op jit(solution)/shard_map/ppermute | solution.py:553
  56.8 1.9 %collective-permute-start.13 = (f32[256,256]{1,0:T(8,128)S(1)}, f32[256,256]{1,0:T(8,128)S(1)}, u32[]{:S(2)}, u32[]{:S(2)}) collective-permute-start(f32[256,256]{1,0:T(8,128)S(1)} %get-tuple-element.81), channel_id=1, source_target_pairs={{1,2},{2,1},{3,4},{4,3},{5,6},{6,5},{7,8},{8,7},{9,10},{10,9},{11,... | collective-permute-start | bytes 786440 | tf_op jit(solution)/shard_map/ppermute | solution.py:552
  58.7 1.2 %shard_map.119 = (f32[4240,128]{1,0:T(8,128)S(1)}, f32[4240,128]{1,0:T(8,128)S(1)}, f32[256,256]{1,0:T(8,128)S(1)}, f32[256,256]{1,0:T(8,128)S(1)}) custom-call(f32[4240,128]{1,0:T(8,128)S(1)} %get-tuple-element.71.refs_0_.prior_ref, f32[4240,128]{1,0:T(8,128)S(1)} %get-tuple-element.69.c_ref.refs_1_, ...), custom_call_target="tpu_custom_call" | custom-call | flops 1073741824 | bytes 1048576 | tf_op jit(solution)/shard_map/pallas_call | solution.py:604
  59.9 1.7 %collective-permute-start.16 = (f32[256,256]{1,0:T(8,128)S(1)}, f32[256,256]{1,0:T(8,128)S(1)}, u32[]{:S(2)}, u32[]{:S(2)}) collective-permute-start(f32[256,256]{1,0:T(8,128)S(1)} %get-tuple-element.91), channel_id=1, source_target_pairs={{0,1},{1,0},{2,3},{3,2},{4,5},{5,4},{6,7},{7,6},{8,9},{9,8},{10,11... | collective-permute-start | bytes 786440 | tf_op jit(solution)/shard_map/ppermute | solution.py:553
  61.5 2.1 %collective-permute-start.17 = (f32[256,256]{1,0:T(8,128)S(1)}, f32[256,256]{1,0:T(8,128)S(1)}, u32[]{:S(2)}, u32[]{:S(2)}) collective-permute-start(f32[256,256]{1,0:T(8,128)S(1)} %get-tuple-element.92), channel_id=1, source_target_pairs={{1,2},{2,1},{3,4},{4,3},{5,6},{6,5},{7,8},{8,7},{9,10},{10,9},{11,... | collective-permute-start | bytes 786440 | tf_op jit(solution)/shard_map/ppermute | solution.py:552
  63.6 3.3 %shard_map.120 = (f32[4240,128]{1,0:T(8,128)S(1)}, f32[4240,128]{1,0:T(8,128)S(1)}, f32[1,8,256,256]{3,2,1,0:T(8,128)}) custom-call(f32[4240,128]{1,0:T(8,128)S(1)} %get-tuple-element.71.refs_0_.prior_ref, f32[4240,128]{1,0:T(8,128)S(1)} %get-tuple-element.69.c_ref.refs_1_, ...), custom_call_target="tpu_custom_call", output_to_operand_aliasing={{0}: (9, {}), {1}: (10, {})} | custom-call | flops 2147483648 | bytes 1048576 | tf_op jit(solution)/shard_map/pallas_call | solution.py:611
  67.0 0.1 collective-permute-start.18
  67.1 1.4 %shard_map.121 = (f32[4240,128]{1,0:T(8,128)S(1)}, f32[4240,128]{1,0:T(8,128)S(1)}, f32[4240,128]{1,0:T(8,128)S(1)}, f32[256,256]{1,0:T(8,128)S(1)}, f32[256,256]{1,0:T(8,128)S(1)}) custom-call(f32[264,256]{1,0:T(8,128)S(1)} %collective-permute-done.12.chip_ref, ...), custom_call_target="tpu_custom_call", output_to_operand_aliasing={{0}: (2, {}), {2}: (11, {})} | custom-call | flops 1073741824 | bytes 1048576 | tf_op jit(solution)/shard_map/pallas_call | solution.py:617
  68.5 1.9 %collective-permute-start.14 = (f32[256,256]{1,0:T(8,128)S(1)}, f32[256,256]{1,0:T(8,128)S(1)}, u32[]{:S(2)}, u32[]{:S(2)}) collective-permute-start(f32[256,256]{1,0:T(8,128)S(1)} %get-tuple-element.88), channel_id=1, source_target_pairs={{0,1},{1,0},{2,3},{3,2},{4,5},{5,4},{6,7},{7,6},{8,9},{9,8},{10,11... | collective-permute-start | bytes 786440 | tf_op jit(solution)/shard_map/ppermute | solution.py:553
  70.4 3.2 %collective-permute-start.15 = (f32[256,256]{1,0:T(8,128)S(1)}, f32[256,256]{1,0:T(8,128)S(1)}, u32[]{:S(2)}, u32[]{:S(2)}) collective-permute-start(f32[256,256]{1,0:T(8,128)S(1)} %get-tuple-element.89), channel_id=1, source_target_pairs={{1,2},{2,1},{3,4},{4,3},{5,6},{6,5},{7,8},{8,7},{9,10},{10,9},{11,... | collective-permute-start | bytes 786440 | tf_op jit(solution)/shard_map/ppermute | solution.py:552
  73.7 1.1 %collective-permute-start.19 = (f32[8,256]{1,0:T(8,128)S(1)}, f32[8,256]{1,0:T(8,128)S(1)}, u32[]{:S(2)}, u32[]{:S(2)}) collective-permute-start(f32[8,256]{1,0:T(8,128)S(1)} %add.54), channel_id=1, source_target_pairs={{0,4},{1,5},{2,6},{3,7},{4,0},{5,1},{6,2},{7,3},{8,12},{9,13},{10,... | collective-permute-start | bytes 24584 | tf_op jit(solution)/shard_map/ppermute | solution.py:541
  74.8 3.2 %shard_map.122 = (f32[4240,128]{1,0:T(8,128)S(1)}, f32[4240,128]{1,0:T(8,128)S(1)}) custom-call(f32[4240,128]{1,0:T(8,128)S(1)} %get-tuple-element.90.refs_0_.prior_ref, f32[4240,128]{1,0:T(8,128)S(1)} %get-tuple-element.65.c_ref.refs_0_.refs_1_, ...), custom_call_target="tpu_custom_call", output_to_operand_aliasing={{0}: (9, {}), {1}: (10, {})} | custom-call | flops 2147483648 | bytes 1048576 | tf_op jit(solution)/shard_map/pallas_call | solution.py:624
  78.0 2.5 %collective-permute-start.20 = (f32[8,256]{1,0:T(8,128)S(1)}, f32[8,256]{1,0:T(8,128)S(1)}, u32[]{:S(2)}, u32[]{:S(2)}) collective-permute-start(f32[8,256]{1,0:T(8,128)S(1)} %add.55), channel_id=1, source_target_pairs={{0,8},{1,9},{2,10},{3,11},{4,12},{5,13},{6,14},{7,15},{8,0},{9,1},... | collective-permute-start | bytes 24584 | tf_op jit(solution)/shard_map/ppermute | solution.py:541
  80.5 4.5 %shard_map.123 = (f32[4240,128]{1,0:T(8,128)S(1)}, f32[4240,128]{1,0:T(8,128)S(1)}, f32[4240,128]{1,0:T(8,128)S(1)}) custom-call(f32[256,256]{1,0:T(8,128)S(1)} %collective-permute-done.16.chip_ref, f32[256,256]{1,0:T(8,128)S(1)} %collective-permute-done.17.near_ref, ...), custom_call_target="tpu_custom_call", output_to_operand_aliasing={{0}: (3, {}), {2}: (12, {})} | custom-call | flops 3221225472 | bytes 1048576 | tf_op jit(solution)/shard_map/pallas_call | solution.py:630
  85.0 1.5 %shard_map.124 = (f32[2,4224]{1,0:T(2,128)S(1)}, f32[4240,128]{1,0:T(8,128)S(1)}) custom-call(f32[1]{0:T(128)S(6)} %copy.38.limit_ref, f32[256,256]{1,0:T(8,128)S(1)} %collective-permute-done.14.chip_ref, f32[256,256]{1,0:T(8,128)S(1)} %collective-permute-done.15.near_ref, ...), custom_call_target="tpu_custom_call", output_to_operand_aliasing={{1}: (4, {})} | custom-call | flops 268435456 | bytes 1048576 | tf_op jit(solution)/shard_map/pallas_call | solution.py:636
  86.5 3.7 %collective-permute-start.22 = (f32[2,4224]{1,0:T(2,128)S(1)}, f32[2,4224]{1,0:T(2,128)S(1)}, u32[]{:S(2)}, u32[]{:S(2)}) collective-permute-start(f32[2,4224]{1,0:T(2,128)S(1)} %get-tuple-element.103), channel_id=1, source_target_pairs={{0,32},{16,48},{32,0},{48,16},{64,96},{80,112},{96,64},{112,80},{1... | collective-permute-start | bytes 101384 | tf_op jit(solution)/shard_map/ppermute | solution.py:545
  90.2 1.1 %collective-permute-start.23 = (f32[2,4224]{1,0:T(2,128)S(1)}, f32[2,4224]{1,0:T(2,128)S(1)}, u32[]{:S(2)}, u32[]{:S(2)}) collective-permute-start(f32[2,4224]{1,0:T(2,128)S(1)} %get-tuple-element.103), channel_id=1, source_target_pairs={{0,48},{16,32},{32,16},{48,0},{64,112},{80,96},{96,80},{112,64},{1... | collective-permute-start | bytes 101384 | tf_op jit(solution)/shard_map/ppermute | solution.py:545
  91.3 0.8 collective-permute-done.22
  92.1 3.2 %collective-permute-done.23 = f32[2,4224]{1,0:T(2,128)S(1)} collective-permute-done((f32[2,4224]{1,0:T(2,128)S(1)}, f32[2,4224]{1,0:T(2,128)S(1)}, u32[]{:S(2)}, u32[]{:S(2)}) %collective-permute-start.23) | collective-permute-done | bytes 33824 | tf_op jit(solution)/shard_map/ppermute | solution.py:545
  95.4 1.2 %collective-permute-start.24 = (f32[2,4224]{1,0:T(2,128)S(1)}, f32[2,4224]{1,0:T(2,128)S(1)}, u32[]{:S(2)}, u32[]{:S(2)}) collective-permute-start(f32[2,4224]{1,0:T(2,128)S(1)} %add_add_fusion), channel_id=1, source_target_pairs={{0,64},{16,80},{32,96},{48,112},{64,0},{80,16},{96,32},{112,48},{1... | collective-permute-start | bytes 101384 | tf_op jit(solution)/shard_map/ppermute | solution.py:541
  96.6 4.3 %collective-permute-done.24 = f32[2,4224]{1,0:T(2,128)S(1)} collective-permute-done((f32[2,4224]{1,0:T(2,128)S(1)}, f32[2,4224]{1,0:T(2,128)S(1)}, u32[]{:S(2)}, u32[]{:S(2)}) %collective-permute-start.24) | collective-permute-done | bytes 33824 | tf_op jit(solution)/shard_map/ppermute | solution.py:541
  101.0 0.7 bitcast_subtract_fusion
  101.6 0.5 slice.26
  (36 shorter events, 0.2 us)
Async XLA Ops:
  1.4 8.0 %collective-permute-start.3 = (f32[2,4096]{1,0:T(2,128)S(1)}, f32[2,4096]{1,0:T(2,128)S(1)}, u32[]{:S(2)}, u32[]{:S(2)}) collective-permute-start(f32[2,4096]{1,0:T(2,128)S(1)} %bitcast.9), channel_id=1, source_target_pairs={{0,32},{16,48},{32,0},{48,16},{64,96},{80,112},{96,64},{112,80},{1... | collective-permute-start | bytes 98312 | tf_op jit(solution)/shard_map/ppermute | solution.py:545
  4.7 5.1 %collective-permute-start.4 = (f32[2,4096]{1,0:T(2,128)S(1)}, f32[2,4096]{1,0:T(2,128)S(1)}, u32[]{:S(2)}, u32[]{:S(2)}) collective-permute-start(f32[2,4096]{1,0:T(2,128)S(1)} %bitcast.10), channel_id=1, source_target_pairs={{0,48},{16,32},{32,16},{48,0},{64,112},{80,96},{96,80},{112,64},{1... | collective-permute-start | bytes 98312 | tf_op jit(solution)/shard_map/ppermute | solution.py:545
  5.8 4.1 %collective-permute-start.2 = (f32[2,4096]{1,0:T(2,128)S(1)}, f32[2,4096]{1,0:T(2,128)S(1)}, u32[]{:S(2)}, u32[]{:S(2)}) collective-permute-start(f32[2,4096]{1,0:T(2,128)S(1)} %bitcast.11), channel_id=1, source_target_pairs={{0,16},{16,0},{32,48},{48,32},{64,80},{80,64},{96,112},{112,96},{1... | collective-permute-start | bytes 98312 | tf_op jit(solution)/shard_map/ppermute | solution.py:545
  6.8 13.1 %collective-permute-start = (f32[256,256]{1,0:T(8,128)S(1)}, f32[256,256]{1,0:T(8,128)S(1)}, u32[]{:S(2)}, u32[]{:S(2)}) collective-permute-start(f32[256,256]{1,0:T(8,128)S(1)} %get-tuple-element.107), channel_id=1, source_target_pairs={{0,1},{1,0},{2,3},{3,2},{4,5},{5,4},{6,7},{7,6},{8,9},{9,8},{10,11... | collective-permute-start | bytes 786440 | tf_op jit(solution)/shard_map/ppermute | solution.py:553
  6.9 13.0 %collective-permute-start.1 = (f32[256,256]{1,0:T(8,128)S(1)}, f32[256,256]{1,0:T(8,128)S(1)}, u32[]{:S(2)}, u32[]{:S(2)}) collective-permute-start(f32[256,256]{1,0:T(8,128)S(1)} %get-tuple-element.106), channel_id=1, source_target_pairs={{1,2},{2,1},{3,4},{4,3},{5,6},{6,5},{7,8},{8,7},{9,10},{10,9},{11,... | collective-permute-start | bytes 786440 | tf_op jit(solution)/shard_map/ppermute | solution.py:552
  9.9 10.1 %copy-start = (s32[8,256,256]{2,1,0:T(8,128)S(1)}, s32[8,256,256]{2,1,0:T(8,128)}, u32[]{:S(2)}) copy-start(s32[8,256,256]{2,1,0:T(8,128)} %wells_ref.3) | copy-start | bytes 6291460
  9.9 10.0 %collective-permute-start.5 = (f32[2,4096]{1,0:T(2,128)S(1)}, f32[2,4096]{1,0:T(2,128)S(1)}, u32[]{:S(2)}, u32[]{:S(2)}) collective-permute-start(f32[2,4096]{1,0:T(2,128)S(1)} %add_add_fusion.1), channel_id=1, source_target_pairs={{0,64},{16,80},{32,96},{48,112},{64,0},{80,16},{96,32},{112,48},{1... | collective-permute-start | bytes 98312 | tf_op jit(solution)/shard_map/ppermute | solution.py:541
  21.1 10.4 %collective-permute-start.6 = (f32[256,256]{1,0:T(8,128)S(1)}, f32[256,256]{1,0:T(8,128)S(1)}, u32[]{:S(2)}, u32[]{:S(2)}) collective-permute-start(f32[256,256]{1,0:T(8,128)S(1)} %get-tuple-element.56), channel_id=1, source_target_pairs={{0,1},{1,0},{2,3},{3,2},{4,5},{5,4},{6,7},{7,6},{8,9},{9,8},{10,11... | collective-permute-start | bytes 786440 | tf_op jit(solution)/shard_map/ppermute | solution.py:553
  22.2 9.3 %collective-permute-start.7 = (f32[256,256]{1,0:T(8,128)S(1)}, f32[256,256]{1,0:T(8,128)S(1)}, u32[]{:S(2)}, u32[]{:S(2)}) collective-permute-start(f32[256,256]{1,0:T(8,128)S(1)} %get-tuple-element.57), channel_id=1, source_target_pairs={{1,2},{2,1},{3,4},{4,3},{5,6},{6,5},{7,8},{8,7},{9,10},{10,9},{11,... | collective-permute-start | bytes 786440 | tf_op jit(solution)/shard_map/ppermute | solution.py:552
  31.5 4.1 %copy-start.1 = (f32[4240,128]{1,0:T(8,128)}, f32[4240,128]{1,0:T(8,128)S(1)}, u32[]{:S(2)}) copy-start(f32[4240,128]{1,0:T(8,128)S(1)} %get-tuple-element.99.refs_7_) | copy-start | bytes 6512644
  31.8 10.7 %collective-permute-start.8 = (f32[256,256]{1,0:T(8,128)S(1)}, f32[256,256]{1,0:T(8,128)S(1)}, u32[]{:S(2)}, u32[]{:S(2)}) collective-permute-start(f32[256,256]{1,0:T(8,128)S(1)} %get-tuple-element.63), channel_id=1, source_target_pairs={{0,1},{1,0},{2,3},{3,2},{4,5},{5,4},{6,7},{7,6},{8,9},{9,8},{10,11... | collective-permute-start | bytes 786440 | tf_op jit(solution)/shard_map/ppermute | solution.py:553
  33.7 8.8 %collective-permute-start.9 = (f32[256,256]{1,0:T(8,128)S(1)}, f32[256,256]{1,0:T(8,128)S(1)}, u32[]{:S(2)}, u32[]{:S(2)}) collective-permute-start(f32[256,256]{1,0:T(8,128)S(1)} %get-tuple-element.64), channel_id=1, source_target_pairs={{1,2},{2,1},{3,4},{4,3},{5,6},{6,5},{7,8},{8,7},{9,10},{10,9},{11,... | collective-permute-start | bytes 786440 | tf_op jit(solution)/shard_map/ppermute | solution.py:552
  42.7 11.0 %collective-permute-start.10 = (f32[256,256]{1,0:T(8,128)S(1)}, f32[256,256]{1,0:T(8,128)S(1)}, u32[]{:S(2)}, u32[]{:S(2)}) collective-permute-start(f32[256,256]{1,0:T(8,128)S(1)} %get-tuple-element.67), channel_id=1, source_target_pairs={{0,1},{1,0},{2,3},{3,2},{4,5},{5,4},{6,7},{7,6},{8,9},{9,8},{10,11... | collective-permute-start | bytes 786440 | tf_op jit(solution)/shard_map/ppermute | solution.py:553
  44.9 8.8 %collective-permute-start.11 = (f32[256,256]{1,0:T(8,128)S(1)}, f32[256,256]{1,0:T(8,128)S(1)}, u32[]{:S(2)}, u32[]{:S(2)}) collective-permute-start(f32[256,256]{1,0:T(8,128)S(1)} %get-tuple-element.68), channel_id=1, source_target_pairs={{1,2},{2,1},{3,4},{4,3},{5,6},{6,5},{7,8},{8,7},{9,10},{10,9},{11,... | collective-permute-start | bytes 786440 | tf_op jit(solution)/shard_map/ppermute | solution.py:552
  46.8 6.9 %copy-start.3 = (s32[8,256,256]{2,1,0:T(8,128)S(1)}, s32[8,256,256]{2,1,0:T(8,128)}, u32[]{:S(2)}) copy-start(s32[8,256,256]{2,1,0:T(8,128)} %monitors_ref.1) | copy-start | bytes 6291460
  54.5 12.5 %collective-permute-start.12 = (f32[264,256]{1,0:T(8,128)S(1)}, f32[264,256]{1,0:T(8,128)S(1)}, u32[]{:S(2)}, u32[]{:S(2)}) collective-permute-start(f32[264,256]{1,0:T(8,128)S(1)} %get-tuple-element.80), channel_id=1, source_target_pairs={{0,1},{1,0},{2,3},{3,2},{4,5},{5,4},{6,7},{7,6},{8,9},{9,8},{10,11... | collective-permute-start | bytes 811016 | tf_op jit(solution)/shard_map/ppermute | solution.py:553
  56.8 10.3 %collective-permute-start.13 = (f32[256,256]{1,0:T(8,128)S(1)}, f32[256,256]{1,0:T(8,128)S(1)}, u32[]{:S(2)}, u32[]{:S(2)}) collective-permute-start(f32[256,256]{1,0:T(8,128)S(1)} %get-tuple-element.81), channel_id=1, source_target_pairs={{1,2},{2,1},{3,4},{4,3},{5,6},{6,5},{7,8},{8,7},{9,10},{10,9},{11,... | collective-permute-start | bytes 786440 | tf_op jit(solution)/shard_map/ppermute | solution.py:552
  59.9 20.6 %collective-permute-start.16 = (f32[256,256]{1,0:T(8,128)S(1)}, f32[256,256]{1,0:T(8,128)S(1)}, u32[]{:S(2)}, u32[]{:S(2)}) collective-permute-start(f32[256,256]{1,0:T(8,128)S(1)} %get-tuple-element.91), channel_id=1, source_target_pairs={{0,1},{1,0},{2,3},{3,2},{4,5},{5,4},{6,7},{7,6},{8,9},{9,8},{10,11... | collective-permute-start | bytes 786440 | tf_op jit(solution)/shard_map/ppermute | solution.py:553
  61.5 18.9 %collective-permute-start.17 = (f32[256,256]{1,0:T(8,128)S(1)}, f32[256,256]{1,0:T(8,128)S(1)}, u32[]{:S(2)}, u32[]{:S(2)}) collective-permute-start(f32[256,256]{1,0:T(8,128)S(1)} %get-tuple-element.92), channel_id=1, source_target_pairs={{1,2},{2,1},{3,4},{4,3},{5,6},{6,5},{7,8},{8,7},{9,10},{10,9},{11,... | collective-permute-start | bytes 786440 | tf_op jit(solution)/shard_map/ppermute | solution.py:552
  67.0 6.7 %collective-permute-start.18 = (f32[8,256]{1,0:T(8,128)S(1)}, f32[8,256]{1,0:T(8,128)S(1)}, u32[]{:S(2)}, u32[]{:S(2)}) collective-permute-start(f32[8,256]{1,0:T(8,128)S(1)} %slice_add_fusion), channel_id=1, source_target_pairs={{0,2},{1,3},{2,0},{3,1},{4,6},{5,7},{6,4},{7,5},{8,10},{9,11},{10,... | collective-permute-start | bytes 24584 | tf_op jit(solution)/shard_map/ppermute | solution.py:541
  68.5 16.4 %collective-permute-start.14 = (f32[256,256]{1,0:T(8,128)S(1)}, f32[256,256]{1,0:T(8,128)S(1)}, u32[]{:S(2)}, u32[]{:S(2)}) collective-permute-start(f32[256,256]{1,0:T(8,128)S(1)} %get-tuple-element.88), channel_id=1, source_target_pairs={{0,1},{1,0},{2,3},{3,2},{4,5},{5,4},{6,7},{7,6},{8,9},{9,8},{10,11... | collective-permute-start | bytes 786440 | tf_op jit(solution)/shard_map/ppermute | solution.py:553
  70.4 14.5 %collective-permute-start.15 = (f32[256,256]{1,0:T(8,128)S(1)}, f32[256,256]{1,0:T(8,128)S(1)}, u32[]{:S(2)}, u32[]{:S(2)}) collective-permute-start(f32[256,256]{1,0:T(8,128)S(1)} %get-tuple-element.89), channel_id=1, source_target_pairs={{1,2},{2,1},{3,4},{4,3},{5,6},{6,5},{7,8},{8,7},{9,10},{10,9},{11,... | collective-permute-start | bytes 786440 | tf_op jit(solution)/shard_map/ppermute | solution.py:552
  73.7 4.3 %collective-permute-start.19 = (f32[8,256]{1,0:T(8,128)S(1)}, f32[8,256]{1,0:T(8,128)S(1)}, u32[]{:S(2)}, u32[]{:S(2)}) collective-permute-start(f32[8,256]{1,0:T(8,128)S(1)} %add.54), channel_id=1, source_target_pairs={{0,4},{1,5},{2,6},{3,7},{4,0},{5,1},{6,2},{7,3},{8,12},{9,13},{10,... | collective-permute-start | bytes 24584 | tf_op jit(solution)/shard_map/ppermute | solution.py:541
  74.8 5.7 %copy-start.2 = (f32[4240,128]{1,0:T(8,128)S(1)}, f32[4240,128]{1,0:T(8,128)}, u32[]{:S(2)}) copy-start(f32[4240,128]{1,0:T(8,128)} %copy-done.1) | copy-start | bytes 6512644
  78.0 6.9 %collective-permute-start.20 = (f32[8,256]{1,0:T(8,128)S(1)}, f32[8,256]{1,0:T(8,128)S(1)}, u32[]{:S(2)}, u32[]{:S(2)}) collective-permute-start(f32[8,256]{1,0:T(8,128)S(1)} %add.55), channel_id=1, source_target_pairs={{0,8},{1,9},{2,10},{3,11},{4,12},{5,13},{6,14},{7,15},{8,0},{9,1},... | collective-permute-start | bytes 24584 | tf_op jit(solution)/shard_map/ppermute | solution.py:541
  86.5 5.6 %collective-permute-start.22 = (f32[2,4224]{1,0:T(2,128)S(1)}, f32[2,4224]{1,0:T(2,128)S(1)}, u32[]{:S(2)}, u32[]{:S(2)}) collective-permute-start(f32[2,4224]{1,0:T(2,128)S(1)} %get-tuple-element.103), channel_id=1, source_target_pairs={{0,32},{16,48},{32,0},{48,16},{64,96},{80,112},{96,64},{112,80},{1... | collective-permute-start | bytes 101384 | tf_op jit(solution)/shard_map/ppermute | solution.py:545
  90.2 5.1 %collective-permute-start.23 = (f32[2,4224]{1,0:T(2,128)S(1)}, f32[2,4224]{1,0:T(2,128)S(1)}, u32[]{:S(2)}, u32[]{:S(2)}) collective-permute-start(f32[2,4224]{1,0:T(2,128)S(1)} %get-tuple-element.103), channel_id=1, source_target_pairs={{0,48},{16,32},{32,16},{48,0},{64,112},{80,96},{96,80},{112,64},{1... | collective-permute-start | bytes 101384 | tf_op jit(solution)/shard_map/ppermute | solution.py:545
  91.3 4.1 %collective-permute-start.21 = (f32[2,4224]{1,0:T(2,128)S(1)}, f32[2,4224]{1,0:T(2,128)S(1)}, u32[]{:S(2)}, u32[]{:S(2)}) collective-permute-start(f32[2,4224]{1,0:T(2,128)S(1)} %get-tuple-element.103), channel_id=1, source_target_pairs={{0,16},{16,0},{32,48},{48,32},{64,80},{80,64},{96,112},{112,96},{1... | collective-permute-start | bytes 101384 | tf_op jit(solution)/shard_map/ppermute | solution.py:545
  95.4 5.5 %collective-permute-start.24 = (f32[2,4224]{1,0:T(2,128)S(1)}, f32[2,4224]{1,0:T(2,128)S(1)}, u32[]{:S(2)}, u32[]{:S(2)}) collective-permute-start(f32[2,4224]{1,0:T(2,128)S(1)} %add_add_fusion), channel_id=1, source_target_pairs={{0,64},{16,80},{32,96},{48,112},{64,0},{80,16},{96,32},{112,48},{1... | collective-permute-start | bytes 101384 | tf_op jit(solution)/shard_map/ppermute | solution.py:541
